TPU v7x, 256 devices: a whole 4x4x8 slice. The times are simulated.
256 devices in a mesh: mat: 4 (over z_lo), tile: 64 (over y, z_hi, x, core).
Axes of the slice: x: 4, y: 4, z: 8 (z_hi: 2, z_lo: 4; z = z_hi * 4 + z_lo), core: 2. Of those that a mesh axis runs over, the one named last changes fastest.
Arguments:
- volume: bfloat16 [4, 512, 64, 1024], P('mat', None, 'tile'), may hold values from -4 to 4
- system: bfloat16 [64, 1024, 32, 128], P('tile'), may hold values from 0 to 0.009521484
- geometry: int32 [64, 16], replicated, may hold values from 0 to 2
- attenuation: float32 [4, 64], replicated, may hold values from 0.05 to 0.5
- response: float32 [8, 64], replicated, may hold values from 0.002 to 0.06
- crosstalk: float32 [8], replicated, may hold values from 0.04 to 0.24
Outputs:
- counts: float32 [8, 512, 16, 512], P(None, ('mat', 'tile'))
Inputs may be any that keep to these rules, and one draw needn't show every extreme that they name: A tile touches, in view v, exactly the 2 detector blocks geometry[t, v] to geometry[t, v] + 1.
All inputs are finite; a program needn't handle non-finite values.
Results may differ from a plain program's by a relative error of at most 0.0003.
Values may be sent and summed in bfloat16 or wider, within the bound.
No kernel may reach another device: no remote copies, remote signals or barrier semaphores. Data moves between devices by JAX's collectives and lax.ppermute only.
A program may use at most 128 MiB of HBM per device.

v0:
```python
import jax
import jax.numpy as jnp
from jax import lax
from jax.sharding import PartitionSpec as P

PIXELS = 512
PB = 128
TOUCH = 2
CBINS = 8
SL_DEV = 2
PBLK = 4
KT = 32


def extended(x, sides, width):
    edges = {}
    for axis, dim in sides:
        devices, length = (lax.axis_size(axis), x.shape[dim])
        up = [(i, (i + 1) % devices) for i in range(devices - 1)]
        last = lax.slice_in_dim(x, length - width, length, axis=dim)
        first = lax.slice_in_dim(x, 0, width, axis=dim)
        edges[dim] = (
            lax.ppermute(last, axis, up),
            lax.ppermute(first, axis, [(b, a) for a, b in up]),
        )
    done = []
    for _, dim in sides:
        low, high = edges[dim]
        around = [(width, width) if d in done else (0, 0) for d in range(x.ndim)]
        x = jnp.concatenate([jnp.pad(low, around), x, jnp.pad(high, around)], axis=dim)
        done.append(dim)
    return x


def place_table(first_block, touch_count, block_count):
    touch_ids = jnp.arange(touch_count, dtype=jnp.int32)
    block_ids = jnp.arange(block_count, dtype=jnp.int32)
    return (first_block[..., None, None] + touch_ids[:, None] == block_ids).astype(jnp.float32)


def per_device(volume, system, geometry, attenuation, response, crosstalk):
    mat_count = lax.axis_size("mat")
    tile_count = lax.axis_size("tile")
    slice_count = volume.shape[1]
    tile_vox = volume.shape[3]
    view_count = geometry.shape[1]
    ray_count = view_count * PIXELS
    matrix = system.reshape(tile_vox, KT * PB)
    columns = volume.reshape(mat_count, tile_count, SL_DEV, tile_vox)
    columns = columns.transpose(1, 0, 2, 3).reshape(slice_count, tile_vox)
    row_share = mat_count * SL_DEV
    partial_value = jnp.dot(columns, matrix, preferred_element_type=jnp.float32)
    partial_value = partial_value.reshape(tile_count, row_share, view_count, TOUCH, PB)
    received = lax.all_to_all(partial_value, "tile", split_axis=0, concat_axis=0, tiled=True)
    placed_all = place_table(geometry, TOUCH, PBLK)
    summed = jnp.einsum("qrvjp,qvjb->rvbp", received, placed_all, precision=lax.Precision.HIGHEST)
    summed = summed.reshape(row_share, ray_count)
    integrals = lax.all_to_all(
        summed.reshape(mat_count, SL_DEV, ray_count), "mat", split_axis=0, concat_axis=0, tiled=True
    )
    stacked = integrals.reshape(mat_count, SL_DEV * ray_count)
    exponent = jnp.dot(
        attenuation.T, stacked, preferred_element_type=jnp.float32, precision=lax.Precision.HIGHEST
    )
    detected = jnp.dot(
        response,
        jnp.exp(-exponent),
        preferred_element_type=jnp.float32,
        precision=lax.Precision.HIGHEST,
    )
    detected = detected.reshape(CBINS, SL_DEV, ray_count)
    padded = extended(detected, ((("mat", "tile"), 1),), 1)
    leakage = crosstalk[:, None, None]
    counts = (1.0 - 2.0 * leakage) * detected + leakage * (padded[:, :-2] + padded[:, 2:])
    return counts.reshape(CBINS, SL_DEV, view_count, PIXELS)


def solution(mesh):
    in_specs = (P("mat", None, "tile", None), P("tile", None, None, None), P(), P(), P(), P())
    out_specs = P(None, ("mat", "tile"), None, None)
    return jax.shard_map(
        per_device, mesh=mesh, in_specs=in_specs, out_specs=out_specs, check_vma=False
    )
```

profile of v0, /device:TPU:223, one launch (start us, length us, event | category | flops | bytes accessed | tf_op | source)
XLA Modules:
  0.0 299.2 jit_solution(13730433758599868148)
XLA Ops:
  0.0 15.1 %copy.35 = bf16[128,8,32,128]{3,1,2,0:T(8,128)(2,1)} copy(bf16[128,8,32,128]{3,2,1,0:T(8,128)(2,1)} %bitcast.51) | data formatting | bytes 16777216
  15.1 12.0 %copy.15 = bf16[4096,1024]{1,0:T(8,128)(2,1)} copy(bf16[4096,1024]{0,1:T(8,128)(2,1)} %bitcast.50) | data formatting | bytes 16777216 | tf_op jit(solution)/shard_map/dot_general | solution.py:52
  27.1 0.0 copy-done.1
  27.2 0.4 reshape.32
  27.6 0.3 copy.14
  27.9 7.1 %fusion.13 = f32[64,8,16,2,128]{4,0,3,2,1:T(8,128)S(1)} fusion(bf16[64,8,1024,1,1]{2,0,4,3,1:T(8,128)(2,1)S(1)} %bitcast.59, bf16[16,2,128,1024,1]{3,2,1,0,4:T(8,128)(2,1)} %bitcast.52), kind=kOutput, calls=%fused_computation.18 | convolution fusion | flops 4294967296 | bytes 17825792 | tf_op jit(solution)/shard_map/dot_general | solution.py:52
  34.9 9.8 %copy.16 = f32[64,8,16,2,128]{4,3,1,2,0:T(2,128)} copy(f32[64,8,16,2,128]{4,0,3,2,1:T(8,128)S(1)} %fusion.13) | data formatting | bytes 16777216 | tf_op jit(solution)/shard_map/dot_general | solution.py:52
  44.7 13.3 %all-to-all-start = ((f32[64,8,16,2,128]{4,3,1,2,0:T(2,128)}), f32[64,8,16,2,128]{4,3,1,2,0:T(2,128)}, u32[]{:S(2)}, u32[]{:S(2)}) async-start(f32[64,8,16,2,128]{4,3,1,2,0:T(2,128)} %copy.16), calls=%async_computation | async-start | bytes 16777216 | tf_op jit(solution)/shard_map/all_to_all | solution.py:54
  58.1 0.0 copy-start.3
  58.1 0.0 copy-start.4
  58.1 183.9 %all-to-all-done = f32[64,8,16,2,128]{4,3,1,2,0:T(2,128)} async-done(((f32[64,8,16,2,128]{4,3,1,2,0:T(2,128)}), f32[64,8,16,2,128]{4,3,1,2,0:T(2,128)}, u32[]{:S(2)}, u32[]{:S(2)}) %all-to-all-start) | async-done | bytes 8388640 | tf_op jit(solution)/shard_map/all_to_all | solution.py:54
  242.0 10.5 %fusion.3 = f32[8,16,4,128]{3,2,0,1:T(4,128)S(1)} fusion(f32[64,8,16,2,128]{4,3,1,2,0:T(2,128)} %all-to-all-done, s32[64,16,2]{0,2,1:T(2,128)S(1)} %iota_add_fusion), kind=kOutput, calls=%fused_computation.5 | convolution fusion | flops 100671488 | bytes 8658944 | tf_op jit(solution)/shard_map/qrvjp,qvjb->rvbp/dot_general | solution.py:56
  252.5 0.2 reshape_reshape.3
  252.7 9.4 %all_to_all.10 = f32[4,2,8192]{2,1,0:T(2,128)S(1)} all-to-all(f32[4,2,8192]{2,1,0:T(2,128)S(1)} %reshape_reshape.3), channel_id=1, replica_groups=mesh['mat'=4,'tile'=64] {'mat'}, dimensions={0} | all-to-all | bytes 524288 | tf_op jit(solution)/shard_map/all_to_all | solution.py:58
  262.1 0.2 copy.27
  262.3 3.6 %fusion = f32[16384,64]{0,1:T(8,128)S(1)} fusion(f32[4,16384]{1,0:T(4,128)S(1)} %bitcast.58, f32[4,64]{1,0:T(4,128)S(1)} %copy-done.3), kind=kOutput, calls=%fused_computation.1 | convolution fusion | flops 51380224 | bytes 4457472 | tf_op jit(solution)/shard_map/dot_general | solution.py:62
  265.9 2.3 fusion.14
  268.1 9.5 %collective-permute-start = (f32[8,1,8192]{2,0,1:T(8,128)S(1)}, f32[8,1,8192]{2,0,1:T(8,128)S(1)}, u32[]{:S(2)}, u32[]{:S(2)}) collective-permute-start(f32[8,1,8192]{2,0,1:T(8,128)S(1)} %get-tuple-element.5), channel_id=1, source_target_pairs={{0,1},{1,2},{2,3},{3,4},{4,5},{5,6},{6,7},{7,8},{8,9},{9,10},{10,1... | collective-permute-start | bytes 786440 | tf_op jit(solution)/shard_map/ppermute | solution.py:23
  277.7 1.9 collective-permute-start.1
  279.6 2.8 collective-permute-done
  282.4 15.5 %collective-permute-done.1 = f32[8,1,8192]{2,0,1:T(8,128)S(1)} collective-permute-done((f32[8,1,8192]{2,0,1:T(8,128)S(1)}, f32[8,1,8192]{2,0,1:T(8,128)S(1)}, u32[]{:S(2)}, u32[]{:S(2)}) %collective-permute-start.1) | collective-permute-done | bytes 262176 | tf_op jit(solution)/shard_map/ppermute | solution.py:24
  297.8 0.2 fusion.8
  298.0 0.3 copy.36
  298.3 0.8 copy.25
  (11 shorter events, 0.1 us)
Async XLA Ops:
  0.0 265.8 %copy-start = (f32[8,64]{1,0:T(8,128)S(1)}, f32[8,64]{1,0:T(8,128)}, u32[]{:S(2)}) copy-start(f32[8,64]{1,0:T(8,128)} %param.10) | copy-start | bytes 6148
  15.1 12.0 %copy-start.1 = (bf16[1,512,1,1024]{3,1,2,0:T(8,128)(2,1)S(1)}, bf16[1,512,1,1024]{3,1,2,0:T(8,128)(2,1)}, u32[]{:S(2)}) copy-start(bf16[1,512,1,1024]{3,1,2,0:T(8,128)(2,1)} %param.6) | copy-start | bytes 3145732
  44.7 13.4 %copy-start.2 = (s32[64,16]{0,1:T(8,128)S(1)}, s32[64,16]{0,1:T(8,128)}, u32[]{:S(2)}) copy-start(s32[64,16]{0,1:T(8,128)} %param.8) | copy-start | bytes 12292
  44.7 197.3 %all-to-all-start = ((f32[64,8,16,2,128]{4,3,1,2,0:T(2,128)}), f32[64,8,16,2,128]{4,3,1,2,0:T(2,128)}, u32[]{:S(2)}, u32[]{:S(2)}) async-start(f32[64,8,16,2,128]{4,3,1,2,0:T(2,128)} %copy.16), calls=%async_computation | async-start | bytes 16777216 | tf_op jit(solution)/shard_map/all_to_all | solution.py:54
  58.1 204.2 %copy-start.3 = (f32[4,64]{1,0:T(4,128)S(1)}, f32[4,64]{1,0:T(4,128)}, u32[]{:S(2)}) copy-start(f32[4,64]{1,0:T(4,128)} %param.9) | copy-start | bytes 3076
  58.1 221.5 %copy-start.4 = (f32[8]{0:T(128)S(1)}, f32[8]{0:T(128)}, u32[]{:S(2)}) copy-start(f32[8]{0:T(128)} %param.11) | copy-start | bytes 100
  268.1 14.2 %collective-permute-start = (f32[8,1,8192]{2,0,1:T(8,128)S(1)}, f32[8,1,8192]{2,0,1:T(8,128)S(1)}, u32[]{:S(2)}, u32[]{:S(2)}) collective-permute-start(f32[8,1,8192]{2,0,1:T(8,128)S(1)} %get-tuple-element.5), channel_id=1, source_target_pairs={{0,1},{1,2},{2,3},{3,4},{4,5},{5,6},{6,7},{7,8},{8,9},{9,10},{10,1... | collective-permute-start | bytes 786440 | tf_op jit(solution)/shard_map/ppermute | solution.py:23
  277.7 20.2 %collective-permute-start.1 = (f32[8,1,8192]{2,0,1:T(8,128)S(1)}, f32[8,1,8192]{2,0,1:T(8,128)S(1)}, u32[]{:S(2)}, u32[]{:S(2)}) collective-permute-start(f32[8,1,8192]{2,0,1:T(8,128)S(1)} %get-tuple-element.6), channel_id=1, source_target_pairs={{1,0},{2,1},{3,2},{4,3},{5,4},{6,5},{7,6},{8,7},{9,8},{10,9},{11,1... | collective-permute-start | bytes 786440 | tf_op jit(solution)/shard_map/ppermute | solution.py:24
where the time goes:
time: 300 us; the launch traced here: 299 us
  waiting for transfers between devices  202 us (67%)
  local copies, waits for them, and re-layouts  39.3 us (13%)
  starting transfers between devices  24.8 us (8%)
  matrix products  23.3 us (8%)
  blocking collectives  9.38 us (3%)
    all_to_all x1, waiting for transfers between devices, per_device(): lax.all_to_all(partial_value, 'tile', split_axis=0, concat_axis=0, tiled=...  184 us
    dot_general x2, local copies, waits for them, and re-layouts, per_device(): partial_value = jnp.dot(columns, matrix, preferred_element_type=jnp.float32)  21.8 us
    unnamed x13, local copies, waits for them, and re-layouts  15.6 us
    ppermute x1, waiting for transfers between devices, extended(): lax.ppermute(first, axis, [(b, a) for a, b in up])  15.5 us
    all_to_all x1, starting transfers between devices, per_device(): lax.all_to_all(partial_value, 'tile', split_axis=0, concat_axis=0, tiled=...  13.3 us
    dot_general x1, matrix products, per_device(): jnp.einsum('qrvjp,qvjb->rvbp', received, placed_all, precision=lax.Precis...  10.5 us
    ppermute x1, starting transfers between devices, extended(): lax.ppermute(last, axis, up)  9.51 us
    all_to_all x1, blocking collectives, per_device(): lax.all_to_all(summed.reshape(mat_count, SL_DEV, ray_count), 'mat', split...  9.38 us
  transfers between devices with their start and end apart: 3, of which 3 were waited for; matrix products, arithmetic and copies ran while one was open for 0% of the time, Pallas kernels for 0%

commit v1 on v0

v1 whole, which is shorter than its diff:
```python
import functools

import jax
import jax.numpy as jnp
from jax import lax
from jax.experimental import pallas as pl
from jax.experimental.pallas import tpu as pltpu
from jax.sharding import Mesh, PartitionSpec as P

PB = 128
PBLK = 4
CBINS = 8
EBINS = 64
MATS = 4
AXES = ("mat", "y", "zh", "x", "core")
TILE_AXES = ("y", "zh", "x", "core")
PAIRS = ([(0, 1), (1, 0), (2, 3), (3, 2)], [(1, 2), (2, 1), (3, 0), (0, 3)])
ORDERS = (
    (("x", 0), ("y", 0), ("x", 1), ("y", 1)),
    (("x", 1), ("y", 1), ("x", 0), ("y", 0)),
    (("y", 0), ("x", 0), ("y", 1), ("x", 1)),
    (("y", 1), ("x", 1), ("y", 0), ("x", 0)),
)
DIM_OF = {("x", 0): 2, ("x", 1): 3, ("y", 0): 4, ("y", 1): 5}


def pair_bits(i):
    return ((i + 1) // 2) % 2, i // 2


def row_order(slice_count):
    pos = jnp.arange(slice_count, dtype=jnp.int32)
    bits = [(pos // (256 >> n)) % 2 for n in range(5)]
    rest = pos % 16
    core = bits[0] ^ lax.axis_index("core")

    def place(b0, b1, name):
        mine = pair_bits(lax.axis_index(name))
        b0, b1 = b0 ^ mine[0], b1 ^ mine[1]
        return 2 * b1 + (b0 ^ b1)

    x = place(bits[1], bits[2], "x")
    y = place(bits[3], bits[4], "y")
    mat, zh, r = rest // 4, (rest // 2) % 2, rest % 2
    return mat * 128 + y * 32 + zh * 16 + x * 4 + core * 2 + r


def project_body(vol_ref, sys_ref, out_ref):
    @pl.when(pl.program_id(0) == 0)
    def _():
        out_ref[...] = jnp.zeros_like(out_ref)

    weights = jnp.swapaxes(sys_ref[...], 0, 1)
    for k in range(0, 8, 2):
        pair = jnp.concatenate([weights[k], weights[k + 1]], axis=1)
        got = jnp.dot(vol_ref[...], pair, preferred_element_type=jnp.float32)
        out_ref[k] += got[:, :PB]
        out_ref[k + 1] += got[:, PB:]


def project(columns, matrix, portion):
    rows, depth = columns.shape
    step = 256
    return pl.pallas_call(
        project_body,
        grid=(depth // step,),
        in_specs=[
            pl.BlockSpec((rows, step), lambda i: (0, i)),
            pl.BlockSpec((step, 8, PB), lambda i: (i, portion, 0)),
        ],
        out_specs=pl.BlockSpec((8, rows, PB), lambda i: (0, 0, 0)),
        out_shape=jax.ShapeDtypeStruct((8, rows, PB), jnp.float32),
        name="project",
    )(columns, matrix)


def placed(pieces, first):
    shape = (4, PBLK) + (1,) * (pieces.ndim - 2)
    offset = jnp.arange(PBLK, dtype=jnp.int32)[None, :] - first[:, None]
    offset = offset.reshape(shape)
    zero = jnp.float32(0)
    low, high = pieces[:, 0:1].astype(jnp.float32), pieces[:, 1:2].astype(jnp.float32)
    return jnp.where(offset == 0, low, jnp.where(offset == 1, high, zero))


def per_device(volume, system, geometry, attenuation, response, crosstalk):
    rows = volume.shape[1]
    depth = volume.shape[3]
    tile = lax.axis_index(TILE_AXES)
    vol = volume.reshape(rows, depth)
    order = row_order(rows)
    chosen = (order[:, None] == jnp.arange(rows, dtype=jnp.int32)[None, :]).astype(jnp.bfloat16)
    columns = jnp.dot(chosen, vol, preferred_element_type=jnp.float32).astype(jnp.bfloat16)
    matrix = system.reshape(depth, 32, PB)
    mine = lax.dynamic_index_in_dim(geometry, tile, 0, keepdims=False)
    partner = lax.dynamic_index_in_dim(geometry, tile ^ 1, 0, keepdims=False)

    current = []
    for w in range(4):
        part = project(columns, matrix, w).reshape(4, 2, 2, 2, 2, 2, 2, 16, PB)
        sent = part[:, :, 1].astype(jnp.float16)
        got = lax.ppermute(sent, "core", [(0, 1), (1, 0)])
        first, other = mine[4 * w : 4 * w + 4], partner[4 * w : 4 * w + 4]
        current.append(placed(part[:, :, 0], first) + placed(got, other))
    for n in range(4):
        for w in range(4):
            step = ORDERS[w][n]
            dim = DIM_OF[step]
            keep = lax.slice_in_dim(current[w], 0, 1, axis=dim)
            sent = lax.slice_in_dim(current[w], 1, 2, axis=dim).astype(jnp.float16)
            got = lax.ppermute(sent, step[0], PAIRS[step[1]])
            current[w] = keep + got.astype(jnp.float32)

    whole = jnp.concatenate([c.reshape(4, PBLK, MATS, 2, 2, PB) for c in current], axis=0)
    outgoing = whole.transpose(3, 2, 4, 0, 1, 5).astype(jnp.float16).reshape(8, 2, 64, PB)
    received = lax.all_to_all(outgoing, ("zh", "mat"), 0, 0, tiled=True)
    received = received.reshape(2, MATS, 2 * 64 * PB).astype(jnp.float32)
    stacked = received[0] + received[1]
    exponent = jnp.dot(attenuation.T, stacked, preferred_element_type=jnp.float32, precision=lax.Precision.HIGHEST)
    detected = jnp.dot(
        response, jnp.exp(-exponent), preferred_element_type=jnp.float32, precision=lax.Precision.HIGHEST
    )
    detected = detected.reshape(CBINS, 2, 64 * PB)
    axes = ("mat",) + TILE_AXES
    count = lax.axis_size(axes)
    up = [(i, i + 1) for i in range(count - 1)]
    above = lax.ppermute(detected[:, 1:], axes, up)
    below = lax.ppermute(detected[:, :1], axes, [(b, a) for a, b in up])
    padded = jnp.concatenate([above, detected, below], axis=1)
    leakage = crosstalk[:, None, None]
    counts = (1.0 - 2.0 * leakage) * detected + leakage * (padded[:, :-2] + padded[:, 2:])
    return counts.reshape(CBINS, 2, 16, PBLK * PB)


def solution(mesh):
    fine = Mesh(mesh.devices.reshape(4, 4, 2, 4, 2), AXES)
    in_specs = (P("mat", None, TILE_AXES, None), P(TILE_AXES, None, None, None), P(), P(), P(), P())
    out_specs = P(None, AXES, None, None)
    return jax.shard_map(per_device, mesh=fine, in_specs=in_specs, out_specs=out_specs, check_vma=False)
```

time: 300 us -> 135 us (0.45)
  waiting for transfers between devices: 202 us -> 36.4 us
  local copies, waits for them, and re-layouts: 39.3 us -> 6.51 us
  other arithmetic: 0.16 us -> 22.2 us
  Pallas kernels: 0 us -> 20.5 us
  matrix products: 23.3 us -> 7.62 us
  starting transfers between devices: 24.8 us -> 29.1 us
    all_to_all x1 -> x0, waiting for transfers between devices: 184 us -> none  [per_device(): lax.all_to_all(partial_value, 'tile', split_axis=0, concat_axis=0, tiled=...]
    dot_general x2 -> x0, local copies, waits for them, and re-layouts: 21.8 us -> none  [per_device(): partial_value = jnp.dot(columns, matrix, preferred_element_type=jnp.float32)]
    pallas_call x0 -> x4, Pallas kernels: none -> 20.5 us  [project(): pl.pallas_call(project_body, grid=(depth // step,), in_specs=[pl.BlockSpe...]
    ppermute x2 -> x22, waiting for transfers between devices: 18.2 us -> 36.4 us  [the longest x16 17.8 us: per_device(): got = lax.ppermute(sent, step[0], PAIRS[step[1]])]
    ppermute x2 -> x22, starting transfers between devices: 11.4 us -> 29.1 us  [the longest x16 13.2 us: per_device(): got = lax.ppermute(sent, step[0], PAIRS[step[1]])]
    dot_general x2 -> x1, matrix products: 17.5 us -> 1.72 us  [per_device(): jnp.dot(chosen, vol, preferred_element_type=jnp.float32)]
    unnamed x13 -> x21, local copies, waits for them, and re-layouts: 15.6 us -> 1.56 us
    all_to_all x1 -> x0, starting transfers between devices: 13.3 us -> none  [per_device(): lax.all_to_all(partial_value, 'tile', split_axis=0, concat_axis=0, tiled=...]
  transfers between devices with their start and end apart: 3 -> 22, of which waited for: 3 -> 12; matrix products, arithmetic and copies ran while one was open for 0% -> 17% of each run, Pallas kernels for 0% -> 11%
where the time goes in v1:
time: 135 us; the launch traced here: 134 us
  waiting for transfers between devices  36.4 us (27%)
  starting transfers between devices  29.1 us (22%)
  other arithmetic  22.2 us (16%)
  Pallas kernels  20.5 us (15%)
  blocking collectives  11.3 us (8%)
  matrix products  7.62 us (6%)
  local copies, waits for them, and re-layouts  6.51 us (5%)
    pallas_call x4, Pallas kernels, project(): pl.pallas_call(project_body, grid=(depth // step,), in_specs=[pl.BlockSpe...  20.5 us
    ppermute x16, waiting for transfers between devices, per_device(): got = lax.ppermute(sent, step[0], PAIRS[step[1]])  17.8 us
    ppermute x1, waiting for transfers between devices, per_device(): below = lax.ppermute(detected[:, :1], axes, [(b, a) for a, b in up])  16 us
    ppermute x16, starting transfers between devices, per_device(): got = lax.ppermute(sent, step[0], PAIRS[step[1]])  13.2 us
    ppermute x1, starting transfers between devices, per_device(): above = lax.ppermute(detected[:, 1:], axes, up)  12.8 us
    all_to_all x1, blocking collectives, per_device(): received = lax.all_to_all(outgoing, ('zh', 'mat'), 0, 0, tiled=True)  11.3 us
    squeeze x4, other arithmetic, per_device(): current.append(placed(part[:, :, 0], first) + placed(got, other))  10.9 us
    broadcast_in_dim x4, other arithmetic, placed(): return jnp.where(offset == 0, low, jnp.where(offset == 1, high, zero))  4.69 us
  transfers between devices with their start and end apart: 22, of which 12 were waited for; matrix products, arithmetic and copies ran while one was open for 17% of the time, Pallas kernels for 11%

profile of v1, /device:TPU:223, one launch (start us, length us, event | category | flops | bytes accessed | tf_op | source)
XLA Modules:
  0.0 134.2 jit_solution(9575345322857711926)
XLA Ops:
  1.2 1.7 %convolution_convert_fusion.vol_ref = bf16[512,1024]{1,0:T(8,128)(2,1)} fusion(bf16[1,512,1,1024]{3,1,2,0:T(8,128)(2,1)S(1)} %copy-done, s32[512]{0:T(512)S(1)} %fusion.30), kind=kOutput, calls=%fused_computation.6 | convolution fusion | flops 537657344 | bytes 2099200 | tf_op jit(solution)/shard_map/dot_general | solution.py:93
  2.9 5.1 %project.4 = f32[8,512,128]{2,1,0:T(8,128)} custom-call(bf16[512,1024]{1,0:T(8,128)(2,1)} %convolution_convert_fusion.vol_ref, bf16[1024,32,128]{2,1,0:T(8,128)(2,1)} %bitcast.106), custom_call_target="tpu_custom_call" | custom-call | tf_op jit(solution)/shard_map/project/pallas_call | solution.py:64
  8.1 3.0 %slice_bitcast_fusion.3 = (f32[4,2,2,2,2,2,16,128]{7,6,5,4,3,2,1,0:T(8,128)}, f16[4,2,2,2,2,2,16,128]{7,6,5,4,3,2,1,0:T(8,128)(2,1)}) fusion(f32[4,2,2,2,2,2,2,16,128]{8,7,6,5,4,3,2,1,0:T(8,128)} %bitcast.111), kind=kLoop, calls=%fused_computation.22 | loop fusion | flops 262144 | bytes 3670016 | tf_op jit(solution)/shard_map/squeeze | solution.py:104
  11.8 5.1 %project.5 = f32[8,512,128]{2,1,0:T(8,128)} custom-call(bf16[512,1024]{1,0:T(8,128)(2,1)} %convolution_convert_fusion.vol_ref, bf16[1024,32,128]{2,1,0:T(8,128)(2,1)} %bitcast.107), custom_call_target="tpu_custom_call" | custom-call | tf_op jit(solution)/shard_map/project/pallas_call | solution.py:64
  16.9 2.6 %slice_bitcast_fusion.2 = (f32[4,2,2,2,2,2,16,128]{7,6,5,4,3,2,1,0:T(8,128)S(1)}, f16[4,2,2,2,2,2,16,128]{7,6,5,4,3,2,1,0:T(8,128)(2,1)}) fusion(f32[4,2,2,2,2,2,2,16,128]{8,7,6,5,4,3,2,1,0:T(8,128)} %bitcast.112), kind=kLoop, calls=%fused_computation.18 | loop fusion | flops 262144 | bytes 3670016 | tf_op jit(solution)/shard_map/squeeze | solution.py:104
  19.5 5.1 %project.6 = f32[8,512,128]{2,1,0:T(8,128)} custom-call(bf16[512,1024]{1,0:T(8,128)(2,1)} %convolution_convert_fusion.vol_ref, bf16[1024,32,128]{2,1,0:T(8,128)(2,1)} %bitcast.108), custom_call_target="tpu_custom_call" | custom-call | tf_op jit(solution)/shard_map/project/pallas_call | solution.py:64
  24.6 2.7 %slice_bitcast_fusion.1 = (f32[4,2,2,2,2,2,16,128]{7,6,5,4,3,2,1,0:T(8,128)S(1)}, f16[4,2,2,2,2,2,16,128]{7,6,5,4,3,2,1,0:T(8,128)(2,1)}) fusion(f32[4,2,2,2,2,2,2,16,128]{8,7,6,5,4,3,2,1,0:T(8,128)} %bitcast.113), kind=kLoop, calls=%fused_computation.14 | loop fusion | flops 262144 | bytes 3670016 | tf_op jit(solution)/shard_map/squeeze | solution.py:104
  27.8 5.1 %project.7 = f32[8,512,128]{2,1,0:T(8,128)} custom-call(bf16[512,1024]{1,0:T(8,128)(2,1)} %convolution_convert_fusion.vol_ref, bf16[1024,32,128]{2,1,0:T(8,128)(2,1)} %bitcast.109), custom_call_target="tpu_custom_call" | custom-call | tf_op jit(solution)/shard_map/project/pallas_call | solution.py:64
  33.0 2.6 %slice_bitcast_fusion = (f32[4,2,2,2,2,2,16,128]{7,6,5,4,3,2,1,0:T(8,128)S(1)}, f16[4,2,2,2,2,2,16,128]{7,6,5,4,3,2,1,0:T(8,128)(2,1)}) fusion(f32[4,2,2,2,2,2,2,16,128]{8,7,6,5,4,3,2,1,0:T(8,128)} %bitcast.110), kind=kLoop, calls=%fused_computation.10 | loop fusion | flops 262144 | bytes 3670016 | tf_op jit(solution)/shard_map/squeeze | solution.py:104
  35.5 2.4 %slice_bitcast_fusion.11 = (f32[4,2,2,2,2,16,128]{6,5,4,3,2,1,0:T(8,128)}, f32[4,2,2,2,2,16,128]{6,5,4,3,2,1,0:T(8,128)}) fusion(f32[4,2,2,2,2,2,16,128]{7,6,5,4,3,2,1,0:T(8,128)} %get-tuple-element.13), kind=kLoop, calls=%fused_computation.50 | loop fusion | bytes 2097152 | tf_op jit(solution)/shard_map/jit(_where)/broadcast_in_dim | solution.py:83
  52.0 3.2 %collective-permute-done.1 = f16[4,4,1,2,2,2,16,128]{7,6,1,0,5,4,3,2:T(8,128)(2,1)S(1)} collective-permute-done((f16[4,4,1,2,2,2,16,128]{7,6,1,0,5,4,3,2:T(8,128)(2,1)S(1)}, f16[4,4,1,2,2,2,16,128]{7,6,1,0,5,4,3,2:T(8,128)(2,1)S(1)}, u32[]{:S(2)}, u32[]{:S(2)}) %collective-permute-start.1) | collective-permute-done | bytes 524320 | tf_op jit(solution)/shard_map/ppermute | solution.py:111
  56.0 3.0 %collective-permute-done.6 = f16[4,4,2,1,2,2,16,128]{7,6,1,0,5,4,3,2:T(8,128)(2,1)S(1)} collective-permute-done((f16[4,4,2,1,2,2,16,128]{7,6,1,0,5,4,3,2:T(8,128)(2,1)S(1)}, f16[4,4,2,1,2,2,16,128]{7,6,1,0,5,4,3,2:T(8,128)(2,1)S(1)}, u32[]{:S(2)}, u32[]{:S(2)}) %collective-permute-start.6) | collective-permute-done | bytes 524320 | tf_op jit(solution)/shard_map/ppermute | solution.py:111
  61.5 3.0 %collective-permute-done.16 = f16[4,4,2,2,2,1,16,128]{7,6,1,0,5,4,3,2:T(8,128)(2,1)S(1)} collective-permute-done((f16[4,4,2,2,2,1,16,128]{7,6,1,0,5,4,3,2:T(8,128)(2,1)S(1)}, f16[4,4,2,2,2,1,16,128]{7,6,1,0,5,4,3,2:T(8,128)(2,1)S(1)}, u32[]{:S(2)}, u32[]{:S(2)}) %collective-permute-start.16) | collective-permute-done | bytes 524320 | tf_op jit(solution)/shard_map/ppermute | solution.py:111
  64.8 1.9 %collective-permute-start.17 = (f16[4,4,2,1,2,1,16,128]{7,6,1,0,5,4,3,2:T(8,128)(2,1)S(1)}, f16[4,4,2,1,2,1,16,128]{7,6,1,0,5,4,3,2:T(8,128)(2,1)S(1)}, u32[]{:S(2)}, u32[]{:S(2)}) collective-permute-start(f16[4,4,2,1,2,1,16,128]{7,6,1,0,5,4,3,2:T(8,128)(2,1)S(1)} %slice_convert_fusion.8), channel_id=1, source_target_pairs={{2,4},{4,2},{6,0},{0,6},{3,5},{5,3},{7,1},{1,7},{10,12},{12,10},{1... | collective-permute-start | bytes 786440 | tf_op jit(solution)/shard_map/ppermute | solution.py:111
  66.8 1.7 %collective-permute-start.3 = (f16[4,4,1,1,1,2,16,128]{7,6,1,0,5,4,3,2:T(8,128)(2,1)S(1)}, f16[4,4,1,1,1,2,16,128]{7,6,1,0,5,4,3,2:T(8,128)(2,1)S(1)}, u32[]{:S(2)}, u32[]{:S(2)}) collective-permute-start(f16[4,4,1,1,1,2,16,128]{7,6,1,0,5,4,3,2:T(8,128)(2,1)S(1)} %slice_convert_fusion.15), channel_id=1, source_target_pairs={{2,4},{4,2},{6,0},{0,6},{3,5},{5,3},{7,1},{1,7},{10,12},{12,10},{1... | collective-permute-start | bytes 393224 | tf_op jit(solution)/shard_map/ppermute | solution.py:111
  76.3 1.9 %collective-permute-start.14 = (f16[4,4,1,1,1,1,16,128]{7,6,1,0,5,4,3,2:T(8,128)(2,1)S(1)}, f16[4,4,1,1,1,1,16,128]{7,6,1,0,5,4,3,2:T(8,128)(2,1)S(1)}, u32[]{:S(2)}, u32[]{:S(2)}) collective-permute-start(f16[4,4,1,1,1,1,16,128]{7,6,1,0,5,4,3,2:T(8,128)(2,1)S(1)} %slice_convert_fusion.17), channel_id=1, source_target_pairs={{2,4},{4,2},{6,0},{0,6},{3,5},{5,3},{7,1},{1,7},{10,12},{12,10},{1... | collective-permute-start | bytes 196616 | tf_op jit(solution)/shard_map/ppermute | solution.py:111
  78.7 2.1 %collective-permute-done.14 = f16[4,4,1,1,1,1,16,128]{7,6,1,0,5,4,3,2:T(8,128)(2,1)S(1)} collective-permute-done((f16[4,4,1,1,1,1,16,128]{7,6,1,0,5,4,3,2:T(8,128)(2,1)S(1)}, f16[4,4,1,1,1,1,16,128]{7,6,1,0,5,4,3,2:T(8,128)(2,1)S(1)}, u32[]{:S(2)}, u32[]{:S(2)}) %collective-permute-start.14) | collective-permute-done | bytes 65568 | tf_op jit(solution)/shard_map/ppermute | solution.py:111
  82.1 11.3 %all_to_all.5 = f16[8,2,64,128]{3,2,1,0:T(8,128)(2,1)S(1)} all-to-all(f16[8,2,64,128]{3,2,1,0:T(8,128)(2,1)S(1)} %bitcast.119), channel_id=1, replica_groups=mesh['mat'=4,'y'=4,'zh'=2,'x'=4,'core'=2] {'zh','mat'}, dimensions={0} | all-to-all | bytes 524288 | tf_op jit(solution)/shard_map/all_to_all | solution.py:116
  93.5 3.6 %fusion = f32[16384,64]{0,1:T(8,128)S(1)} fusion(f32[4,64]{1,0:T(4,128)S(1)} %copy-done.8, f32[1,4,128,128]{3,2,1,0:T(8,128)S(1)} %bitcast.118), kind=kOutput, calls=%fused_computation.1 | convolution fusion | flops 51380224 | bytes 4457472 | tf_op jit(solution)/shard_map/dot_general | solution.py:119
  97.2 2.3 %fusion.81 = f32[16384,8]{0,1:T(8,128)S(1)} fusion(f32[16384,64]{0,1:T(8,128)S(1)} %fusion, f32[8,64]{1,0:T(8,128)S(1)} %copy-done.7), kind=kOutput, calls=%fused_computation.210 | convolution fusion | flops 100663296 | bytes 4720640 | tf_op jit(solution)/shard_map/dot_general | solution.py:120
  99.5 12.8 %collective-permute-start.20 = (f32[8,1,8192]{2,0,1:T(8,128)S(1)}, f32[8,1,8192]{2,0,1:T(8,128)S(1)}, u32[]{:S(2)}, u32[]{:S(2)}) collective-permute-start(f32[8,1,8192]{2,0,1:T(8,128)S(1)} %get-tuple-element.29), channel_id=1, source_target_pairs={{0,1},{1,2},{2,3},{3,4},{4,5},{5,6},{6,7},{7,8},{8,9},{9,10},{10,1... | collective-permute-start | bytes 786440 | tf_op jit(solution)/shard_map/ppermute | solution.py:127
  112.3 1.9 %collective-permute-start.21 = (f32[8,1,8192]{2,0,1:T(8,128)S(1)}, f32[8,1,8192]{2,0,1:T(8,128)S(1)}, u32[]{:S(2)}, u32[]{:S(2)}) collective-permute-start(f32[8,1,8192]{2,0,1:T(8,128)S(1)} %get-tuple-element.30), channel_id=1, source_target_pairs={{1,0},{2,1},{3,2},{4,3},{5,4},{6,5},{7,6},{8,7},{9,8},{10,9},{11,1... | collective-permute-start | bytes 786440 | tf_op jit(solution)/shard_map/ppermute | solution.py:128
  114.3 2.6 %collective-permute-done.20 = f32[8,1,8192]{2,0,1:T(8,128)S(1)} collective-permute-done((f32[8,1,8192]{2,0,1:T(8,128)S(1)}, f32[8,1,8192]{2,0,1:T(8,128)S(1)}, u32[]{:S(2)}, u32[]{:S(2)}) %collective-permute-start.20) | collective-permute-done | bytes 262176 | tf_op jit(solution)/shard_map/ppermute | solution.py:127
  116.9 16.0 %collective-permute-done.21 = f32[8,1,8192]{2,0,1:T(8,128)S(1)} collective-permute-done((f32[8,1,8192]{2,0,1:T(8,128)S(1)}, f32[8,1,8192]{2,0,1:T(8,128)S(1)}, u32[]{:S(2)}, u32[]{:S(2)}) %collective-permute-start.21) | collective-permute-done | bytes 262176 | tf_op jit(solution)/shard_map/ppermute | solution.py:128
  (111 shorter events, 30.8 us)
Async XLA Ops:
  11.1 28.7 %collective-permute-start = (f16[4,2,2,2,2,2,16,128]{7,6,5,4,3,2,1,0:T(8,128)(2,1)}, f16[4,2,2,2,2,2,16,128]{7,6,5,4,3,2,1,0:T(8,128)(2,1)}, u32[]{:S(2)}, u32[]{:S(2)}) collective-permute-start(f16[4,2,2,2,2,2,16,128]{7,6,5,4,3,2,1,0:T(8,128)(2,1)} %get-tuple-element.14), channel_id=1, source_target_pairs={{0,1},{1,0},{2,3},{3,2},{4,5},{5,4},{6,7},{7,6},{8,9},{9,8},{10,11... | collective-permute-start | bytes 1572872 | tf_op jit(solution)/shard_map/ppermute | solution.py:102
  19.5 23.3 %collective-permute-start.5 = (f16[4,2,2,2,2,2,16,128]{7,6,5,4,3,2,1,0:T(8,128)(2,1)}, f16[4,2,2,2,2,2,16,128]{7,6,5,4,3,2,1,0:T(8,128)(2,1)}, u32[]{:S(2)}, u32[]{:S(2)}) collective-permute-start(f16[4,2,2,2,2,2,16,128]{7,6,5,4,3,2,1,0:T(8,128)(2,1)} %get-tuple-element.16), channel_id=1, source_target_pairs={{0,1},{1,0},{2,3},{3,2},{4,5},{5,4},{6,7},{7,6},{8,9},{9,8},{10,11... | collective-permute-start | bytes 1572872 | tf_op jit(solution)/shard_map/ppermute | solution.py:102
  27.3 18.6 %collective-permute-start.10 = (f16[4,2,2,2,2,2,16,128]{7,6,5,4,3,2,1,0:T(8,128)(2,1)}, f16[4,2,2,2,2,2,16,128]{7,6,5,4,3,2,1,0:T(8,128)(2,1)}, u32[]{:S(2)}, u32[]{:S(2)}) collective-permute-start(f16[4,2,2,2,2,2,16,128]{7,6,5,4,3,2,1,0:T(8,128)(2,1)} %get-tuple-element.18), channel_id=1, source_target_pairs={{0,1},{1,0},{2,3},{3,2},{4,5},{5,4},{6,7},{7,6},{8,9},{9,8},{10,11... | collective-permute-start | bytes 1572872 | tf_op jit(solution)/shard_map/ppermute | solution.py:102
  35.5 13.4 %collective-permute-start.15 = (f16[4,2,2,2,2,2,16,128]{7,6,5,4,3,2,1,0:T(8,128)(2,1)}, f16[4,2,2,2,2,2,16,128]{7,6,5,4,3,2,1,0:T(8,128)(2,1)}, u32[]{:S(2)}, u32[]{:S(2)}) collective-permute-start(f16[4,2,2,2,2,2,16,128]{7,6,5,4,3,2,1,0:T(8,128)(2,1)} %get-tuple-element.20), channel_id=1, source_target_pairs={{0,1},{1,0},{2,3},{3,2},{4,5},{5,4},{6,7},{7,6},{8,9},{9,8},{10,11... | collective-permute-start | bytes 1572872 | tf_op jit(solution)/shard_map/ppermute | solution.py:102
  42.1 13.1 %collective-permute-start.1 = (f16[4,4,1,2,2,2,16,128]{7,6,1,0,5,4,3,2:T(8,128)(2,1)S(1)}, f16[4,4,1,2,2,2,16,128]{7,6,1,0,5,4,3,2:T(8,128)(2,1)S(1)}, u32[]{:S(2)}, u32[]{:S(2)}) collective-permute-start(f16[4,4,1,2,2,2,16,128]{7,6,1,0,5,4,3,2:T(8,128)(2,1)S(1)} %slice_convert_fusion.6), channel_id=1, source_target_pairs={{0,2},{2,0},{4,6},{6,4},{1,3},{3,1},{5,7},{7,5},{8,10},{10,8},{12,... | collective-permute-start | bytes 1572872 | tf_op jit(solution)/shard_map/ppermute | solution.py:111
  45.0 14.0 %collective-permute-start.6 = (f16[4,4,2,1,2,2,16,128]{7,6,1,0,5,4,3,2:T(8,128)(2,1)S(1)}, f16[4,4,2,1,2,2,16,128]{7,6,1,0,5,4,3,2:T(8,128)(2,1)S(1)}, u32[]{:S(2)}, u32[]{:S(2)}) collective-permute-start(f16[4,4,2,1,2,2,16,128]{7,6,1,0,5,4,3,2:T(8,128)(2,1)S(1)} %slice_convert_fusion.4), channel_id=1, source_target_pairs={{2,4},{4,2},{6,0},{0,6},{3,5},{5,3},{7,1},{1,7},{10,12},{12,10},{1... | collective-permute-start | bytes 1572872 | tf_op jit(solution)/shard_map/ppermute | solution.py:111
  48.2 12.7 %collective-permute-start.11 = (f16[4,4,2,2,1,2,16,128]{7,6,1,0,5,4,3,2:T(8,128)(2,1)S(1)}, f16[4,4,2,2,1,2,16,128]{7,6,1,0,5,4,3,2:T(8,128)(2,1)S(1)}, u32[]{:S(2)}, u32[]{:S(2)}) collective-permute-start(f16[4,4,2,2,1,2,16,128]{7,6,1,0,5,4,3,2:T(8,128)(2,1)S(1)} %slice_convert_fusion.2), channel_id=1, source_target_pairs={{0,16},{16,0},{32,48},{48,32},{1,17},{17,1},{33,49},{49,33},{2,18}... | collective-permute-start | bytes 1572872 | tf_op jit(solution)/shard_map/ppermute | solution.py:111
  51.1 13.4 %collective-permute-start.16 = (f16[4,4,2,2,2,1,16,128]{7,6,1,0,5,4,3,2:T(8,128)(2,1)S(1)}, f16[4,4,2,2,2,1,16,128]{7,6,1,0,5,4,3,2:T(8,128)(2,1)S(1)}, u32[]{:S(2)}, u32[]{:S(2)}) collective-permute-start(f16[4,4,2,2,2,1,16,128]{7,6,1,0,5,4,3,2:T(8,128)(2,1)S(1)} %slice_convert_fusion), channel_id=1, source_target_pairs={{16,32},{32,16},{48,0},{0,48},{17,33},{33,17},{49,1},{1,49},{18,34... | collective-permute-start | bytes 1572872 | tf_op jit(solution)/shard_map/ppermute | solution.py:111
  55.5 11.2 %collective-permute-start.2 = (f16[4,4,1,2,1,2,16,128]{7,6,1,0,5,4,3,2:T(8,128)(2,1)S(1)}, f16[4,4,1,2,1,2,16,128]{7,6,1,0,5,4,3,2:T(8,128)(2,1)S(1)}, u32[]{:S(2)}, u32[]{:S(2)}) collective-permute-start(f16[4,4,1,2,1,2,16,128]{7,6,1,0,5,4,3,2:T(8,128)(2,1)S(1)} %slice_convert_fusion.11), channel_id=1, source_target_pairs={{0,16},{16,0},{32,48},{48,32},{1,17},{17,1},{33,49},{49,33},{2,18}... | collective-permute-start | bytes 786440 | tf_op jit(solution)/shard_map/ppermute | solution.py:111
  59.2 11.0 %collective-permute-start.7 = (f16[4,4,2,1,2,1,16,128]{7,6,1,0,5,4,3,2:T(8,128)(2,1)S(1)}, f16[4,4,2,1,2,1,16,128]{7,6,1,0,5,4,3,2:T(8,128)(2,1)S(1)}, u32[]{:S(2)}, u32[]{:S(2)}) collective-permute-start(f16[4,4,2,1,2,1,16,128]{7,6,1,0,5,4,3,2:T(8,128)(2,1)S(1)} %slice_convert_fusion.10), channel_id=1, source_target_pairs={{16,32},{32,16},{48,0},{0,48},{17,33},{33,17},{49,1},{1,49},{18,34... | collective-permute-start | bytes 786440 | tf_op jit(solution)/shard_map/ppermute | solution.py:111
  61.1 9.7 %collective-permute-start.12 = (f16[4,4,1,2,1,2,16,128]{7,6,1,0,5,4,3,2:T(8,128)(2,1)S(1)}, f16[4,4,1,2,1,2,16,128]{7,6,1,0,5,4,3,2:T(8,128)(2,1)S(1)}, u32[]{:S(2)}, u32[]{:S(2)}) collective-permute-start(f16[4,4,1,2,1,2,16,128]{7,6,1,0,5,4,3,2:T(8,128)(2,1)S(1)} %slice_convert_fusion.9), channel_id=1, source_target_pairs={{0,2},{2,0},{4,6},{6,4},{1,3},{3,1},{5,7},{7,5},{8,10},{10,8},{12,... | collective-permute-start | bytes 786440 | tf_op jit(solution)/shard_map/ppermute | solution.py:111
  64.8 7.0 %collective-permute-start.17 = (f16[4,4,2,1,2,1,16,128]{7,6,1,0,5,4,3,2:T(8,128)(2,1)S(1)}, f16[4,4,2,1,2,1,16,128]{7,6,1,0,5,4,3,2:T(8,128)(2,1)S(1)}, u32[]{:S(2)}, u32[]{:S(2)}) collective-permute-start(f16[4,4,2,1,2,1,16,128]{7,6,1,0,5,4,3,2:T(8,128)(2,1)S(1)} %slice_convert_fusion.8), channel_id=1, source_target_pairs={{2,4},{4,2},{6,0},{0,6},{3,5},{5,3},{7,1},{1,7},{10,12},{12,10},{1... | collective-permute-start | bytes 786440 | tf_op jit(solution)/shard_map/ppermute | solution.py:111
  66.8 5.9 %collective-permute-start.3 = (f16[4,4,1,1,1,2,16,128]{7,6,1,0,5,4,3,2:T(8,128)(2,1)S(1)}, f16[4,4,1,1,1,2,16,128]{7,6,1,0,5,4,3,2:T(8,128)(2,1)S(1)}, u32[]{:S(2)}, u32[]{:S(2)}) collective-permute-start(f16[4,4,1,1,1,2,16,128]{7,6,1,0,5,4,3,2:T(8,128)(2,1)S(1)} %slice_convert_fusion.15), channel_id=1, source_target_pairs={{2,4},{4,2},{6,0},{0,6},{3,5},{5,3},{7,1},{1,7},{10,12},{12,10},{1... | collective-permute-start | bytes 393224 | tf_op jit(solution)/shard_map/ppermute | solution.py:111
  70.3 4.2 %collective-permute-start.8 = (f16[4,4,1,1,2,1,16,128]{7,6,1,0,5,4,3,2:T(8,128)(2,1)S(1)}, f16[4,4,1,1,2,1,16,128]{7,6,1,0,5,4,3,2:T(8,128)(2,1)S(1)}, u32[]{:S(2)}, u32[]{:S(2)}) collective-permute-start(f16[4,4,1,1,2,1,16,128]{7,6,1,0,5,4,3,2:T(8,128)(2,1)S(1)} %slice_convert_fusion.14), channel_id=1, source_target_pairs={{0,2},{2,0},{4,6},{6,4},{1,3},{3,1},{5,7},{7,5},{8,10},{10,8},{12,... | collective-permute-start | bytes 393224 | tf_op jit(solution)/shard_map/ppermute | solution.py:111
  70.8 5.4 %collective-permute-start.13 = (f16[4,4,1,2,1,1,16,128]{7,6,1,0,5,4,3,2:T(8,128)(2,1)S(1)}, f16[4,4,1,2,1,1,16,128]{7,6,1,0,5,4,3,2:T(8,128)(2,1)S(1)}, u32[]{:S(2)}, u32[]{:S(2)}) collective-permute-start(f16[4,4,1,2,1,1,16,128]{7,6,1,0,5,4,3,2:T(8,128)(2,1)S(1)} %slice_convert_fusion.13), channel_id=1, source_target_pairs={{16,32},{32,16},{48,0},{0,48},{17,33},{33,17},{49,1},{1,49},{18,34... | collective-permute-start | bytes 393224 | tf_op jit(solution)/shard_map/ppermute | solution.py:111
  71.8 6.4 %collective-permute-start.18 = (f16[4,4,2,1,1,1,16,128]{7,6,1,0,5,4,3,2:T(8,128)(2,1)S(1)}, f16[4,4,2,1,1,1,16,128]{7,6,1,0,5,4,3,2:T(8,128)(2,1)S(1)}, u32[]{:S(2)}, u32[]{:S(2)}) collective-permute-start(f16[4,4,2,1,1,1,16,128]{7,6,1,0,5,4,3,2:T(8,128)(2,1)S(1)} %slice_convert_fusion.12), channel_id=1, source_target_pairs={{0,16},{16,0},{32,48},{48,32},{1,17},{17,1},{33,49},{49,33},{2,18}... | collective-permute-start | bytes 393224 | tf_op jit(solution)/shard_map/ppermute | solution.py:111
  72.7 5.8 %collective-permute-start.4 = (f16[4,4,1,1,1,1,16,128]{7,6,1,0,5,4,3,2:T(8,128)(2,1)S(1)}, f16[4,4,1,1,1,1,16,128]{7,6,1,0,5,4,3,2:T(8,128)(2,1)S(1)}, u32[]{:S(2)}, u32[]{:S(2)}) collective-permute-start(f16[4,4,1,1,1,1,16,128]{7,6,1,0,5,4,3,2:T(8,128)(2,1)S(1)} %slice_convert_fusion.19), channel_id=1, source_target_pairs={{16,32},{32,16},{48,0},{0,48},{17,33},{33,17},{49,1},{1,49},{18,34... | collective-permute-start | bytes 196616 | tf_op jit(solution)/shard_map/ppermute | solution.py:111
  74.5 4.1 %collective-permute-start.9 = (f16[4,4,1,1,1,1,16,128]{7,6,1,0,5,4,3,2:T(8,128)(2,1)S(1)}, f16[4,4,1,1,1,1,16,128]{7,6,1,0,5,4,3,2:T(8,128)(2,1)S(1)}, u32[]{:S(2)}, u32[]{:S(2)}) collective-permute-start(f16[4,4,1,1,1,1,16,128]{7,6,1,0,5,4,3,2:T(8,128)(2,1)S(1)} %slice_convert_fusion.18), channel_id=1, source_target_pairs={{0,16},{16,0},{32,48},{48,32},{1,17},{17,1},{33,49},{49,33},{2,18}... | collective-permute-start | bytes 196616 | tf_op jit(solution)/shard_map/ppermute | solution.py:111
  76.3 4.4 %collective-permute-start.14 = (f16[4,4,1,1,1,1,16,128]{7,6,1,0,5,4,3,2:T(8,128)(2,1)S(1)}, f16[4,4,1,1,1,1,16,128]{7,6,1,0,5,4,3,2:T(8,128)(2,1)S(1)}, u32[]{:S(2)}, u32[]{:S(2)}) collective-permute-start(f16[4,4,1,1,1,1,16,128]{7,6,1,0,5,4,3,2:T(8,128)(2,1)S(1)} %slice_convert_fusion.17), channel_id=1, source_target_pairs={{2,4},{4,2},{6,0},{0,6},{3,5},{5,3},{7,1},{1,7},{10,12},{12,10},{1... | collective-permute-start | bytes 196616 | tf_op jit(solution)/shard_map/ppermute | solution.py:111
  78.2 3.2 %collective-permute-start.19 = (f16[4,4,1,1,1,1,16,128]{7,6,1,0,5,4,3,2:T(8,128)(2,1)S(1)}, f16[4,4,1,1,1,1,16,128]{7,6,1,0,5,4,3,2:T(8,128)(2,1)S(1)}, u32[]{:S(2)}, u32[]{:S(2)}) collective-permute-start(f16[4,4,1,1,1,1,16,128]{7,6,1,0,5,4,3,2:T(8,128)(2,1)S(1)} %slice_convert_fusion.16), channel_id=1, source_target_pairs={{0,2},{2,0},{4,6},{6,4},{1,3},{3,1},{5,7},{7,5},{8,10},{10,8},{12,... | collective-permute-start | bytes 196616 | tf_op jit(solution)/shard_map/ppermute | solution.py:111
  97.2 17.1 %copy-start.9 = (f32[8]{0:T(128)S(1)}, f32[8]{0:T(128)}, u32[]{:S(2)}) copy-start(f32[8]{0:T(128)} %param.11) | copy-start | bytes 100
  99.5 34.7 %copy-start.1 = (bf16[1,512,1,1024]{3,1,2,0:T(8,128)(2,1)S(1)}, bf16[1,512,1,1024]{3,1,2,0:T(8,128)(2,1)}, u32[]{:S(2)}) copy-start(bf16[1,512,1,1024]{3,1,2,0:T(8,128)(2,1)} %param.6) | copy-start | bytes 3145732
  99.5 17.4 %collective-permute-start.20 = (f32[8,1,8192]{2,0,1:T(8,128)S(1)}, f32[8,1,8192]{2,0,1:T(8,128)S(1)}, u32[]{:S(2)}, u32[]{:S(2)}) collective-permute-start(f32[8,1,8192]{2,0,1:T(8,128)S(1)} %get-tuple-element.29), channel_id=1, source_target_pairs={{0,1},{1,2},{2,3},{3,4},{4,5},{5,6},{6,7},{7,8},{8,9},{9,10},{10,1... | collective-permute-start | bytes 786440 | tf_op jit(solution)/shard_map/ppermute | solution.py:127
  112.3 20.5 %collective-permute-start.21 = (f32[8,1,8192]{2,0,1:T(8,128)S(1)}, f32[8,1,8192]{2,0,1:T(8,128)S(1)}, u32[]{:S(2)}, u32[]{:S(2)}) collective-permute-start(f32[8,1,8192]{2,0,1:T(8,128)S(1)} %get-tuple-element.30), channel_id=1, source_target_pairs={{1,0},{2,1},{3,2},{4,3},{5,4},{6,5},{7,6},{8,7},{9,8},{10,9},{11,1... | collective-permute-start | bytes 786440 | tf_op jit(solution)/shard_map/ppermute | solution.py:128
  (8 other events, 30.2 us)

commit v2 on v1

v2 whole, which is shorter than its diff:
```python
import functools

import jax
import jax.numpy as jnp
from jax import lax
from jax.experimental import pallas as pl
from jax.experimental.pallas import tpu as pltpu
from jax.sharding import Mesh, PartitionSpec as P

PB = 128
PBLK = 4
CBINS = 8
EBINS = 64
MATS = 4
AXES = ("mat", "y", "zh", "x", "core")
TILE_AXES = ("y", "zh", "x", "core")
PAIRS = ([(0, 1), (1, 0), (2, 3), (3, 2)], [(1, 2), (2, 1), (3, 0), (0, 3)])
ORDERS = (
    (("x", 0), ("y", 0), ("x", 1), ("y", 1)),
    (("x", 1), ("y", 1), ("x", 0), ("y", 0)),
    (("y", 0), ("x", 0), ("y", 1), ("x", 1)),
    (("y", 1), ("x", 1), ("y", 0), ("x", 0)),
)
DIM_OF = {("x", 0): 2, ("x", 1): 3, ("y", 0): 4, ("y", 1): 5}


def pair_bits(i):
    return ((i + 1) // 2) % 2, i // 2


def row_order(slice_count):
    pos = jnp.arange(slice_count, dtype=jnp.int32)
    bits = [(pos // (256 >> n)) % 2 for n in range(5)]
    rest = pos % 16
    core = bits[0] ^ lax.axis_index("core")

    def place(b0, b1, name):
        mine = pair_bits(lax.axis_index(name))
        b0, b1 = b0 ^ mine[0], b1 ^ mine[1]
        return 2 * b1 + (b0 ^ b1)

    x = place(bits[1], bits[2], "x")
    y = place(bits[3], bits[4], "y")
    mat, zh, r = rest // 4, (rest // 2) % 2, rest % 2
    return mat * 128 + y * 32 + zh * 16 + x * 4 + core * 2 + r


def vmem_params(mib):
    return pltpu.CompilerParams(vmem_limit_bytes=mib << 20)


VMEM = pl.BlockSpec(memory_space=pltpu.VMEM)
SMEM = pl.BlockSpec(memory_space=pltpu.SMEM)
HBM = pl.BlockSpec(memory_space=pltpu.HBM)


def multiply(columns, matrix_ref, own_hbm, away_hbm, buf, sems):
    weights = jnp.swapaxes(matrix_ref[...], 0, 1)
    half = columns.shape[0] // 2
    copies = []
    for v in range(4):
        pair = jnp.concatenate([weights[2 * v], weights[2 * v + 1]], axis=1)
        got = jnp.dot(columns, pair, preferred_element_type=jnp.float32)
        buf[v, 0] = got[:, :PB]
        buf[v, 1] = got[:, PB:]
        copies.append(pltpu.make_async_copy(buf.at[v, :, pl.ds(half, half), :], away_hbm.at[v], sems.at[2 * v]))
        copies.append(pltpu.make_async_copy(buf.at[v, :, pl.ds(0, half), :], own_hbm.at[v], sems.at[2 * v + 1]))
        copies[-2].start()
        copies[-1].start()
    return copies


def wait_all(copies):
    for copy in copies:
        copy.wait()


def first_body(
    order_ref, vol_hbm, sys_hbm, own_hbm, away_hbm, col_ref, m1_ref, m2_ref, m3_ref, vol_buf, m0_buf, buf, sems, out_sems
):
    copies = [pltpu.make_async_copy(vol_hbm, vol_buf, sems.at[4])]
    for w, target in enumerate((m0_buf, m1_ref, m2_ref, m3_ref)):
        copies.append(pltpu.make_async_copy(sys_hbm.at[:, pl.ds(8 * w, 8), :], target, sems.at[w]))
    for copy in copies:
        copy.start()
    rows = vol_buf.shape[0]
    chosen = (order_ref[...] == lax.broadcasted_iota(jnp.int32, (rows, rows), 1)).astype(jnp.bfloat16)
    copies[0].wait()
    columns = jnp.dot(chosen, vol_buf[...], preferred_element_type=jnp.float32).astype(jnp.bfloat16)
    col_ref[...] = columns
    copies[1].wait()
    outs = multiply(columns, m0_buf, own_hbm, away_hbm, buf, out_sems)
    wait_all(copies[2:])
    wait_all(outs)


def in_hbm(x):
    return pltpu.with_memory_space_constraint(x, pltpu.HBM)


def project_first(order, vol, matrix):
    rows, depth = vol.shape
    half = pltpu.HBM((4, 2, rows // 2, PB), jnp.float32)
    part = pltpu.VMEM((depth, 8, PB), jnp.bfloat16)
    return pl.pallas_call(
        first_body,
        in_specs=[VMEM, HBM, HBM],
        out_specs=[HBM] * 2 + [VMEM] * 4,
        out_shape=[half, half, pltpu.VMEM((rows, depth), jnp.bfloat16), part, part, part],
        scratch_shapes=[
            pltpu.VMEM((rows, depth), jnp.bfloat16),
            pltpu.VMEM((depth, 8, PB), jnp.bfloat16),
            pltpu.VMEM((4, 2, rows, PB), jnp.float32),
            pltpu.SemaphoreType.DMA((5,)),
            pltpu.SemaphoreType.DMA((8,)),
        ],
        cost_estimate=pl.CostEstimate(flops=2 * rows * depth * 12 * PB, transcendentals=0, bytes_accessed=12 << 20),
        compiler_params=vmem_params(16),
        name="project_first",
    )(order, in_hbm(vol), in_hbm(matrix))


def project_body(col_ref, matrix_ref, own_hbm, away_hbm, buf, out_sems):
    wait_all(multiply(col_ref[...], matrix_ref, own_hbm, away_hbm, buf, out_sems))


def project(columns, matrix):
    rows, depth = columns.shape
    half = pltpu.HBM((4, 2, rows // 2, PB), jnp.float32)
    return pl.pallas_call(
        project_body,
        in_specs=[VMEM, VMEM],
        out_specs=[HBM, HBM],
        out_shape=[half, half],
        scratch_shapes=[pltpu.VMEM((4, 2, rows, PB), jnp.float32), pltpu.SemaphoreType.DMA((8,))],
        cost_estimate=pl.CostEstimate(flops=2 * rows * depth * 8 * PB, transcendentals=0, bytes_accessed=5 << 20),
        compiler_params=vmem_params(10),
        name="project",
    )(columns, matrix)


def merge_body(first_ref, other_ref, own_any, got_any, out_ref, own_buf, got_buf, sems, *, portion, side):
    copies = []
    for v in range(4):
        copies.append(pltpu.make_async_copy(own_any.at[v, :, :, side], own_buf.at[v], sems.at[2 * v]))
        copies.append(pltpu.make_async_copy(got_any.at[v, :, :, side], got_buf.at[v], sems.at[2 * v + 1]))
    for copy in copies:
        copy.start()
    for v in range(4):
        wait_all(copies[2 * v : 2 * v + 2])
        first, other = first_ref[4 * portion + v], other_ref[4 * portion + v]
        for b in range(PBLK):
            mine = jnp.where(first == b, own_buf[v, 0], jnp.where(first + 1 == b, own_buf[v, 1], 0.0))
            theirs = jnp.where(other == b, got_buf[v, 0], jnp.where(other + 1 == b, got_buf[v, 1], 0.0))
            out_ref[v, b] = mine + theirs


ANY = pl.BlockSpec(memory_space=pl.ANY)


def merge(first, other, own, got, portion, bit, side):
    rows = own.shape[2] // 2
    cut = (1 << bit, rows >> bit)
    own, got = (t.reshape(4, 2, cut[0], 2, cut[1], PB) for t in (own, got))
    return pl.pallas_call(
        functools.partial(merge_body, portion=portion, side=side),
        in_specs=[SMEM, SMEM, ANY, ANY],
        out_specs=VMEM,
        out_shape=pltpu.VMEM((4, PBLK) + cut + (PB,), jnp.float32),
        scratch_shapes=[pltpu.VMEM((4, 2) + cut + (PB,), jnp.float32)] * 2 + [pltpu.SemaphoreType.DMA((8,))],
        cost_estimate=pl.CostEstimate(flops=1 << 30, transcendentals=0, bytes_accessed=2 << 20),
        compiler_params=vmem_params(4),
        name="merge_send" if side else "merge_keep",
    )(first, other, in_hbm(own), got)


def detect(table_ref, sums, passed):
    for e in range(EBINS):
        row = [table_ref[16 * e + m : 16 * e + m + 1, :] for m in range(MATS)]
        power = sums[0] * row[0]
        for m in range(1, MATS):
            power = power + sums[m] * row[m]
        passed[e] = jnp.exp(power)
    bins = [None] * CBINS
    for e in range(EBINS):
        value = passed[e]
        for c in range(CBINS):
            part = table_ref[16 * e + 4 + c : 16 * e + 5 + c, :] * value
            bins[c] = part if e == 0 else bins[c] + part
    return bins


DETECT_COST = pl.CostEstimate(flops=1 << 31, transcendentals=1 << 20, bytes_accessed=1 << 20)


def inner_body(cross_ref, place_ref, table_ref, sums_ref, near_ref, partial_ref, passed, passed_near):
    core = place_ref[0]

    def block(b, carry):
        own = detect(table_ref, [sums_ref[m, :, b] for m in range(MATS)], passed)
        near = detect(table_ref, [near_ref[m, b] for m in range(MATS)], passed_near)
        for c in range(CBINS):
            leak = cross_ref[c]
            for row in (0, 1):
                side = jnp.where(core == 1 - row, near[c], 0.0)
                partial_ref[c, row, b] = (1.0 - 2.0 * leak) * own[c][row] + leak * (own[c][1 - row] + side)
        return carry

    lax.fori_loop(0, PBLK, block, 0)


def inner(crosstalk, place, table, sums, near):
    rows = jax.ShapeDtypeStruct((CBINS,) + sums.shape[1:], jnp.float32)
    return pl.pallas_call(
        inner_body,
        in_specs=[SMEM] * 2 + [VMEM] * 3,
        out_specs=VMEM,
        out_shape=rows,
        scratch_shapes=[pltpu.VMEM((EBINS, 2, 16, PB), jnp.float32), pltpu.VMEM((EBINS, 16, PB), jnp.float32)],
        cost_estimate=DETECT_COST,
        compiler_params=vmem_params(8),
        name="inner",
    )(crosstalk, place, table, sums, near)


def finish_body(cross_ref, place_ref, table_ref, far_ref, partial_ref, out_ref, passed):
    core, present = place_ref[0], place_ref[1]

    def block(b, carry):
        far = detect(table_ref, [far_ref[m, b] for m in range(MATS)], passed)
        columns = pl.ds(pl.multiple_of(b * PB, PB), PB)
        for c in range(CBINS):
            side = cross_ref[c] * jnp.where(present == 1, far[c], 0.0)
            out_ref[c, core, :, columns] = partial_ref[c, core, b] + side
            out_ref[c, 1 - core, :, columns] = partial_ref[c, 1 - core, b]
        return carry

    lax.fori_loop(0, PBLK, block, 0)


def finish(crosstalk, place, table, far, partial):
    return pl.pallas_call(
        finish_body,
        in_specs=[SMEM] * 2 + [VMEM] * 3,
        out_specs=VMEM,
        out_shape=jax.ShapeDtypeStruct((CBINS, 2, 16, PBLK * PB), jnp.float32),
        scratch_shapes=[pltpu.VMEM((EBINS, 16, PB), jnp.float32)],
        cost_estimate=DETECT_COST,
        compiler_params=vmem_params(8),
        name="finish",
    )(crosstalk, place, table, far, partial)


def per_device(volume, system, geometry, attenuation, response, crosstalk):
    rows = volume.shape[1]
    depth = volume.shape[3]
    tile = lax.axis_index(TILE_AXES)
    vol = volume.reshape(rows, depth)
    order = row_order(rows)[:, None]
    matrix = system.reshape(depth, 32, PB)
    mine = lax.dynamic_index_in_dim(geometry, tile, 0, keepdims=False)
    partner = lax.dynamic_index_in_dim(geometry, tile ^ 1, 0, keepdims=False)

    own, away, columns, *rest = project_first(order, vol, matrix)
    crossing = [None] * 4
    current = [None] * 4

    def cross(w, own, away):
        crossing[w] = own, lax.ppermute(away, "core", [(0, 1), (1, 0)])

    def first_send(w):
        axis, which = ORDERS[w][0]
        return merge(mine, partner, *crossing[w], w, DIM_OF[axis, which] - 2, 1).astype(jnp.float16)

    cross(0, own, away)
    cross(1, *project(columns, rest[0]))
    cross(2, *project(columns, rest[1]))
    sends = [first_send(0)]
    sends[0], columns = lax.optimization_barrier((sends[0], columns))
    last = project(columns, rest[2])
    cross(3, *last)
    sends += [first_send(w) for w in range(1, 4)]
    keeps, sends[3] = lax.optimization_barrier((crossing, sends[3]))
    for w in range(4):
        axis, which = ORDERS[w][0]
        bit = DIM_OF[axis, which] - 2
        shape = [4, PBLK, 2, 2, 2, 2, 16, PB]
        shape[2 + bit] = 1
        got = lax.ppermute(sends[w], axis, PAIRS[which])
        keep = merge(mine, partner, *keeps[w], w, bit, 0)
        current[w] = [keep.reshape(shape), got.reshape(shape)]

    def total(parts):
        value = parts[0]
        for part in parts[1:]:
            value = value + part.astype(jnp.float32)
        return value

    for n in range(1, 4):
        sends = []
        for w in range(4):
            axis, which = ORDERS[w][n]
            dim = DIM_OF[axis, which]
            sent = total([lax.slice_in_dim(t, 1, 2, axis=dim) for t in current[w]]).astype(jnp.float16)
            current[w] = [lax.slice_in_dim(t, 0, 1, axis=dim) for t in current[w]]
            if n == 1:
                sent, kept = lax.optimization_barrier((sent, total(current[w])))
                current[w] = [kept]
            sends.append(sent)
        for w in range(4):
            axis, which = ORDERS[w][n]
            current[w].append(lax.ppermute(sends[w], axis, PAIRS[which]))
    for w in range(4):
        current[w] = total(current[w]).astype(jnp.float16)

    whole = jnp.concatenate([c.reshape(4, PBLK, MATS, 2, 2, PB) for c in current], axis=0)
    outgoing = whole.transpose(3, 2, 4, 1, 0, 5).reshape(8, 2, 64, PB)
    received = lax.all_to_all(outgoing, ("zh", "mat"), 0, 0, tiled=True)
    received = received.reshape(2, MATS, 2, PBLK, 16, PB).astype(jnp.float32)
    sums = received[0] + received[1]

    core = lax.axis_index("core")
    rounded = sums.astype(jnp.float16)
    top, bottom = rounded[:, 0], rounded[:, 1]
    axes = ("mat",) + TILE_AXES
    count = lax.axis_size(axes)
    me = lax.axis_index(axes)
    swap = [(i, i + 1) for i in range(1, count - 1, 2)]
    near = lax.ppermute(jnp.where(core == 0, bottom, top), "core", [(0, 1), (1, 0)])
    far = lax.ppermute(jnp.where(core == 0, top, bottom), axes, swap + [(j, i) for i, j in swap])
    present = jnp.logical_and(me > 0, me < count - 1).astype(jnp.int32)
    place = jnp.stack([core, present])
    table = jnp.concatenate([-attenuation.T, response.T, jnp.zeros((EBINS, 4), jnp.float32)], axis=1)
    table = jnp.broadcast_to(table.reshape(16 * EBINS, 1), (16 * EBINS, PB))
    partial = inner(crosstalk, place, table, sums, near.astype(jnp.float32))
    return finish(crosstalk, place, table, far.astype(jnp.float32), partial)


def solution(mesh):
    fine = Mesh(mesh.devices.reshape(4, 4, 2, 4, 2), AXES)
    in_specs = (P("mat", None, TILE_AXES, None), P(TILE_AXES, None, None, None), P(), P(), P(), P())
    out_specs = P(None, AXES, None, None)

    return jax.shard_map(per_device, mesh=fine, in_specs=in_specs, out_specs=out_specs, check_vma=False)
```

time: 135 us -> 108 us (0.80)
  the two profiles are of different devices: /device:TPU:223 before, /device:TPU:8 now
where the time goes in v2:
time: 108 us
  Pallas kernels  37 us (34%)
  starting transfers between devices  36.9 us (34%)
  waiting for transfers between devices  29.2 us (27%)
  other arithmetic  3.38 us (3%)
    ppermute x12, starting transfers between devices, per_device(): current[w].append(lax.ppermute(sends[w], axis, PAIRS[which]))  17.3 us
    pallas_call x8, Pallas kernels, merge(): pl.pallas_call(functools.partial(merge_body, portion=portion, side=side),...  15.1 us
    ppermute x12, waiting for transfers between devices, per_device(): current[w].append(lax.ppermute(sends[w], axis, PAIRS[which]))  13.3 us
    all_to_all x1, waiting for transfers between devices, per_device(): received = lax.all_to_all(outgoing, ('zh', 'mat'), 0, 0, tiled=True)  10.2 us
    all_to_all x1, starting transfers between devices, per_device(): received = lax.all_to_all(outgoing, ('zh', 'mat'), 0, 0, tiled=True)  8.6 us
    pallas_call x3, Pallas kernels, project(): pl.pallas_call(project_body, in_specs=[VMEM, VMEM], out_specs=[HBM, HBM],...  7 us
    pallas_call x1, Pallas kernels, inner(): pl.pallas_call(inner_body, in_specs=[SMEM] * 2 + [VMEM] * 3, out_specs=VM...  6.82 us
    ppermute x4, starting transfers between devices, per_device(): got = lax.ppermute(sends[w], axis, PAIRS[which])  6.1 us
  transfers between devices with their start and end apart: 23, of which 8 were waited for; matrix products, arithmetic and copies ran while one was open for 2% of the time, Pallas kernels for 27%

profile of v2, /device:TPU:8, one launch (start us, length us, event | category | flops | bytes accessed | tf_op | source)
XLA Modules:
  0.0 107.8 jit_solution(4748920473837321308)
XLA Ops:
  0.5 4.4 %project_first.1 = (f32[4,2,256,128]{3,2,1,0:T(8,128)}, f32[4,2,256,128]{3,2,1,0:T(8,128)}, bf16[512,1024]{1,0:T(8,128)(2,1)S(1)}, bf16[1024,8,128]{2,1,0:T(8,12...) custom-call(s32[512,1]{1,0:T(8,128)S(1)} %fusion.10.order_ref, ...), custom_call_target="tpu_custom_call" | custom-call | flops 1610612736 | bytes 12582912 | tf_op jit(solution)/shard_map/project_first/pallas_call | solution.py:105
  5.0 2.3 %project.4 = (f32[4,2,256,128]{3,2,1,0:T(8,128)}, f32[4,2,256,128]{3,2,1,0:T(8,128)}) custom-call(bf16[512,1024]{1,0:T(8,128)(2,1)S(1)} %get-tuple-element.45.col_ref, bf16[1024,8,128]{2,1,0:T(8,128)(2,1)S(1)} %get-tuple-element.42.matrix_ref), custom_call_target="tpu_custom_call" | custom-call | flops 1073741824 | bytes 5242880 | tf_op jit(solution)/shard_map/project/pallas_call | solution.py:130
  7.9 2.3 %project.3 = (f32[4,2,256,128]{3,2,1,0:T(8,128)}, f32[4,2,256,128]{3,2,1,0:T(8,128)}) custom-call(bf16[512,1024]{1,0:T(8,128)(2,1)S(1)} %get-tuple-element.45.col_ref, bf16[1024,8,128]{2,1,0:T(8,128)(2,1)S(1)} %get-tuple-element.39.matrix_ref), custom_call_target="tpu_custom_call" | custom-call | flops 1073741824 | bytes 5242880 | tf_op jit(solution)/shard_map/project/pallas_call | solution.py:130
  10.6 1.9 %merge_send.4 = f32[4,4,1,128,128]{4,3,2,1,0:T(8,128)S(1)} custom-call(s32[16]{0:T(128)S(1)} %get-tuple-element.68.first_ref, s32[16]{0:T(128)S(1)} %get-tuple-element.67.other_ref, f32[4,2,1,2,128,128]{5,4,3,2,1,0:T(8,128)} %bitcast.65, f32[4,2,1,2,128,128]{5,4,3,2,1,0:T(8,128)S(1)} %bitcast.49), custom_call_target="tpu_custom_call" | custom-call | flops 1073741824 | bytes 2097152 | tf_op jit(solution)/shard_map/merge_send/pallas_call | solution.py:165
  12.6 2.3 %project.5 = (f32[4,2,256,128]{3,2,1,0:T(8,128)}, f32[4,2,256,128]{3,2,1,0:T(8,128)}) custom-call(bf16[512,1024]{1,0:T(8,128)(2,1)S(1)} %copy-done.1, bf16[1024,8,128]{2,1,0:T(8,128)(2,1)S(1)} %get-tuple-element.46.matrix_ref), custom_call_target="tpu_custom_call" | custom-call | flops 1073741824 | bytes 5242880 | tf_op jit(solution)/shard_map/project/pallas_call | solution.py:130
  15.5 1.9 %merge_send.7 = f32[4,4,4,32,128]{4,3,2,1,0:T(8,128)S(1)} custom-call(s32[16]{0:T(128)S(1)} %get-tuple-element.68.first_ref, s32[16]{0:T(128)S(1)} %get-tuple-element.67.other_ref, f32[4,2,4,2,32,128]{5,4,3,2,1,0:T(8,128)} %bitcast.69, f32[4,2,4,2,32,128]{5,4,3,2,1,0:T(8,128)} %bitcast.26.got_any), custom_call_target="tpu_custom_call" | custom-call | flops 1073741824 | bytes 2097152 | tf_op jit(solution)/shard_map/merge_send/pallas_call | solution.py:165
  17.6 2.2 %collective-permute-start.12 = (f16[4,4,4,32,128]{4,3,2,1,0:T(8,128)(2,1)S(1)}, f16[4,4,4,32,128]{4,3,2,1,0:T(8,128)(2,1)S(1)}, u32[]{:S(2)}, u32[]{:S(2)}) collective-permute-start(f16[4,4,4,32,128]{4,3,2,1,0:T(8,128)(2,1)S(1)} %convert_element_type.197), channel_id=1, source_target_pairs={{0,16},{16,0},{32,48},{48,32},{1,17},{17,1},{33,49},{49,33},{2,18}... | collective-permute-start | bytes 1572872 | tf_op jit(solution)/shard_map/ppermute | solution.py:289
  19.8 1.9 %merge_send.6 = f32[4,4,2,64,128]{4,3,2,1,0:T(8,128)S(1)} custom-call(s32[16]{0:T(128)S(1)} %get-tuple-element.68.first_ref, s32[16]{0:T(128)S(1)} %get-tuple-element.67.other_ref, f32[4,2,2,2,64,128]{5,4,3,2,1,0:T(8,128)} %bitcast.67, f32[4,2,2,2,64,128]{5,4,3,2,1,0:T(8,128)} %bitcast.19.got_any), custom_call_target="tpu_custom_call" | custom-call | flops 1073741824 | bytes 2097152 | tf_op jit(solution)/shard_map/merge_send/pallas_call | solution.py:165
  25.1 2.5 %collective-permute-start.16 = (f16[4,4,8,16,128]{4,3,2,1,0:T(8,128)(2,1)S(1)}, f16[4,4,8,16,128]{4,3,2,1,0:T(8,128)(2,1)S(1)}, u32[]{:S(2)}, u32[]{:S(2)}) collective-permute-start(f16[4,4,8,16,128]{4,3,2,1,0:T(8,128)(2,1)S(1)} %convert_element_type.171), channel_id=1, source_target_pairs={{16,32},{32,16},{48,0},{0,48},{17,33},{33,17},{49,1},{1,49},{18,34... | collective-permute-start | bytes 1572872 | tf_op jit(solution)/shard_map/ppermute | solution.py:289
  27.6 1.9 %merge_keep.6 = f32[4,4,4,32,128]{4,3,2,1,0:T(8,128)S(1)} custom-call(s32[16]{0:T(128)S(1)} %get-tuple-element.68.first_ref, s32[16]{0:T(128)S(1)} %get-tuple-element.67.other_ref, f32[4,2,4,2,32,128]{5,4,3,2,1,0:T(8,128)} %bitcast.70, f32[4,2,4,2,32,128]{5,4,3,2,1,0:T(8,128)} %bitcast.23.got_any), custom_call_target="tpu_custom_call" | custom-call | flops 1073741824 | bytes 2097152 | tf_op jit(solution)/shard_map/merge_keep/pallas_call | solution.py:165
  29.6 2.4 %collective-permute-done.12 = f16[4,4,4,32,128]{4,3,2,1,0:T(8,128)(2,1)S(1)} collective-permute-done((f16[4,4,4,32,128]{4,3,2,1,0:T(8,128)(2,1)S(1)}, f16[4,4,4,32,128]{4,3,2,1,0:T(8,128)(2,1)S(1)}, u32[]{:S(2)}, u32[]{:S(2)}) %collective-permute-start.12) | collective-permute-done | bytes 524320 | tf_op jit(solution)/shard_map/ppermute | solution.py:289
  33.5 1.9 %merge_keep.5 = f32[4,4,2,64,128]{4,3,2,1,0:T(8,128)S(1)} custom-call(s32[16]{0:T(128)S(1)} %get-tuple-element.68.first_ref, s32[16]{0:T(128)S(1)} %get-tuple-element.67.other_ref, f32[4,2,2,2,64,128]{5,4,3,2,1,0:T(8,128)} %bitcast.68, f32[4,2,2,2,64,128]{5,4,3,2,1,0:T(8,128)} %bitcast.16.got_any), custom_call_target="tpu_custom_call" | custom-call | flops 1073741824 | bytes 2097152 | tf_op jit(solution)/shard_map/merge_keep/pallas_call | solution.py:165
  45.0 2.9 %collective-permute-start.10 = (f16[4,4,1,1,2,1,16,128]{7,6,5,4,2,1,0,3:T(8,128)(2,1)S(1)}, f16[4,4,1,1,2,1,16,128]{7,6,5,4,2,1,0,3:T(8,128)(2,1)S(1)}, u32[]{:S(2)}, u32[]{:S(2)}) collective-permute-start(f16[4,4,1,1,2,1,16,128]{7,6,5,4,2,1,0,3:T(8,128)(2,1)S(1)} %add_convert_fusion.2), channel_id=1, source_target_pairs={{0,2},{2,0},{4,6},{6,4},{1,3},{3,1},{5,7},{7,5},{8,10},{10,8},{12,... | collective-permute-start | bytes 393224 | tf_op jit(solution)/shard_map/ppermute | solution.py:312
  51.4 2.2 %collective-permute-start.11 = (f16[4,4,1,1,1,1,16,128]{7,6,5,4,2,1,0,3:T(8,128)(2,1)S(1)}, f16[4,4,1,1,1,1,16,128]{7,6,5,4,2,1,0,3:T(8,128)(2,1)S(1)}, u32[]{:S(2)}, u32[]{:S(2)}) collective-permute-start(f16[4,4,1,1,1,1,16,128]{7,6,5,4,2,1,0,3:T(8,128)(2,1)S(1)} %add_convert_fusion.9), channel_id=1, source_target_pairs={{0,16},{16,0},{32,48},{48,32},{1,17},{17,1},{33,49},{49,33},{2,18}... | collective-permute-start | bytes 196616 | tf_op jit(solution)/shard_map/ppermute | solution.py:312
  54.8 2.0 %collective-permute-start.7 = (f16[4,4,1,1,1,1,16,128]{7,6,5,4,3,1,0,2:T(8,128)(2,1)S(1)}, f16[4,4,1,1,1,1,16,128]{7,6,5,4,3,1,0,2:T(8,128)(2,1)S(1)}, u32[]{:S(2)}, u32[]{:S(2)}) collective-permute-start(f16[4,4,1,1,1,1,16,128]{7,6,5,4,3,1,0,2:T(8,128)(2,1)S(1)} %add_convert_fusion.11), channel_id=1, source_target_pairs={{16,32},{32,16},{48,0},{0,48},{17,33},{33,17},{49,1},{1,49},{18,34... | collective-permute-start | bytes 196616 | tf_op jit(solution)/shard_map/ppermute | solution.py:312
  56.9 4.6 %collective-permute-done.17 = f16[4,4,2,1,2,1,16,128]{7,6,4,3,2,1,0,5:T(8,128)(2,1)S(1)} collective-permute-done((f16[4,4,2,1,2,1,16,128]{7,6,4,3,2,1,0,5:T(8,128)(2,1)S(1)}, f16[4,4,2,1,2,1,16,128]{7,6,4,3,2,1,0,5:T(8,128)(2,1)S(1)}, u32[]{:S(2)}, u32[]{:S(2)}) %collective-permute-start.17) | collective-permute-done | bytes 262176 | tf_op jit(solution)/shard_map/ppermute | solution.py:312
  62.2 4.4 %collective-permute-done.18 = f16[4,4,2,1,1,1,16,128]{7,6,4,3,2,1,0,5:T(8,128)(2,1)S(1)} collective-permute-done((f16[4,4,2,1,1,1,16,128]{7,6,4,3,2,1,0,5:T(8,128)(2,1)S(1)}, f16[4,4,2,1,1,1,16,128]{7,6,4,3,2,1,0,5:T(8,128)(2,1)S(1)}, u32[]{:S(2)}, u32[]{:S(2)}) %collective-permute-start.18) | collective-permute-done | bytes 131104 | tf_op jit(solution)/shard_map/ppermute | solution.py:312
  67.2 3.8 %collective-permute-done.19 = f16[4,4,1,1,1,1,16,128]{7,6,4,3,2,1,0,5:T(8,128)(2,1)S(1)} collective-permute-done((f16[4,4,1,1,1,1,16,128]{7,6,4,3,2,1,0,5:T(8,128)(2,1)S(1)}, f16[4,4,1,1,1,1,16,128]{7,6,4,3,2,1,0,5:T(8,128)(2,1)S(1)}, u32[]{:S(2)}, u32[]{:S(2)}) %collective-permute-start.19) | collective-permute-done | bytes 65568 | tf_op jit(solution)/shard_map/ppermute | solution.py:312
  72.1 8.6 %all-to-all-start = ((f16[8,2,64,128]{3,2,1,0:T(8,128)(2,1)}), f16[8,2,64,128]{3,2,1,0:T(8,128)(2,1)S(1)}, u32[]{:S(2)}, u32[]{:S(2)}) async-start(f16[8,2,64,128]{3,2,1,0:T(8,128)(2,1)} %bitcast.35), calls=%async_computation | async-start | bytes 524288 | tf_op jit(solution)/shard_map/all_to_all | solution.py:318
  81.0 10.2 %all-to-all-done = f16[8,2,64,128]{3,2,1,0:T(8,128)(2,1)S(1)} async-done(((f16[8,2,64,128]{3,2,1,0:T(8,128)(2,1)}), f16[8,2,64,128]{3,2,1,0:T(8,128)(2,1)S(1)}, u32[]{:S(2)}, u32[]{:S(2)}) %all-to-all-start) | async-done | bytes 262176 | tf_op jit(solution)/shard_map/all_to_all | solution.py:318
  91.5 3.4 %collective-permute-start.20 = (f16[4,4,16,128]{3,2,1,0:T(8,128)(2,1)S(1)}, f16[4,4,16,128]{3,2,1,0:T(8,128)(2,1)S(1)}, u32[]{:S(2)}, u32[]{:S(2)}) collective-permute-start(f16[4,4,16,128]{3,2,1,0:T(8,128)(2,1)S(1)} %get-tuple-element.78), channel_id=1, source_target_pairs={{1,2},{3,4},{5,6},{7,8},{9,10},{11,12},{13,14},{15,16},{17,18},{19... | collective-permute-start | bytes 196616 | tf_op jit(solution)/shard_map/ppermute | solution.py:330
  95.2 6.8 %inner.1.partial_ref = f32[8,2,4,16,128]{4,3,2,1,0:T(8,128)S(1)} custom-call(f32[8]{0:T(128)S(1)} %copy-done.2, s32[2]{0:T(128)S(1)} %pad_add_fusion.place_ref, f32[1024,128]{1,0:T(8,128)S(1)} %broadcast_in_dim.13.table_ref, f32[4,2,4,16,128]{4,3,2,1,0:T(8,128)S(1)} %bitcast.44, f32[4,4,16,128]{3,2,1,0:T(8,128)S(1)} %convert_element_type.225.near_ref), custom_call_target="tpu_custom_call" | custom-call | flops 2147483648 | bytes 1048576 | tf_op jit(solution)/shard_map/inner/pallas_call | solution.py:214
  102.0 2.0 %collective-permute-done.20 = f16[4,4,16,128]{3,2,1,0:T(8,128)(2,1)S(1)} collective-permute-done((f16[4,4,16,128]{3,2,1,0:T(8,128)(2,1)S(1)}, f16[4,4,16,128]{3,2,1,0:T(8,128)(2,1)S(1)}, u32[]{:S(2)}, u32[]{:S(2)}) %collective-permute-start.20) | collective-permute-done | bytes 65568 | tf_op jit(solution)/shard_map/ppermute | solution.py:330
  104.1 3.7 %finish.1 = f32[8,2,16,512]{3,2,1,0:T(8,128)} custom-call(f32[8]{0:T(128)S(1)} %copy-done.2, s32[2]{0:T(128)S(1)} %pad_add_fusion.place_ref, f32[1024,128]{1,0:T(8,128)S(1)} %broadcast_in_dim.13.table_ref, f32[4,4,16,128]{3,2,1,0:T(8,128)S(1)} %convert_element_type.224.far_ref, f32[8,2,4,16,128]{4,3,2,1,0:T(8,128)S(1)} %inner.1.partial_ref), custom_call_target="tpu_custom_call" | custom-call | flops 2147483648 | bytes 1048576 | tf_op jit(solution)/shard_map/finish/pallas_call | solution.py:242
  (90 shorter events, 24.6 us)
Async XLA Ops:
  4.9 5.7 %collective-permute-start = (f32[4,2,256,128]{3,2,1,0:T(8,128)}, f32[4,2,256,128]{3,2,1,0:T(8,128)S(1)}, u32[]{:S(2)}, u32[]{:S(2)}) collective-permute-start(f32[4,2,256,128]{3,2,1,0:T(8,128)} %get-tuple-element.37), channel_id=1, source_target_pairs={{0,1},{1,0},{2,3},{3,2},{4,5},{5,4},{6,7},{7,6},{8,9},{9,8},{10,11... | collective-permute-start | bytes 3145736 | tf_op jit(solution)/shard_map/ppermute | solution.py:269
  7.3 8.2 %collective-permute-start.2 = (f32[4,2,256,128]{3,2,1,0:T(8,128)}, f32[4,2,256,128]{3,2,1,0:T(8,128)}, u32[]{:S(2)}, u32[]{:S(2)}) collective-permute-start(f32[4,2,256,128]{3,2,1,0:T(8,128)} %get-tuple-element.44), channel_id=1, source_target_pairs={{0,1},{1,0},{2,3},{3,2},{4,5},{5,4},{6,7},{7,6},{8,9},{9,8},{10,11... | collective-permute-start | bytes 3145736 | tf_op jit(solution)/shard_map/ppermute | solution.py:269
  10.2 9.6 %collective-permute-start.1 = (f32[4,2,256,128]{3,2,1,0:T(8,128)}, f32[4,2,256,128]{3,2,1,0:T(8,128)}, u32[]{:S(2)}, u32[]{:S(2)}) collective-permute-start(f32[4,2,256,128]{3,2,1,0:T(8,128)} %get-tuple-element.41), channel_id=1, source_target_pairs={{0,1},{1,0},{2,3},{3,2},{4,5},{5,4},{6,7},{7,6},{8,9},{9,8},{10,11... | collective-permute-start | bytes 3145736 | tf_op jit(solution)/shard_map/ppermute | solution.py:269
  14.9 8.3 %collective-permute-start.3 = (f32[4,2,256,128]{3,2,1,0:T(8,128)}, f32[4,2,256,128]{3,2,1,0:T(8,128)S(1)}, u32[]{:S(2)}, u32[]{:S(2)}) collective-permute-start(f32[4,2,256,128]{3,2,1,0:T(8,128)} %get-tuple-element.48), channel_id=1, source_target_pairs={{0,1},{1,0},{2,3},{3,2},{4,5},{5,4},{6,7},{7,6},{8,9},{9,8},{10,11... | collective-permute-start | bytes 3145736 | tf_op jit(solution)/shard_map/ppermute | solution.py:269
  17.6 14.4 %collective-permute-start.12 = (f16[4,4,4,32,128]{4,3,2,1,0:T(8,128)(2,1)S(1)}, f16[4,4,4,32,128]{4,3,2,1,0:T(8,128)(2,1)S(1)}, u32[]{:S(2)}, u32[]{:S(2)}) collective-permute-start(f16[4,4,4,32,128]{4,3,2,1,0:T(8,128)(2,1)S(1)} %convert_element_type.197), channel_id=1, source_target_pairs={{0,16},{16,0},{32,48},{48,32},{1,17},{17,1},{33,49},{49,33},{2,18}... | collective-permute-start | bytes 1572872 | tf_op jit(solution)/shard_map/ppermute | solution.py:289
  21.9 14.9 %collective-permute-start.8 = (f16[4,4,2,64,128]{4,3,2,1,0:T(8,128)(2,1)S(1)}, f16[4,4,2,64,128]{4,3,2,1,0:T(8,128)(2,1)S(1)}, u32[]{:S(2)}, u32[]{:S(2)}) collective-permute-start(f16[4,4,2,64,128]{4,3,2,1,0:T(8,128)(2,1)S(1)} %convert_element_type.184), channel_id=1, source_target_pairs={{2,4},{4,2},{6,0},{0,6},{3,5},{5,3},{7,1},{1,7},{10,12},{12,10},{1... | collective-permute-start | bytes 1572872 | tf_op jit(solution)/shard_map/ppermute | solution.py:289
  23.0 16.6 %collective-permute-start.4 = (f16[4,4,1,128,128]{4,3,2,1,0:T(8,128)(2,1)S(1)}, f16[4,4,1,128,128]{4,3,2,1,0:T(8,128)(2,1)S(1)}, u32[]{:S(2)}, u32[]{:S(2)}) collective-permute-start(f16[4,4,1,128,128]{4,3,2,1,0:T(8,128)(2,1)S(1)} %convert_element_type.170), channel_id=1, source_target_pairs={{0,2},{2,0},{4,6},{6,4},{1,3},{3,1},{5,7},{7,5},{8,10},{10,8},{12,... | collective-permute-start | bytes 1572872 | tf_op jit(solution)/shard_map/ppermute | solution.py:289
  25.1 28.5 %collective-permute-start.16 = (f16[4,4,8,16,128]{4,3,2,1,0:T(8,128)(2,1)S(1)}, f16[4,4,8,16,128]{4,3,2,1,0:T(8,128)(2,1)S(1)}, u32[]{:S(2)}, u32[]{:S(2)}) collective-permute-start(f16[4,4,8,16,128]{4,3,2,1,0:T(8,128)(2,1)S(1)} %convert_element_type.171), channel_id=1, source_target_pairs={{16,32},{32,16},{48,0},{0,48},{17,33},{33,17},{49,1},{1,49},{18,34... | collective-permute-start | bytes 1572872 | tf_op jit(solution)/shard_map/ppermute | solution.py:289
  32.1 11.0 %collective-permute-start.13 = (f16[4,4,1,2,1,2,16,128]{7,6,5,3,2,1,0,4:T(8,128)(2,1)S(1)}, f16[4,4,1,2,1,2,16,128]{7,6,5,3,2,1,0,4:T(8,128)(2,1)S(1)}, u32[]{:S(2)}, u32[]{:S(2)}) collective-permute-start(f16[4,4,1,2,1,2,16,128]{7,6,5,3,2,1,0,4:T(8,128)(2,1)S(1)} %get-tuple-element.61), channel_id=1, source_target_pairs={{0,2},{2,0},{4,6},{6,4},{1,3},{3,1},{5,7},{7,5},{8,10},{10,8},{12,... | collective-permute-start | bytes 786440 | tf_op jit(solution)/shard_map/ppermute | solution.py:312
  37.0 8.0 %collective-permute-start.9 = (f16[4,4,2,1,2,1,16,128]{7,6,5,4,2,1,0,3:T(8,128)(2,1)S(1)}, f16[4,4,2,1,2,1,16,128]{7,6,5,4,2,1,0,3:T(8,128)(2,1)S(1)}, u32[]{:S(2)}, u32[]{:S(2)}) collective-permute-start(f16[4,4,2,1,2,1,16,128]{7,6,5,4,2,1,0,3:T(8,128)(2,1)S(1)} %get-tuple-element.57), channel_id=1, source_target_pairs={{16,32},{32,16},{48,0},{0,48},{17,33},{33,17},{49,1},{1,49},{18,34... | collective-permute-start | bytes 786440 | tf_op jit(solution)/shard_map/ppermute | solution.py:312
  39.8 8.0 %collective-permute-start.5 = (f16[4,4,1,2,1,2,16,128]{7,6,5,4,3,1,0,2:T(8,128)(2,1)S(1)}, f16[4,4,1,2,1,2,16,128]{7,6,5,4,3,1,0,2:T(8,128)(2,1)S(1)}, u32[]{:S(2)}, u32[]{:S(2)}) collective-permute-start(f16[4,4,1,2,1,2,16,128]{7,6,5,4,3,1,0,2:T(8,128)(2,1)S(1)} %get-tuple-element.53), channel_id=1, source_target_pairs={{0,16},{16,0},{32,48},{48,32},{1,17},{17,1},{33,49},{49,33},{2,18}... | collective-permute-start | bytes 786440 | tf_op jit(solution)/shard_map/ppermute | solution.py:312
  43.2 6.5 %collective-permute-start.14 = (f16[4,4,1,2,1,1,16,128]{7,6,5,3,2,1,0,4:T(8,128)(2,1)S(1)}, f16[4,4,1,2,1,1,16,128]{7,6,5,3,2,1,0,4:T(8,128)(2,1)S(1)}, u32[]{:S(2)}, u32[]{:S(2)}) collective-permute-start(f16[4,4,1,2,1,1,16,128]{7,6,5,3,2,1,0,4:T(8,128)(2,1)S(1)} %add_convert_fusion.1), channel_id=1, source_target_pairs={{16,32},{32,16},{48,0},{0,48},{17,33},{33,17},{49,1},{1,49},{18,34... | collective-permute-start | bytes 393224 | tf_op jit(solution)/shard_map/ppermute | solution.py:312
  45.0 6.4 %collective-permute-start.10 = (f16[4,4,1,1,2,1,16,128]{7,6,5,4,2,1,0,3:T(8,128)(2,1)S(1)}, f16[4,4,1,1,2,1,16,128]{7,6,5,4,2,1,0,3:T(8,128)(2,1)S(1)}, u32[]{:S(2)}, u32[]{:S(2)}) collective-permute-start(f16[4,4,1,1,2,1,16,128]{7,6,5,4,2,1,0,3:T(8,128)(2,1)S(1)} %add_convert_fusion.2), channel_id=1, source_target_pairs={{0,2},{2,0},{4,6},{6,4},{1,3},{3,1},{5,7},{7,5},{8,10},{10,8},{12,... | collective-permute-start | bytes 393224 | tf_op jit(solution)/shard_map/ppermute | solution.py:312
  47.9 6.8 %collective-permute-start.6 = (f16[4,4,1,1,1,2,16,128]{7,6,5,4,3,1,0,2:T(8,128)(2,1)S(1)}, f16[4,4,1,1,1,2,16,128]{7,6,5,4,3,1,0,2:T(8,128)(2,1)S(1)}, u32[]{:S(2)}, u32[]{:S(2)}) collective-permute-start(f16[4,4,1,1,1,2,16,128]{7,6,5,4,3,1,0,2:T(8,128)(2,1)S(1)} %add_convert_fusion.3), channel_id=1, source_target_pairs={{2,4},{4,2},{6,0},{0,6},{3,5},{5,3},{7,1},{1,7},{10,12},{12,10},{1... | collective-permute-start | bytes 393224 | tf_op jit(solution)/shard_map/ppermute | solution.py:312
  49.7 7.2 %collective-permute-start.15 = (f16[4,4,1,1,1,1,16,128]{7,6,5,3,2,1,0,4:T(8,128)(2,1)S(1)}, f16[4,4,1,1,1,1,16,128]{7,6,5,3,2,1,0,4:T(8,128)(2,1)S(1)}, u32[]{:S(2)}, u32[]{:S(2)}) collective-permute-start(f16[4,4,1,1,1,1,16,128]{7,6,5,3,2,1,0,4:T(8,128)(2,1)S(1)} %add_convert_fusion.7), channel_id=1, source_target_pairs={{2,4},{4,2},{6,0},{0,6},{3,5},{5,3},{7,1},{1,7},{10,12},{12,10},{1... | collective-permute-start | bytes 196616 | tf_op jit(solution)/shard_map/ppermute | solution.py:312
  51.4 10.7 %collective-permute-start.11 = (f16[4,4,1,1,1,1,16,128]{7,6,5,4,2,1,0,3:T(8,128)(2,1)S(1)}, f16[4,4,1,1,1,1,16,128]{7,6,5,4,2,1,0,3:T(8,128)(2,1)S(1)}, u32[]{:S(2)}, u32[]{:S(2)}) collective-permute-start(f16[4,4,1,1,1,1,16,128]{7,6,5,4,2,1,0,3:T(8,128)(2,1)S(1)} %add_convert_fusion.9), channel_id=1, source_target_pairs={{0,16},{16,0},{32,48},{48,32},{1,17},{17,1},{33,49},{49,33},{2,18}... | collective-permute-start | bytes 196616 | tf_op jit(solution)/shard_map/ppermute | solution.py:312
  53.8 7.7 %collective-permute-start.17 = (f16[4,4,2,1,2,1,16,128]{7,6,4,3,2,1,0,5:T(8,128)(2,1)S(1)}, f16[4,4,2,1,2,1,16,128]{7,6,4,3,2,1,0,5:T(8,128)(2,1)S(1)}, u32[]{:S(2)}, u32[]{:S(2)}) collective-permute-start(f16[4,4,2,1,2,1,16,128]{7,6,4,3,2,1,0,5:T(8,128)(2,1)S(1)} %get-tuple-element.66), channel_id=1, source_target_pairs={{2,4},{4,2},{6,0},{0,6},{3,5},{5,3},{7,1},{1,7},{10,12},{12,10},{1... | collective-permute-start | bytes 786440 | tf_op jit(solution)/shard_map/ppermute | solution.py:312
  54.8 25.9 %copy-start.5 = (f32[4,64]{1,0:T(4,128)S(1)}, f32[4,64]{1,0:T(4,128)}, u32[]{:S(2)}) copy-start(f32[4,64]{1,0:T(4,128)} %param.9) | copy-start | bytes 3076
  54.8 12.2 %collective-permute-start.7 = (f16[4,4,1,1,1,1,16,128]{7,6,5,4,3,1,0,2:T(8,128)(2,1)S(1)}, f16[4,4,1,1,1,1,16,128]{7,6,5,4,3,1,0,2:T(8,128)(2,1)S(1)}, u32[]{:S(2)}, u32[]{:S(2)}) collective-permute-start(f16[4,4,1,1,1,1,16,128]{7,6,5,4,3,1,0,2:T(8,128)(2,1)S(1)} %add_convert_fusion.11), channel_id=1, source_target_pairs={{16,32},{32,16},{48,0},{0,48},{17,33},{33,17},{49,1},{1,49},{18,34... | collective-permute-start | bytes 196616 | tf_op jit(solution)/shard_map/ppermute | solution.py:312
  61.6 5.1 %collective-permute-start.18 = (f16[4,4,2,1,1,1,16,128]{7,6,4,3,2,1,0,5:T(8,128)(2,1)S(1)}, f16[4,4,2,1,1,1,16,128]{7,6,4,3,2,1,0,5:T(8,128)(2,1)S(1)}, u32[]{:S(2)}, u32[]{:S(2)}) collective-permute-start(f16[4,4,2,1,1,1,16,128]{7,6,4,3,2,1,0,5:T(8,128)(2,1)S(1)} %add_convert_fusion), channel_id=1, source_target_pairs={{0,16},{16,0},{32,48},{48,32},{1,17},{17,1},{33,49},{49,33},{2,18}... | collective-permute-start | bytes 393224 | tf_op jit(solution)/shard_map/ppermute | solution.py:312
  66.7 4.4 %collective-permute-start.19 = (f16[4,4,1,1,1,1,16,128]{7,6,4,3,2,1,0,5:T(8,128)(2,1)S(1)}, f16[4,4,1,1,1,1,16,128]{7,6,4,3,2,1,0,5:T(8,128)(2,1)S(1)}, u32[]{:S(2)}, u32[]{:S(2)}) collective-permute-start(f16[4,4,1,1,1,1,16,128]{7,6,4,3,2,1,0,5:T(8,128)(2,1)S(1)} %add_convert_fusion.5), channel_id=1, source_target_pairs={{0,2},{2,0},{4,6},{6,4},{1,3},{3,1},{5,7},{7,5},{8,10},{10,8},{12,... | collective-permute-start | bytes 196616 | tf_op jit(solution)/shard_map/ppermute | solution.py:312
  72.1 19.1 %all-to-all-start = ((f16[8,2,64,128]{3,2,1,0:T(8,128)(2,1)}), f16[8,2,64,128]{3,2,1,0:T(8,128)(2,1)S(1)}, u32[]{:S(2)}, u32[]{:S(2)}) async-start(f16[8,2,64,128]{3,2,1,0:T(8,128)(2,1)} %bitcast.35), calls=%async_computation | async-start | bytes 524288 | tf_op jit(solution)/shard_map/all_to_all | solution.py:318
  91.3 3.6 %collective-permute-start.21 = (f16[4,4,16,128]{3,2,1,0:T(8,128)(2,1)S(1)}, f16[4,4,16,128]{3,2,1,0:T(8,128)(2,1)S(1)}, u32[]{:S(2)}, u32[]{:S(2)}) collective-permute-start(f16[4,4,16,128]{3,2,1,0:T(8,128)(2,1)S(1)} %get-tuple-element.77), channel_id=1, source_target_pairs={{0,1},{1,0},{2,3},{3,2},{4,5},{5,4},{6,7},{7,6},{8,9},{9,8},{10,11... | collective-permute-start | bytes 196616 | tf_op jit(solution)/shard_map/ppermute | solution.py:329
  91.5 12.5 %collective-permute-start.20 = (f16[4,4,16,128]{3,2,1,0:T(8,128)(2,1)S(1)}, f16[4,4,16,128]{3,2,1,0:T(8,128)(2,1)S(1)}, u32[]{:S(2)}, u32[]{:S(2)}) collective-permute-start(f16[4,4,16,128]{3,2,1,0:T(8,128)(2,1)S(1)} %get-tuple-element.78), channel_id=1, source_target_pairs={{1,2},{3,4},{5,6},{7,8},{9,10},{11,12},{13,14},{15,16},{17,18},{19... | collective-permute-start | bytes 196616 | tf_op jit(solution)/shard_map/ppermute | solution.py:330
  (5 other events, 59.5 us)

commit v3 on v2

--- a/solution.py
+++ b/solution.py
@@ -96,6 +96,10 @@
 
 def in_hbm(x):
     return pltpu.with_memory_space_constraint(x, pltpu.HBM)
+
+
+def in_vmem(x):
+    return pltpu.with_memory_space_constraint(x, pltpu.VMEM)
 
 
 def project_first(order, vol, matrix):
@@ -120,23 +124,29 @@
     )(order, in_hbm(vol), in_hbm(matrix))
 
 
-def project_body(col_ref, matrix_ref, own_hbm, away_hbm, buf, out_sems):
-    wait_all(multiply(col_ref[...], matrix_ref, own_hbm, away_hbm, buf, out_sems))
-
-
-def project(columns, matrix):
+def project_body(col_ref, *refs):
+    matrices, outs, bufs, sems = refs[:3], refs[3:9], refs[9:12], refs[12:]
+    columns = col_ref[...]
+    copies = []
+    for i in range(3):
+        copies += multiply(columns, matrices[i], outs[2 * i], outs[2 * i + 1], bufs[i], sems[i])
+    wait_all(copies)
+
+
+def project(columns, matrices):
     rows, depth = columns.shape
     half = pltpu.HBM((4, 2, rows // 2, PB), jnp.float32)
-    return pl.pallas_call(
+    got = pl.pallas_call(
         project_body,
-        in_specs=[VMEM, VMEM],
-        out_specs=[HBM, HBM],
-        out_shape=[half, half],
-        scratch_shapes=[pltpu.VMEM((4, 2, rows, PB), jnp.float32), pltpu.SemaphoreType.DMA((8,))],
-        cost_estimate=pl.CostEstimate(flops=2 * rows * depth * 8 * PB, transcendentals=0, bytes_accessed=5 << 20),
-        compiler_params=vmem_params(10),
+        in_specs=[VMEM] * 4,
+        out_specs=[HBM] * 6,
+        out_shape=[half] * 6,
+        scratch_shapes=[pltpu.VMEM((4, 2, rows, PB), jnp.float32)] * 3 + [pltpu.SemaphoreType.DMA((8,))] * 3,
+        cost_estimate=pl.CostEstimate(flops=6 * rows * depth * 8 * PB, transcendentals=0, bytes_accessed=15 << 20),
+        compiler_params=vmem_params(14),
         name="project",
-    )(columns, matrix)
+    )(in_vmem(columns), *[in_vmem(m) for m in matrices])
+    return got[0:2], got[2:4], got[4:6]
 
 
 def merge_body(first_ref, other_ref, own_any, got_any, out_ref, own_buf, got_buf, sems, *, portion, side):
@@ -171,63 +181,68 @@
         cost_estimate=pl.CostEstimate(flops=1 << 30, transcendentals=0, bytes_accessed=2 << 20),
         compiler_params=vmem_params(4),
         name="merge_send" if side else "merge_keep",
-    )(first, other, in_hbm(own), got)
-
-
-def detect(table_ref, sums, passed):
-    for e in range(EBINS):
-        row = [table_ref[16 * e + m : 16 * e + m + 1, :] for m in range(MATS)]
-        power = sums[0] * row[0]
+    )(first, other, own, got)
+
+
+def detect(natt_ref, resp_ref, sums):
+    high, low = [], []
+    for v in range(16):
+        power = natt_ref[0] * sums[0][v : v + 1]
         for m in range(1, MATS):
-            power = power + sums[m] * row[m]
-        passed[e] = jnp.exp(power)
-    bins = [None] * CBINS
-    for e in range(EBINS):
-        value = passed[e]
-        for c in range(CBINS):
-            part = table_ref[16 * e + 4 + c : 16 * e + 5 + c, :] * value
-            bins[c] = part if e == 0 else bins[c] + part
-    return bins
+            power = power + natt_ref[m] * sums[m][v : v + 1]
+        passed = jnp.exp(power)
+        top = passed.astype(jnp.bfloat16)
+        high.append(top)
+        low.append((passed - top.astype(jnp.float32)).astype(jnp.bfloat16))
+    terms = jnp.concatenate([jnp.concatenate(high, axis=1), jnp.concatenate(low, axis=1)], axis=0)
+    got = jnp.dot(resp_ref[...], terms, preferred_element_type=jnp.float32)
+    got = got[:CBINS] + got[CBINS:]
+    return jnp.swapaxes(jnp.stack([got[:, v * PB : (v + 1) * PB] for v in range(16)]), 0, 1)
+
+
+def split_response(response):
+    top = lax.reduce_precision(response, 8, 7)
+    rest = response - top
+    rows = jnp.concatenate([jnp.concatenate([top, top], axis=1), jnp.pad(rest, ((0, 0), (0, EBINS)))], axis=0)
+    return rows.astype(jnp.bfloat16)
 
 
 DETECT_COST = pl.CostEstimate(flops=1 << 31, transcendentals=1 << 20, bytes_accessed=1 << 20)
 
 
-def inner_body(cross_ref, place_ref, table_ref, sums_ref, near_ref, partial_ref, passed, passed_near):
+def inner_body(cross_ref, place_ref, natt_ref, resp_ref, sums_ref, near_ref, partial_ref):
     core = place_ref[0]
 
     def block(b, carry):
-        own = detect(table_ref, [sums_ref[m, :, b] for m in range(MATS)], passed)
-        near = detect(table_ref, [near_ref[m, b] for m in range(MATS)], passed_near)
+        own = [detect(natt_ref, resp_ref, [sums_ref[m, r, b] for m in range(MATS)]) for r in (0, 1)]
+        near = detect(natt_ref, resp_ref, [near_ref[m, b] for m in range(MATS)])
         for c in range(CBINS):
             leak = cross_ref[c]
             for row in (0, 1):
                 side = jnp.where(core == 1 - row, near[c], 0.0)
-                partial_ref[c, row, b] = (1.0 - 2.0 * leak) * own[c][row] + leak * (own[c][1 - row] + side)
+                partial_ref[c, row, b] = (1.0 - 2.0 * leak) * own[row][c] + leak * (own[1 - row][c] + side)
         return carry
 
     lax.fori_loop(0, PBLK, block, 0)
 
 
-def inner(crosstalk, place, table, sums, near):
-    rows = jax.ShapeDtypeStruct((CBINS,) + sums.shape[1:], jnp.float32)
+def inner(crosstalk, place, natt, resp, sums, near):
     return pl.pallas_call(
         inner_body,
-        in_specs=[SMEM] * 2 + [VMEM] * 3,
+        in_specs=[SMEM] * 2 + [VMEM] * 4,
         out_specs=VMEM,
-        out_shape=rows,
-        scratch_shapes=[pltpu.VMEM((EBINS, 2, 16, PB), jnp.float32), pltpu.VMEM((EBINS, 16, PB), jnp.float32)],
+        out_shape=jax.ShapeDtypeStruct((CBINS,) + sums.shape[1:], jnp.float32),
         cost_estimate=DETECT_COST,
         compiler_params=vmem_params(8),
         name="inner",
-    )(crosstalk, place, table, sums, near)
-
-
-def finish_body(cross_ref, place_ref, table_ref, far_ref, partial_ref, out_ref, passed):
+    )(crosstalk, place, natt, resp, sums, near)
+
+
+def finish_body(cross_ref, place_ref, natt_ref, resp_ref, far_ref, partial_ref, out_ref):
     core, present = place_ref[0], place_ref[1]
 
     def block(b, carry):
-        far = detect(table_ref, [far_ref[m, b] for m in range(MATS)], passed)
+        far = detect(natt_ref, resp_ref, [far_ref[m, b] for m in range(MATS)])
         columns = pl.ds(pl.multiple_of(b * PB, PB), PB)
         for c in range(CBINS):
             side = cross_ref[c] * jnp.where(present == 1, far[c], 0.0)
@@ -238,17 +253,16 @@
     lax.fori_loop(0, PBLK, block, 0)
 
 
-def finish(crosstalk, place, table, far, partial):
+def finish(crosstalk, place, natt, resp, far, partial):
     return pl.pallas_call(
         finish_body,
-        in_specs=[SMEM] * 2 + [VMEM] * 3,
+        in_specs=[SMEM] * 2 + [VMEM] * 4,
         out_specs=VMEM,
         out_shape=jax.ShapeDtypeStruct((CBINS, 2, 16, PBLK * PB), jnp.float32),
-        scratch_shapes=[pltpu.VMEM((EBINS, 16, PB), jnp.float32)],
         cost_estimate=DETECT_COST,
         compiler_params=vmem_params(8),
         name="finish",
-    )(crosstalk, place, table, far, partial)
+    )(crosstalk, place, natt, resp, far, partial)
 
 
 def per_device(volume, system, geometry, attenuation, response, crosstalk):
@@ -273,13 +287,10 @@
         return merge(mine, partner, *crossing[w], w, DIM_OF[axis, which] - 2, 1).astype(jnp.float16)
 
     cross(0, own, away)
-    cross(1, *project(columns, rest[0]))
-    cross(2, *project(columns, rest[1]))
-    sends = [first_send(0)]
-    sends[0], columns = lax.optimization_barrier((sends[0], columns))
-    last = project(columns, rest[2])
-    cross(3, *last)
-    sends += [first_send(w) for w in range(1, 4)]
+    others = project(columns, rest)
+    for w in range(1, 4):
+        cross(w, *others[w - 1])
+    sends = [first_send(w) for w in range(4)]
     keeps, sends[3] = lax.optimization_barrier((crossing, sends[3]))
     for w in range(4):
         axis, which = ORDERS[w][0]
@@ -330,10 +341,10 @@
     far = lax.ppermute(jnp.where(core == 0, top, bottom), axes, swap + [(j, i) for i, j in swap])
     present = jnp.logical_and(me > 0, me < count - 1).astype(jnp.int32)
     place = jnp.stack([core, present])
-    table = jnp.concatenate([-attenuation.T, response.T, jnp.zeros((EBINS, 4), jnp.float32)], axis=1)
-    table = jnp.broadcast_to(table.reshape(16 * EBINS, 1), (16 * EBINS, PB))
-    partial = inner(crosstalk, place, table, sums, near.astype(jnp.float32))
-    return finish(crosstalk, place, table, far.astype(jnp.float32), partial)
+    natt = jnp.broadcast_to(-attenuation[:, :, None], (MATS, EBINS, PB))
+    resp = split_response(response)
+    partial = inner(crosstalk, place, natt, resp, sums, near.astype(jnp.float32))
+    return finish(crosstalk, place, natt, resp, far.astype(jnp.float32), partial)
 
 
 def solution(mesh):

time: 108 us -> 94.6 us (0.88)
  Pallas kernels: 37 us -> 27.8 us
  waiting for transfers between devices: 29.2 us -> 26.3 us
  starting transfers between devices: 36.9 us -> 35.6 us
    pallas_call x5 -> x3, Pallas kernels: 17.5 us -> 11.2 us  [the longest x1 4.79 us: project(): pl.pallas_call(project_body, in_specs=[VMEM] * 4, out_specs=[HBM] * 6, ou...]
    ppermute x12, waiting for transfers between devices: 13.3 us -> 8.46 us  [per_device(): current[w].append(lax.ppermute(sends[w], axis, PAIRS[which]))]
    ppermute x1, waiting for transfers between devices: 2.04 us -> 5.18 us  [per_device(): lax.ppermute(jnp.where(core == 0, top, bottom), axes, swap + [(j, i) for...]
    pallas_call x8, Pallas kernels: 15.1 us -> 12.2 us  [merge(): pl.pallas_call(functools.partial(merge_body, portion=portion, side=side),...]
    ppermute x12, starting transfers between devices: 17.3 us -> 15.7 us  [per_device(): current[w].append(lax.ppermute(sends[w], axis, PAIRS[which]))]
    ppermute x4, waiting for transfers between devices: 3.72 us -> 2.32 us  [per_device(): got = lax.ppermute(sends[w], axis, PAIRS[which])]
  transfers between devices with their start and end apart: 23 -> 23, of which waited for: 8 -> 9; matrix products, arithmetic and copies ran while one was open for 2% -> 2% of each run, Pallas kernels for 27% -> 22%
where the time goes in v3:
time: 94.6 us; the launch traced here: 94.3 us
  starting transfers between devices  35.6 us (38%)
  Pallas kernels  27.8 us (29%)
  waiting for transfers between devices  26.3 us (28%)
  other arithmetic  3.41 us (4%)
    ppermute x12, starting transfers between devices, per_device(): current[w].append(lax.ppermute(sends[w], axis, PAIRS[which]))  15.7 us
    pallas_call x8, Pallas kernels, merge(): pl.pallas_call(functools.partial(merge_body, portion=portion, side=side),...  12.2 us
    all_to_all x1, waiting for transfers between devices, per_device(): received = lax.all_to_all(outgoing, ('zh', 'mat'), 0, 0, tiled=True)  10.4 us
    all_to_all x1, starting transfers between devices, per_device(): received = lax.all_to_all(outgoing, ('zh', 'mat'), 0, 0, tiled=True)  8.47 us
    ppermute x12, waiting for transfers between devices, per_device(): current[w].append(lax.ppermute(sends[w], axis, PAIRS[which]))  8.46 us
    ppermute x4, starting transfers between devices, per_device(): got = lax.ppermute(sends[w], axis, PAIRS[which])  6.7 us
    ppermute x1, waiting for transfers between devices, per_device(): lax.ppermute(jnp.where(core == 0, top, bottom), axes, swap + [(j, i) for...  5.18 us
    pallas_call x1, Pallas kernels, project(): pl.pallas_call(project_body, in_specs=[VMEM] * 4, out_specs=[HBM] * 6, ou...  4.79 us
  transfers between devices with their start and end apart: 23, of which 9 were waited for; matrix products, arithmetic and copies ran while one was open for 2% of the time, Pallas kernels for 22%

profile of v3, /device:TPU:8, one launch (start us, length us, event | category | flops | bytes accessed | tf_op | source)
XLA Modules:
  0.0 94.3 jit_solution(17993500638545309412)
XLA Ops:
  0.5 4.4 %project_first.1 = (f32[4,2,256,128]{3,2,1,0:T(8,128)}, f32[4,2,256,128]{3,2,1,0:T(8,128)}, bf16[512,1024]{1,0:T(8,128)(2,1)S(1)}, bf16[1024,8,128]{2,1,0:T(8,12...) custom-call(s32[512,1]{1,0:T(8,128)S(1)} %fusion.10.order_ref, ...), custom_call_target="tpu_custom_call" | custom-call | flops 1610612736 | bytes 12582912 | tf_op jit(solution)/shard_map/project_first/pallas_call | solution.py:109
  5.0 4.8 %project.1 = (f32[4,2,256,128]{3,2,1,0:T(8,128)}, f32[4,2,256,128]{3,2,1,0:T(8,128)}, f32[4,2,256,128]{3,2,1,0:T(8,128)}, f32[4,2,256,128]{3,2,1,0:T(8,128)}, f3...) custom-call(bf16[512,1024]{1,0:T(8,128)(2,1)S(1)} %get-tuple-element.36.col_ref, ...), custom_call_target="tpu_custom_call" | custom-call | flops 3221225472 | bytes 15728640 | tf_op jit(solution)/shard_map/project/pallas_call | solution.py:139
  12.7 1.6 %collective-permute-start.4 = (f16[4,4,1,128,128]{4,3,2,1,0:T(8,128)(2,1)S(1)}, f16[4,4,1,128,128]{4,3,2,1,0:T(8,128)(2,1)S(1)}, u32[]{:S(2)}, u32[]{:S(2)}) collective-permute-start(f16[4,4,1,128,128]{4,3,2,1,0:T(8,128)(2,1)S(1)} %convert_element_type.174), channel_id=1, source_target_pairs={{0,2},{2,0},{4,6},{6,4},{1,3},{3,1},{5,7},{7,5},{8,10},{10,8},{12,... | collective-permute-start | bytes 1572872 | tf_op jit(solution)/shard_map/ppermute | solution.py:300
  15.3 1.8 %merge_send.6 = f32[4,4,2,64,128]{4,3,2,1,0:T(8,128)S(1)} custom-call(s32[16]{0:T(128)S(1)} %get-tuple-element.64.first_ref, s32[16]{0:T(128)S(1)} %get-tuple-element.63.other_ref, f32[4,2,2,2,64,128]{5,4,3,2,1,0:T(8,128)S(1)} %bitcast.56, f32[4,2,2,2,64,128]{5,4,3,2,1,0:T(8,128)} %bitcast.17.got_any), custom_call_target="tpu_custom_call" | custom-call | flops 1073741824 | bytes 2097152 | tf_op jit(solution)/shard_map/merge_send/pallas_call | solution.py:175
  17.4 2.2 %collective-permute-start.8 = (f16[4,4,2,64,128]{4,3,2,1,0:T(8,128)(2,1)S(1)}, f16[4,4,2,64,128]{4,3,2,1,0:T(8,128)(2,1)S(1)}, u32[]{:S(2)}, u32[]{:S(2)}) collective-permute-start(f16[4,4,2,64,128]{4,3,2,1,0:T(8,128)(2,1)S(1)} %convert_element_type.187), channel_id=1, source_target_pairs={{2,4},{4,2},{6,0},{0,6},{3,5},{5,3},{7,1},{1,7},{10,12},{12,10},{1... | collective-permute-start | bytes 1572872 | tf_op jit(solution)/shard_map/ppermute | solution.py:300
  19.6 1.8 %merge_send.7 = f32[4,4,4,32,128]{4,3,2,1,0:T(8,128)S(1)} custom-call(s32[16]{0:T(128)S(1)} %get-tuple-element.64.first_ref, s32[16]{0:T(128)S(1)} %get-tuple-element.63.other_ref, f32[4,2,4,2,32,128]{5,4,3,2,1,0:T(8,128)S(1)} %bitcast.54, f32[4,2,4,2,32,128]{5,4,3,2,1,0:T(8,128)} %bitcast.24.got_any), custom_call_target="tpu_custom_call" | custom-call | flops 1073741824 | bytes 2097152 | tf_op jit(solution)/shard_map/merge_send/pallas_call | solution.py:175
  22.0 2.4 %collective-permute-start.16 = (f16[4,4,8,16,128]{4,3,2,1,0:T(8,128)(2,1)S(1)}, f16[4,4,8,16,128]{4,3,2,1,0:T(8,128)(2,1)S(1)}, u32[]{:S(2)}, u32[]{:S(2)}) collective-permute-start(f16[4,4,8,16,128]{4,3,2,1,0:T(8,128)(2,1)S(1)} %convert_element_type.173), channel_id=1, source_target_pairs={{16,32},{32,16},{48,0},{0,48},{17,33},{33,17},{49,1},{1,49},{18,34... | collective-permute-start | bytes 1572872 | tf_op jit(solution)/shard_map/ppermute | solution.py:300
  25.9 1.8 %merge_keep.5 = f32[4,4,2,64,128]{4,3,2,1,0:T(8,128)S(1)} custom-call(s32[16]{0:T(128)S(1)} %get-tuple-element.64.first_ref, s32[16]{0:T(128)S(1)} %get-tuple-element.63.other_ref, f32[4,2,2,2,64,128]{5,4,3,2,1,0:T(8,128)S(1)} %bitcast.57, f32[4,2,2,2,64,128]{5,4,3,2,1,0:T(8,128)} %bitcast.14.got_any), custom_call_target="tpu_custom_call" | custom-call | flops 1073741824 | bytes 2097152 | tf_op jit(solution)/shard_map/merge_keep/pallas_call | solution.py:175
  27.8 1.8 %merge_keep.6 = f32[4,4,4,32,128]{4,3,2,1,0:T(8,128)S(1)} custom-call(s32[16]{0:T(128)S(1)} %get-tuple-element.64.first_ref, s32[16]{0:T(128)S(1)} %get-tuple-element.63.other_ref, f32[4,2,4,2,32,128]{5,4,3,2,1,0:T(8,128)S(1)} %bitcast.55, f32[4,2,4,2,32,128]{5,4,3,2,1,0:T(8,128)} %bitcast.21.got_any), custom_call_target="tpu_custom_call" | custom-call | flops 1073741824 | bytes 2097152 | tf_op jit(solution)/shard_map/merge_keep/pallas_call | solution.py:175
  32.5 1.7 %collective-permute-start.9 = (f16[4,4,2,1,2,1,16,128]{7,6,5,4,2,1,0,3:T(8,128)(2,1)S(1)}, f16[4,4,2,1,2,1,16,128]{7,6,5,4,2,1,0,3:T(8,128)(2,1)S(1)}, u32[]{:S(2)}, u32[]{:S(2)}) collective-permute-start(f16[4,4,2,1,2,1,16,128]{7,6,5,4,2,1,0,3:T(8,128)(2,1)S(1)} %get-tuple-element.53), channel_id=1, source_target_pairs={{16,32},{32,16},{48,0},{0,48},{17,33},{33,17},{49,1},{1,49},{18,34... | collective-permute-start | bytes 786440 | tf_op jit(solution)/shard_map/ppermute | solution.py:323
  34.2 2.2 %collective-permute-done.12 = f16[4,4,4,32,128]{4,3,2,1,0:T(8,128)(2,1)S(1)} collective-permute-done((f16[4,4,4,32,128]{4,3,2,1,0:T(8,128)(2,1)S(1)}, f16[4,4,4,32,128]{4,3,2,1,0:T(8,128)(2,1)S(1)}, u32[]{:S(2)}, u32[]{:S(2)}) %collective-permute-start.12) | collective-permute-done | bytes 524320 | tf_op jit(solution)/shard_map/ppermute | solution.py:300
  37.4 1.6 %collective-permute-start.17 = (f16[4,4,2,1,2,1,16,128]{7,6,4,3,2,1,0,5:T(8,128)(2,1)S(1)}, f16[4,4,2,1,2,1,16,128]{7,6,4,3,2,1,0,5:T(8,128)(2,1)S(1)}, u32[]{:S(2)}, u32[]{:S(2)}) collective-permute-start(f16[4,4,2,1,2,1,16,128]{7,6,4,3,2,1,0,5:T(8,128)(2,1)S(1)} %get-tuple-element.62), channel_id=1, source_target_pairs={{2,4},{4,2},{6,0},{0,6},{3,5},{5,3},{7,1},{1,7},{10,12},{12,10},{1... | collective-permute-start | bytes 786440 | tf_op jit(solution)/shard_map/ppermute | solution.py:323
  39.0 1.9 %collective-permute-done.5 = f16[4,4,1,2,1,2,16,128]{7,6,5,4,3,1,0,2:T(8,128)(2,1)S(1)} collective-permute-done((f16[4,4,1,2,1,2,16,128]{7,6,5,4,3,1,0,2:T(8,128)(2,1)S(1)}, f16[4,4,1,2,1,2,16,128]{7,6,5,4,3,1,0,2:T(8,128)(2,1)S(1)}, u32[]{:S(2)}, u32[]{:S(2)}) %collective-permute-start.5) | collective-permute-done | bytes 262176 | tf_op jit(solution)/shard_map/ppermute | solution.py:323
  43.1 1.7 %collective-permute-start.14 = (f16[4,4,1,2,1,1,16,128]{7,6,5,3,2,1,0,4:T(8,128)(2,1)S(1)}, f16[4,4,1,2,1,1,16,128]{7,6,5,3,2,1,0,4:T(8,128)(2,1)S(1)}, u32[]{:S(2)}, u32[]{:S(2)}) collective-permute-start(f16[4,4,1,2,1,1,16,128]{7,6,5,3,2,1,0,4:T(8,128)(2,1)S(1)} %add_convert_fusion.1), channel_id=1, source_target_pairs={{16,32},{32,16},{48,0},{0,48},{17,33},{33,17},{49,1},{1,49},{18,34... | collective-permute-start | bytes 393224 | tf_op jit(solution)/shard_map/ppermute | solution.py:323
  46.3 2.1 %collective-permute-start.18 = (f16[4,4,2,1,1,1,16,128]{7,6,4,3,2,1,0,5:T(8,128)(2,1)S(1)}, f16[4,4,2,1,1,1,16,128]{7,6,4,3,2,1,0,5:T(8,128)(2,1)S(1)}, u32[]{:S(2)}, u32[]{:S(2)}) collective-permute-start(f16[4,4,2,1,1,1,16,128]{7,6,4,3,2,1,0,5:T(8,128)(2,1)S(1)} %add_convert_fusion), channel_id=1, source_target_pairs={{0,16},{16,0},{32,48},{48,32},{1,17},{17,1},{33,49},{49,33},{2,18}... | collective-permute-start | bytes 393224 | tf_op jit(solution)/shard_map/ppermute | solution.py:323
  48.4 2.3 %collective-permute-start.7 = (f16[4,4,1,1,1,1,16,128]{7,6,5,4,3,1,0,2:T(8,128)(2,1)S(1)}, f16[4,4,1,1,1,1,16,128]{7,6,5,4,3,1,0,2:T(8,128)(2,1)S(1)}, u32[]{:S(2)}, u32[]{:S(2)}) collective-permute-start(f16[4,4,1,1,1,1,16,128]{7,6,5,4,3,1,0,2:T(8,128)(2,1)S(1)} %add_convert_fusion.11), channel_id=1, source_target_pairs={{16,32},{32,16},{48,0},{0,48},{17,33},{33,17},{49,1},{1,49},{18,34... | collective-permute-start | bytes 196616 | tf_op jit(solution)/shard_map/ppermute | solution.py:323
  50.8 1.9 %collective-permute-start.11 = (f16[4,4,1,1,1,1,16,128]{7,6,5,4,2,1,0,3:T(8,128)(2,1)S(1)}, f16[4,4,1,1,1,1,16,128]{7,6,5,4,2,1,0,3:T(8,128)(2,1)S(1)}, u32[]{:S(2)}, u32[]{:S(2)}) collective-permute-start(f16[4,4,1,1,1,1,16,128]{7,6,5,4,2,1,0,3:T(8,128)(2,1)S(1)} %add_convert_fusion.9), channel_id=1, source_target_pairs={{0,16},{16,0},{32,48},{48,32},{1,17},{17,1},{33,49},{49,33},{2,18}... | collective-permute-start | bytes 196616 | tf_op jit(solution)/shard_map/ppermute | solution.py:323
  55.2 3.2 %collective-permute-done.15 = f16[4,4,1,1,1,1,16,128]{7,6,5,3,2,1,0,4:T(8,128)(2,1)S(1)} collective-permute-done((f16[4,4,1,1,1,1,16,128]{7,6,5,3,2,1,0,4:T(8,128)(2,1)S(1)}, f16[4,4,1,1,1,1,16,128]{7,6,5,3,2,1,0,4:T(8,128)(2,1)S(1)}, u32[]{:S(2)}, u32[]{:S(2)}) %collective-permute-start.15) | collective-permute-done | bytes 65568 | tf_op jit(solution)/shard_map/ppermute | solution.py:323
  59.7 8.5 %all-to-all-start = ((f16[8,2,64,128]{3,2,1,0:T(8,128)(2,1)}), f16[8,2,64,128]{3,2,1,0:T(8,128)(2,1)S(1)}, u32[]{:S(2)}, u32[]{:S(2)}) async-start(f16[8,2,64,128]{3,2,1,0:T(8,128)(2,1)} %bitcast.33), calls=%async_computation | async-start | bytes 524288 | tf_op jit(solution)/shard_map/all_to_all | solution.py:329
  68.3 10.4 %all-to-all-done = f16[8,2,64,128]{3,2,1,0:T(8,128)(2,1)S(1)} async-done(((f16[8,2,64,128]{3,2,1,0:T(8,128)(2,1)}), f16[8,2,64,128]{3,2,1,0:T(8,128)(2,1)S(1)}, u32[]{:S(2)}, u32[]{:S(2)}) %all-to-all-start) | async-done | bytes 262176 | tf_op jit(solution)/shard_map/all_to_all | solution.py:329
  79.0 3.5 %collective-permute-start.20 = (f16[4,4,16,128]{3,2,1,0:T(8,128)(2,1)S(1)}, f16[4,4,16,128]{3,2,1,0:T(8,128)(2,1)S(1)}, u32[]{:S(2)}, u32[]{:S(2)}) collective-permute-start(f16[4,4,16,128]{3,2,1,0:T(8,128)(2,1)S(1)} %get-tuple-element.74), channel_id=1, source_target_pairs={{1,2},{3,4},{5,6},{7,8},{9,10},{11,12},{13,14},{15,16},{17,18},{19... | collective-permute-start | bytes 196616 | tf_op jit(solution)/shard_map/ppermute | solution.py:341
  82.6 3.7 %inner.1.partial_ref = f32[8,2,4,16,128]{4,3,2,1,0:T(8,128)S(1)} custom-call(f32[8]{0:T(128)S(1)} %copy-done.1, s32[2]{0:T(128)S(1)} %pad_add_fusion.place_ref, f32[4,64,128]{2,1,0:T(8,128)S(1)} %broadcast_in_dim.2.natt_ref, bf16[16,128]{1,0:T(8,128)(2,1)S(1)} %fusion.48.resp_ref, f32[4,2,4,16,128]{4,3,2,1,0:T(8,128)S(1)} %bitcast.41, ...), custom_call_target="tpu_custom_call" | custom-call | flops 2147483648 | bytes 1048576 | tf_op jit(solution)/shard_map/inner/pallas_call | solution.py:230
  86.3 5.2 %collective-permute-done.20 = f16[4,4,16,128]{3,2,1,0:T(8,128)(2,1)S(1)} collective-permute-done((f16[4,4,16,128]{3,2,1,0:T(8,128)(2,1)S(1)}, f16[4,4,16,128]{3,2,1,0:T(8,128)(2,1)S(1)}, u32[]{:S(2)}, u32[]{:S(2)}) %collective-permute-start.20) | collective-permute-done | bytes 65568 | tf_op jit(solution)/shard_map/ppermute | solution.py:341
  91.5 2.8 %finish.1 = f32[8,2,16,512]{3,2,1,0:T(8,128)} custom-call(f32[8]{0:T(128)S(1)} %copy-done.1, s32[2]{0:T(128)S(1)} %pad_add_fusion.place_ref, f32[4,64,128]{2,1,0:T(8,128)S(1)} %broadcast_in_dim.2.natt_ref, bf16[16,128]{1,0:T(8,128)(2,1)S(1)} %fusion.48.resp_ref, f32[4,4,16,128]{3,2,1,0:T(8,128)S(1)} %convert_element_type.227.far_ref, ...), custom_call_target="tpu_custom_call" | custom-call | flops 2147483648 | bytes 1048576 | tf_op jit(solution)/shard_map/finish/pallas_call | solution.py:257
  (89 shorter events, 18.7 us)
Async XLA Ops:
  4.9 6.2 %collective-permute-start = (f32[4,2,256,128]{3,2,1,0:T(8,128)}, f32[4,2,256,128]{3,2,1,0:T(8,128)S(1)}, u32[]{:S(2)}, u32[]{:S(2)}) collective-permute-start(f32[4,2,256,128]{3,2,1,0:T(8,128)} %get-tuple-element.35), channel_id=1, source_target_pairs={{0,1},{1,0},{2,3},{3,2},{4,5},{5,4},{6,7},{7,6},{8,9},{9,8},{10,11... | collective-permute-start | bytes 3145736 | tf_op jit(solution)/shard_map/ppermute | solution.py:283
  9.8 4.5 %collective-permute-start.3 = (f32[4,2,256,128]{3,2,1,0:T(8,128)}, f32[4,2,256,128]{3,2,1,0:T(8,128)S(1)}, u32[]{:S(2)}, u32[]{:S(2)}) collective-permute-start(f32[4,2,256,128]{3,2,1,0:T(8,128)} %get-tuple-element.45), channel_id=1, source_target_pairs={{0,1},{1,0},{2,3},{3,2},{4,5},{5,4},{6,7},{7,6},{8,9},{9,8},{10,11... | collective-permute-start | bytes 3145736 | tf_op jit(solution)/shard_map/ppermute | solution.py:283
  10.4 4.9 %collective-permute-start.1 = (f32[4,2,256,128]{3,2,1,0:T(8,128)}, f32[4,2,256,128]{3,2,1,0:T(8,128)}, u32[]{:S(2)}, u32[]{:S(2)}) collective-permute-start(f32[4,2,256,128]{3,2,1,0:T(8,128)} %get-tuple-element.41), channel_id=1, source_target_pairs={{0,1},{1,0},{2,3},{3,2},{4,5},{5,4},{6,7},{7,6},{8,9},{9,8},{10,11... | collective-permute-start | bytes 3145736 | tf_op jit(solution)/shard_map/ppermute | solution.py:283
  10.5 6.8 %collective-permute-start.2 = (f32[4,2,256,128]{3,2,1,0:T(8,128)}, f32[4,2,256,128]{3,2,1,0:T(8,128)}, u32[]{:S(2)}, u32[]{:S(2)}) collective-permute-start(f32[4,2,256,128]{3,2,1,0:T(8,128)} %get-tuple-element.43), channel_id=1, source_target_pairs={{0,1},{1,0},{2,3},{3,2},{4,5},{5,4},{6,7},{7,6},{8,9},{9,8},{10,11... | collective-permute-start | bytes 3145736 | tf_op jit(solution)/shard_map/ppermute | solution.py:283
  12.7 17.9 %collective-permute-start.4 = (f16[4,4,1,128,128]{4,3,2,1,0:T(8,128)(2,1)S(1)}, f16[4,4,1,128,128]{4,3,2,1,0:T(8,128)(2,1)S(1)}, u32[]{:S(2)}, u32[]{:S(2)}) collective-permute-start(f16[4,4,1,128,128]{4,3,2,1,0:T(8,128)(2,1)S(1)} %convert_element_type.174), channel_id=1, source_target_pairs={{0,2},{2,0},{4,6},{6,4},{1,3},{3,1},{5,7},{7,5},{8,10},{10,8},{12,... | collective-permute-start | bytes 1572872 | tf_op jit(solution)/shard_map/ppermute | solution.py:300
  17.4 14.9 %collective-permute-start.8 = (f16[4,4,2,64,128]{4,3,2,1,0:T(8,128)(2,1)S(1)}, f16[4,4,2,64,128]{4,3,2,1,0:T(8,128)(2,1)S(1)}, u32[]{:S(2)}, u32[]{:S(2)}) collective-permute-start(f16[4,4,2,64,128]{4,3,2,1,0:T(8,128)(2,1)S(1)} %convert_element_type.187), channel_id=1, source_target_pairs={{2,4},{4,2},{6,0},{0,6},{3,5},{5,3},{7,1},{1,7},{10,12},{12,10},{1... | collective-permute-start | bytes 1572872 | tf_op jit(solution)/shard_map/ppermute | solution.py:300
  21.5 14.9 %collective-permute-start.12 = (f16[4,4,4,32,128]{4,3,2,1,0:T(8,128)(2,1)S(1)}, f16[4,4,4,32,128]{4,3,2,1,0:T(8,128)(2,1)S(1)}, u32[]{:S(2)}, u32[]{:S(2)}) collective-permute-start(f16[4,4,4,32,128]{4,3,2,1,0:T(8,128)(2,1)S(1)} %convert_element_type.200), channel_id=1, source_target_pairs={{0,16},{16,0},{32,48},{48,32},{1,17},{17,1},{33,49},{49,33},{2,18}... | collective-permute-start | bytes 1572872 | tf_op jit(solution)/shard_map/ppermute | solution.py:300
  22.0 15.2 %collective-permute-start.16 = (f16[4,4,8,16,128]{4,3,2,1,0:T(8,128)(2,1)S(1)}, f16[4,4,8,16,128]{4,3,2,1,0:T(8,128)(2,1)S(1)}, u32[]{:S(2)}, u32[]{:S(2)}) collective-permute-start(f16[4,4,8,16,128]{4,3,2,1,0:T(8,128)(2,1)S(1)} %convert_element_type.173), channel_id=1, source_target_pairs={{16,32},{32,16},{48,0},{0,48},{17,33},{33,17},{49,1},{1,49},{18,34... | collective-permute-start | bytes 1572872 | tf_op jit(solution)/shard_map/ppermute | solution.py:300
  30.8 10.2 %collective-permute-start.5 = (f16[4,4,1,2,1,2,16,128]{7,6,5,4,3,1,0,2:T(8,128)(2,1)S(1)}, f16[4,4,1,2,1,2,16,128]{7,6,5,4,3,1,0,2:T(8,128)(2,1)S(1)}, u32[]{:S(2)}, u32[]{:S(2)}) collective-permute-start(f16[4,4,1,2,1,2,16,128]{7,6,5,4,3,1,0,2:T(8,128)(2,1)S(1)} %get-tuple-element.49), channel_id=1, source_target_pairs={{0,16},{16,0},{32,48},{48,32},{1,17},{17,1},{33,49},{49,33},{2,18}... | collective-permute-start | bytes 786440 | tf_op jit(solution)/shard_map/ppermute | solution.py:323
  32.5 9.8 %collective-permute-start.9 = (f16[4,4,2,1,2,1,16,128]{7,6,5,4,2,1,0,3:T(8,128)(2,1)S(1)}, f16[4,4,2,1,2,1,16,128]{7,6,5,4,2,1,0,3:T(8,128)(2,1)S(1)}, u32[]{:S(2)}, u32[]{:S(2)}) collective-permute-start(f16[4,4,2,1,2,1,16,128]{7,6,5,4,2,1,0,3:T(8,128)(2,1)S(1)} %get-tuple-element.53), channel_id=1, source_target_pairs={{16,32},{32,16},{48,0},{0,48},{17,33},{33,17},{49,1},{1,49},{18,34... | collective-permute-start | bytes 786440 | tf_op jit(solution)/shard_map/ppermute | solution.py:323
  36.6 6.5 %collective-permute-start.13 = (f16[4,4,1,2,1,2,16,128]{7,6,5,3,2,1,0,4:T(8,128)(2,1)S(1)}, f16[4,4,1,2,1,2,16,128]{7,6,5,3,2,1,0,4:T(8,128)(2,1)S(1)}, u32[]{:S(2)}, u32[]{:S(2)}) collective-permute-start(f16[4,4,1,2,1,2,16,128]{7,6,5,3,2,1,0,4:T(8,128)(2,1)S(1)} %get-tuple-element.57), channel_id=1, source_target_pairs={{0,2},{2,0},{4,6},{6,4},{1,3},{3,1},{5,7},{7,5},{8,10},{10,8},{12,... | collective-permute-start | bytes 786440 | tf_op jit(solution)/shard_map/ppermute | solution.py:323
  37.4 8.8 %collective-permute-start.17 = (f16[4,4,2,1,2,1,16,128]{7,6,4,3,2,1,0,5:T(8,128)(2,1)S(1)}, f16[4,4,2,1,2,1,16,128]{7,6,4,3,2,1,0,5:T(8,128)(2,1)S(1)}, u32[]{:S(2)}, u32[]{:S(2)}) collective-permute-start(f16[4,4,2,1,2,1,16,128]{7,6,4,3,2,1,0,5:T(8,128)(2,1)S(1)} %get-tuple-element.62), channel_id=1, source_target_pairs={{2,4},{4,2},{6,0},{0,6},{3,5},{5,3},{7,1},{1,7},{10,12},{12,10},{1... | collective-permute-start | bytes 786440 | tf_op jit(solution)/shard_map/ppermute | solution.py:323
  41.0 7.3 %collective-permute-start.6 = (f16[4,4,1,1,1,2,16,128]{7,6,5,4,3,1,0,2:T(8,128)(2,1)S(1)}, f16[4,4,1,1,1,2,16,128]{7,6,5,4,3,1,0,2:T(8,128)(2,1)S(1)}, u32[]{:S(2)}, u32[]{:S(2)}) collective-permute-start(f16[4,4,1,1,1,2,16,128]{7,6,5,4,3,1,0,2:T(8,128)(2,1)S(1)} %add_convert_fusion.3), channel_id=1, source_target_pairs={{2,4},{4,2},{6,0},{0,6},{3,5},{5,3},{7,1},{1,7},{10,12},{12,10},{1... | collective-permute-start | bytes 393224 | tf_op jit(solution)/shard_map/ppermute | solution.py:323
  42.3 8.4 %collective-permute-start.10 = (f16[4,4,1,1,2,1,16,128]{7,6,5,4,2,1,0,3:T(8,128)(2,1)S(1)}, f16[4,4,1,1,2,1,16,128]{7,6,5,4,2,1,0,3:T(8,128)(2,1)S(1)}, u32[]{:S(2)}, u32[]{:S(2)}) collective-permute-start(f16[4,4,1,1,2,1,16,128]{7,6,5,4,2,1,0,3:T(8,128)(2,1)S(1)} %add_convert_fusion.2), channel_id=1, source_target_pairs={{0,2},{2,0},{4,6},{6,4},{1,3},{3,1},{5,7},{7,5},{8,10},{10,8},{12,... | collective-permute-start | bytes 393224 | tf_op jit(solution)/shard_map/ppermute | solution.py:323
  43.1 9.7 %collective-permute-start.14 = (f16[4,4,1,2,1,1,16,128]{7,6,5,3,2,1,0,4:T(8,128)(2,1)S(1)}, f16[4,4,1,2,1,1,16,128]{7,6,5,3,2,1,0,4:T(8,128)(2,1)S(1)}, u32[]{:S(2)}, u32[]{:S(2)}) collective-permute-start(f16[4,4,1,2,1,1,16,128]{7,6,5,3,2,1,0,4:T(8,128)(2,1)S(1)} %add_convert_fusion.1), channel_id=1, source_target_pairs={{16,32},{32,16},{48,0},{0,48},{17,33},{33,17},{49,1},{1,49},{18,34... | collective-permute-start | bytes 393224 | tf_op jit(solution)/shard_map/ppermute | solution.py:323
  46.3 7.1 %collective-permute-start.18 = (f16[4,4,2,1,1,1,16,128]{7,6,4,3,2,1,0,5:T(8,128)(2,1)S(1)}, f16[4,4,2,1,1,1,16,128]{7,6,4,3,2,1,0,5:T(8,128)(2,1)S(1)}, u32[]{:S(2)}, u32[]{:S(2)}) collective-permute-start(f16[4,4,2,1,1,1,16,128]{7,6,4,3,2,1,0,5:T(8,128)(2,1)S(1)} %add_convert_fusion), channel_id=1, source_target_pairs={{0,16},{16,0},{32,48},{48,32},{1,17},{17,1},{33,49},{49,33},{2,18}... | collective-permute-start | bytes 393224 | tf_op jit(solution)/shard_map/ppermute | solution.py:323
  48.4 5.2 %collective-permute-start.7 = (f16[4,4,1,1,1,1,16,128]{7,6,5,4,3,1,0,2:T(8,128)(2,1)S(1)}, f16[4,4,1,1,1,1,16,128]{7,6,5,4,3,1,0,2:T(8,128)(2,1)S(1)}, u32[]{:S(2)}, u32[]{:S(2)}) collective-permute-start(f16[4,4,1,1,1,1,16,128]{7,6,5,4,3,1,0,2:T(8,128)(2,1)S(1)} %add_convert_fusion.11), channel_id=1, source_target_pairs={{16,32},{32,16},{48,0},{0,48},{17,33},{33,17},{49,1},{1,49},{18,34... | collective-permute-start | bytes 196616 | tf_op jit(solution)/shard_map/ppermute | solution.py:323
  50.8 4.4 %collective-permute-start.11 = (f16[4,4,1,1,1,1,16,128]{7,6,5,4,2,1,0,3:T(8,128)(2,1)S(1)}, f16[4,4,1,1,1,1,16,128]{7,6,5,4,2,1,0,3:T(8,128)(2,1)S(1)}, u32[]{:S(2)}, u32[]{:S(2)}) collective-permute-start(f16[4,4,1,1,1,1,16,128]{7,6,5,4,2,1,0,3:T(8,128)(2,1)S(1)} %add_convert_fusion.9), channel_id=1, source_target_pairs={{0,16},{16,0},{32,48},{48,32},{1,17},{17,1},{33,49},{49,33},{2,18}... | collective-permute-start | bytes 196616 | tf_op jit(solution)/shard_map/ppermute | solution.py:323
  52.8 5.6 %collective-permute-start.15 = (f16[4,4,1,1,1,1,16,128]{7,6,5,3,2,1,0,4:T(8,128)(2,1)S(1)}, f16[4,4,1,1,1,1,16,128]{7,6,5,3,2,1,0,4:T(8,128)(2,1)S(1)}, u32[]{:S(2)}, u32[]{:S(2)}) collective-permute-start(f16[4,4,1,1,1,1,16,128]{7,6,5,3,2,1,0,4:T(8,128)(2,1)S(1)} %add_convert_fusion.7), channel_id=1, source_target_pairs={{2,4},{4,2},{6,0},{0,6},{3,5},{5,3},{7,1},{1,7},{10,12},{12,10},{1... | collective-permute-start | bytes 196616 | tf_op jit(solution)/shard_map/ppermute | solution.py:323
  53.5 5.1 %collective-permute-start.19 = (f16[4,4,1,1,1,1,16,128]{7,6,4,3,2,1,0,5:T(8,128)(2,1)S(1)}, f16[4,4,1,1,1,1,16,128]{7,6,4,3,2,1,0,5:T(8,128)(2,1)S(1)}, u32[]{:S(2)}, u32[]{:S(2)}) collective-permute-start(f16[4,4,1,1,1,1,16,128]{7,6,4,3,2,1,0,5:T(8,128)(2,1)S(1)} %add_convert_fusion.5), channel_id=1, source_target_pairs={{0,2},{2,0},{4,6},{6,4},{1,3},{3,1},{5,7},{7,5},{8,10},{10,8},{12,... | collective-permute-start | bytes 196616 | tf_op jit(solution)/shard_map/ppermute | solution.py:323
  58.7 23.9 %copy-start.1 = (f32[8]{0:T(128)S(1)}, f32[8]{0:T(128)}, u32[]{:S(2)}) copy-start(f32[8]{0:T(128)} %cross_ref.3) | copy-start | bytes 100
  59.7 19.0 %all-to-all-start = ((f16[8,2,64,128]{3,2,1,0:T(8,128)(2,1)}), f16[8,2,64,128]{3,2,1,0:T(8,128)(2,1)S(1)}, u32[]{:S(2)}, u32[]{:S(2)}) async-start(f16[8,2,64,128]{3,2,1,0:T(8,128)(2,1)} %bitcast.33), calls=%async_computation | async-start | bytes 524288 | tf_op jit(solution)/shard_map/all_to_all | solution.py:329
  78.8 3.7 %collective-permute-start.21 = (f16[4,4,16,128]{3,2,1,0:T(8,128)(2,1)S(1)}, f16[4,4,16,128]{3,2,1,0:T(8,128)(2,1)S(1)}, u32[]{:S(2)}, u32[]{:S(2)}) collective-permute-start(f16[4,4,16,128]{3,2,1,0:T(8,128)(2,1)S(1)} %get-tuple-element.73), channel_id=1, source_target_pairs={{0,1},{1,0},{2,3},{3,2},{4,5},{5,4},{6,7},{7,6},{8,9},{9,8},{10,11... | collective-permute-start | bytes 196616 | tf_op jit(solution)/shard_map/ppermute | solution.py:340
  79.0 12.5 %collective-permute-start.20 = (f16[4,4,16,128]{3,2,1,0:T(8,128)(2,1)S(1)}, f16[4,4,16,128]{3,2,1,0:T(8,128)(2,1)S(1)}, u32[]{:S(2)}, u32[]{:S(2)}) collective-permute-start(f16[4,4,16,128]{3,2,1,0:T(8,128)(2,1)S(1)} %get-tuple-element.74), channel_id=1, source_target_pairs={{1,2},{3,4},{5,6},{7,8},{9,10},{11,12},{13,14},{15,16},{17,18},{19... | collective-permute-start | bytes 196616 | tf_op jit(solution)/shard_map/ppermute | solution.py:341
  (7 other events, 59.7 us)

commit v4 on v3

--- a/solution.py
+++ b/solution.py
@@ -16,12 +16,17 @@
 TILE_AXES = ("y", "zh", "x", "core")
 PAIRS = ([(0, 1), (1, 0), (2, 3), (3, 2)], [(1, 2), (2, 1), (3, 0), (0, 3)])
 ORDERS = (
-    (("x", 0), ("y", 0), ("x", 1), ("y", 1)),
-    (("x", 1), ("y", 1), ("x", 0), ("y", 0)),
-    (("y", 0), ("x", 0), ("y", 1), ("x", 1)),
-    (("y", 1), ("x", 1), ("y", 0), ("x", 0)),
+    (("x", 0), ("x", 1), ("y", 0), ("y", 1)),
+    (("x", 1), ("x", 0), ("y", 1), ("y", 0)),
+    (("y", 0), ("y", 1), ("x", 0), ("x", 1)),
+    (("y", 1), ("y", 0), ("x", 1), ("x", 0)),
 )
+FIRST_BIT = (0, 1, 2, 3)
 DIM_OF = {("x", 0): 2, ("x", 1): 3, ("y", 0): 4, ("y", 1): 5}
+
+
+SEND_GROUPS = ((0,), (1,), (2,), (3,))
+KEEP_GROUPS = ((0, 1, 2, 3),)
 
 
 def pair_bits(i):
@@ -149,39 +154,49 @@
     return got[0:2], got[2:4], got[4:6]
 
 
-def merge_body(first_ref, other_ref, own_any, got_any, out_ref, own_buf, got_buf, sems, *, portion, side):
+def merge_body(first_ref, other_ref, *refs, portions, side):
+    count = len(portions)
+    own, got, out = refs[:count], refs[count : 2 * count], refs[2 * count : 3 * count]
+    own_buf, got_buf, sems = refs[3 * count : 4 * count], refs[4 * count : 5 * count], refs[5 * count]
     copies = []
-    for v in range(4):
-        copies.append(pltpu.make_async_copy(own_any.at[v, :, :, side], own_buf.at[v], sems.at[2 * v]))
-        copies.append(pltpu.make_async_copy(got_any.at[v, :, :, side], got_buf.at[v], sems.at[2 * v + 1]))
+    for i in range(count):
+        for v in range(4):
+            place = 8 * i + 2 * v
+            copies.append(pltpu.make_async_copy(own[i].at[v, :, :, side], own_buf[i].at[v], sems.at[place]))
+            copies.append(pltpu.make_async_copy(got[i].at[v, :, :, side], got_buf[i].at[v], sems.at[place + 1]))
     for copy in copies:
         copy.start()
-    for v in range(4):
-        wait_all(copies[2 * v : 2 * v + 2])
-        first, other = first_ref[4 * portion + v], other_ref[4 * portion + v]
-        for b in range(PBLK):
-            mine = jnp.where(first == b, own_buf[v, 0], jnp.where(first + 1 == b, own_buf[v, 1], 0.0))
-            theirs = jnp.where(other == b, got_buf[v, 0], jnp.where(other + 1 == b, got_buf[v, 1], 0.0))
-            out_ref[v, b] = mine + theirs
+    for i, portion in enumerate(portions):
+        for v in range(4):
+            wait_all(copies[8 * i + 2 * v : 8 * i + 2 * v + 2])
+            view = 4 * portion + v
+            first, other = first_ref[view : view + 1], other_ref[view : view + 1]
+            for b in range(PBLK):
+                low, high = own_buf[i][v, 0], own_buf[i][v, 1]
+                mine = jnp.where(first == b, low, jnp.where(first + 1 == b, high, 0.0))
+                low, high = got_buf[i][v, 0], got_buf[i][v, 1]
+                out[i][v, b] = mine + jnp.where(other == b, low, jnp.where(other + 1 == b, high, 0.0))
 
 
 ANY = pl.BlockSpec(memory_space=pl.ANY)
 
 
-def merge(first, other, own, got, portion, bit, side):
-    rows = own.shape[2] // 2
-    cut = (1 << bit, rows >> bit)
-    own, got = (t.reshape(4, 2, cut[0], 2, cut[1], PB) for t in (own, got))
+def merge(first, other, crossing, portions, side):
+    rows = crossing[0][0].shape[2] // 2
+    cuts = [(1 << FIRST_BIT[w], rows >> FIRST_BIT[w]) for w in portions]
+    count = len(portions)
+    inputs = [crossing[w][k].reshape(4, 2, c[0], 2, c[1], PB) for k in range(2) for w, c in zip(portions, cuts)]
+    buffers = [pltpu.VMEM((4, 2) + c + (PB,), jnp.float32) for c in cuts]
     return pl.pallas_call(
-        functools.partial(merge_body, portion=portion, side=side),
-        in_specs=[SMEM, SMEM, ANY, ANY],
-        out_specs=VMEM,
-        out_shape=pltpu.VMEM((4, PBLK) + cut + (PB,), jnp.float32),
-        scratch_shapes=[pltpu.VMEM((4, 2) + cut + (PB,), jnp.float32)] * 2 + [pltpu.SemaphoreType.DMA((8,))],
-        cost_estimate=pl.CostEstimate(flops=1 << 30, transcendentals=0, bytes_accessed=2 << 20),
-        compiler_params=vmem_params(4),
+        functools.partial(merge_body, portions=portions, side=side),
+        in_specs=[VMEM, VMEM] + [ANY] * (2 * count),
+        out_specs=[VMEM] * count,
+        out_shape=[pltpu.VMEM((4, PBLK) + c + (PB,), jnp.float32) for c in cuts],
+        scratch_shapes=buffers * 2 + [pltpu.SemaphoreType.DMA((8 * count,))],
+        cost_estimate=pl.CostEstimate(flops=count << 30, transcendentals=0, bytes_accessed=count << 21),
+        compiler_params=vmem_params(3 * count + 1),
         name="merge_send" if side else "merge_keep",
-    )(first, other, own, got)
+    )(first, other, *inputs)
 
 
 def detect(natt_ref, resp_ref, sums):
@@ -210,59 +225,56 @@
 DETECT_COST = pl.CostEstimate(flops=1 << 31, transcendentals=1 << 20, bytes_accessed=1 << 20)
 
 
-def inner_body(cross_ref, place_ref, natt_ref, resp_ref, sums_ref, near_ref, partial_ref):
-    core = place_ref[0]
-
+def inner_body(cross_ref, near_share_ref, natt_ref, resp_ref, sums_ref, near_ref, partial_ref):
     def block(b, carry):
         own = [detect(natt_ref, resp_ref, [sums_ref[m, r, b] for m in range(MATS)]) for r in (0, 1)]
         near = detect(natt_ref, resp_ref, [near_ref[m, b] for m in range(MATS)])
         for c in range(CBINS):
-            leak = cross_ref[c]
+            leak = cross_ref[c : c + 1]
             for row in (0, 1):
-                side = jnp.where(core == 1 - row, near[c], 0.0)
-                partial_ref[c, row, b] = (1.0 - 2.0 * leak) * own[row][c] + leak * (own[1 - row][c] + side)
+                share = near_share_ref[row, c : c + 1]
+                side = jnp.where(share > 0.0, share * near[c], 0.0)
+                partial_ref[c, row, b] = (1.0 - 2.0 * leak) * own[row][c] + leak * own[1 - row][c] + side
         return carry
 
     lax.fori_loop(0, PBLK, block, 0)
 
 
-def inner(crosstalk, place, natt, resp, sums, near):
+def inner(leak, share, natt, resp, sums, near):
     return pl.pallas_call(
         inner_body,
-        in_specs=[SMEM] * 2 + [VMEM] * 4,
+        in_specs=[VMEM] * 6,
         out_specs=VMEM,
         out_shape=jax.ShapeDtypeStruct((CBINS,) + sums.shape[1:], jnp.float32),
         cost_estimate=DETECT_COST,
         compiler_params=vmem_params(8),
         name="inner",
-    )(crosstalk, place, natt, resp, sums, near)
-
-
-def finish_body(cross_ref, place_ref, natt_ref, resp_ref, far_ref, partial_ref, out_ref):
-    core, present = place_ref[0], place_ref[1]
-
+    )(leak, share, natt, resp, sums, near)
+
+
+def finish_body(far_share_ref, natt_ref, resp_ref, far_ref, partial_ref, out_ref):
     def block(b, carry):
         far = detect(natt_ref, resp_ref, [far_ref[m, b] for m in range(MATS)])
         columns = pl.ds(pl.multiple_of(b * PB, PB), PB)
         for c in range(CBINS):
-            side = cross_ref[c] * jnp.where(present == 1, far[c], 0.0)
-            out_ref[c, core, :, columns] = partial_ref[c, core, b] + side
-            out_ref[c, 1 - core, :, columns] = partial_ref[c, 1 - core, b]
+            for row in (0, 1):
+                share = far_share_ref[row, c : c + 1]
+                out_ref[c, row, :, columns] = partial_ref[c, row, b] + jnp.where(share > 0.0, share * far[c], 0.0)
         return carry
 
     lax.fori_loop(0, PBLK, block, 0)
 
 
-def finish(crosstalk, place, natt, resp, far, partial):
+def finish(share, natt, resp, far, partial):
     return pl.pallas_call(
         finish_body,
-        in_specs=[SMEM] * 2 + [VMEM] * 4,
+        in_specs=[VMEM] * 5,
         out_specs=VMEM,
         out_shape=jax.ShapeDtypeStruct((CBINS, 2, 16, PBLK * PB), jnp.float32),
         cost_estimate=DETECT_COST,
         compiler_params=vmem_params(8),
         name="finish",
-    )(crosstalk, place, natt, resp, far, partial)
+    )(share, natt, resp, far, partial)
 
 
 def per_device(volume, system, geometry, attenuation, response, crosstalk):
@@ -274,6 +286,7 @@
     matrix = system.reshape(depth, 32, PB)
     mine = lax.dynamic_index_in_dim(geometry, tile, 0, keepdims=False)
     partner = lax.dynamic_index_in_dim(geometry, tile ^ 1, 0, keepdims=False)
+    mine, partner = (jnp.broadcast_to(t[:, None], (16, PB)) for t in (mine, partner))
 
     own, away, columns, *rest = project_first(order, vol, matrix)
     crossing = [None] * 4
@@ -281,25 +294,24 @@
 
     def cross(w, own, away):
         crossing[w] = own, lax.ppermute(away, "core", [(0, 1), (1, 0)])
-
-    def first_send(w):
-        axis, which = ORDERS[w][0]
-        return merge(mine, partner, *crossing[w], w, DIM_OF[axis, which] - 2, 1).astype(jnp.float16)
 
     cross(0, own, away)
     others = project(columns, rest)
     for w in range(1, 4):
         cross(w, *others[w - 1])
-    sends = [first_send(w) for w in range(4)]
-    keeps, sends[3] = lax.optimization_barrier((crossing, sends[3]))
+    sends = []
+    for group in SEND_GROUPS:
+        sends += [part.astype(jnp.float16) for part in merge(mine, partner, crossing, group, 1)]
+    crossing, sends[3] = lax.optimization_barrier((crossing, sends[3]))
+    keeps = []
+    for group in KEEP_GROUPS:
+        keeps += merge(mine, partner, crossing, group, 0)
     for w in range(4):
         axis, which = ORDERS[w][0]
-        bit = DIM_OF[axis, which] - 2
         shape = [4, PBLK, 2, 2, 2, 2, 16, PB]
-        shape[2 + bit] = 1
+        shape[2 + FIRST_BIT[w]] = 1
         got = lax.ppermute(sends[w], axis, PAIRS[which])
-        keep = merge(mine, partner, *keeps[w], w, bit, 0)
-        current[w] = [keep.reshape(shape), got.reshape(shape)]
+        current[w] = [keeps[w].reshape(shape), got.reshape(shape)]
 
     def total(parts):
         value = parts[0]
@@ -339,12 +351,15 @@
     swap = [(i, i + 1) for i in range(1, count - 1, 2)]
     near = lax.ppermute(jnp.where(core == 0, bottom, top), "core", [(0, 1), (1, 0)])
     far = lax.ppermute(jnp.where(core == 0, top, bottom), axes, swap + [(j, i) for i, j in swap])
-    present = jnp.logical_and(me > 0, me < count - 1).astype(jnp.int32)
-    place = jnp.stack([core, present])
+    leak = jnp.broadcast_to(crosstalk[:, None], (CBINS, PB))
+    present = jnp.logical_and(me > 0, me < count - 1)
+    row = jnp.arange(2, dtype=jnp.int32)[:, None, None]
+    near_share = jnp.where(row == 1 - core, leak, 0.0)
+    far_share = jnp.where(jnp.logical_and(row == core, present), leak, 0.0)
     natt = jnp.broadcast_to(-attenuation[:, :, None], (MATS, EBINS, PB))
     resp = split_response(response)
-    partial = inner(crosstalk, place, natt, resp, sums, near.astype(jnp.float32))
-    return finish(crosstalk, place, natt, resp, far.astype(jnp.float32), partial)
+    partial = inner(leak, near_share, natt, resp, sums, near.astype(jnp.float32))
+    return finish(far_share, natt, resp, far.astype(jnp.float32), partial)
 
 
 def solution(mesh):

time: 94.6 us -> 93.2 us (0.985)
  the two profiles are of different devices: /device:TPU:8 before, /device:TPU:32 now
where the time goes in v4:
time: 93.2 us; the launch traced here: 92.9 us
  starting transfers between devices  38.7 us (42%)
  waiting for transfers between devices  28.4 us (30%)
  Pallas kernels  21.2 us (23%)
  other arithmetic  3.39 us (4%)
    ppermute x12, starting transfers between devices, per_device(): current[w].append(lax.ppermute(sends[w], axis, PAIRS[which]))  16.2 us
    all_to_all x1, waiting for transfers between devices, per_device(): received = lax.all_to_all(outgoing, ('zh', 'mat'), 0, 0, tiled=True)  8.9 us
    ppermute x12, waiting for transfers between devices, per_device(): current[w].append(lax.ppermute(sends[w], axis, PAIRS[which]))  8.83 us
    all_to_all x1, starting transfers between devices, per_device(): received = lax.all_to_all(outgoing, ('zh', 'mat'), 0, 0, tiled=True)  8.57 us
    ppermute x4, starting transfers between devices, per_device(): got = lax.ppermute(sends[w], axis, PAIRS[which])  8.27 us
    pallas_call x5, Pallas kernels, merge(): pl.pallas_call(functools.partial(merge_body, portions=portions, side=side...  6.62 us
    ppermute x1, waiting for transfers between devices, per_device(): lax.ppermute(jnp.where(core == 0, top, bottom), axes, swap + [(j, i) for...  6.04 us
    pallas_call x1, Pallas kernels, project(): pl.pallas_call(project_body, in_specs=[VMEM] * 4, out_specs=[HBM] * 6, ou...  4.8 us
  transfers between devices with their start and end apart: 23, of which 12 were waited for; matrix products, arithmetic and copies ran while one was open for 3% of the time, Pallas kernels for 16%

profile of v4, /device:TPU:32, one launch (start us, length us, event | category | flops | bytes accessed | tf_op | source)
XLA Modules:
  0.0 92.9 jit_solution(456473652195472107)
XLA Ops:
  0.5 4.4 %project_first.1 = (f32[4,2,256,128]{3,2,1,0:T(8,128)}, f32[4,2,256,128]{3,2,1,0:T(8,128)}, bf16[512,1024]{1,0:T(8,128)(2,1)S(1)}, bf16[1024,8,128]{2,1,0:T(8,12...) custom-call(s32[512,1]{1,0:T(8,128)S(1)} %fusion.10.order_ref, ...), custom_call_target="tpu_custom_call" | custom-call | flops 1610612736 | bytes 12582912 | tf_op jit(solution)/shard_map/project_first/pallas_call | solution.py:114
  5.0 4.8 %project.1 = (f32[4,2,256,128]{3,2,1,0:T(8,128)}, f32[4,2,256,128]{3,2,1,0:T(8,128)}, f32[4,2,256,128]{3,2,1,0:T(8,128)}, f32[4,2,256,128]{3,2,1,0:T(8,128)}, f3...) custom-call(bf16[512,1024]{1,0:T(8,128)(2,1)S(1)} %get-tuple-element.40.col_ref, ...), custom_call_target="tpu_custom_call" | custom-call | flops 3221225472 | bytes 15728640 | tf_op jit(solution)/shard_map/project/pallas_call | solution.py:144
  12.4 1.6 %collective-permute-start.4 = (f16[4,4,1,128,128]{4,3,2,1,0:T(8,128)(2,1)S(1)}, f16[4,4,1,128,128]{4,3,2,1,0:T(8,128)(2,1)S(1)}, u32[]{:S(2)}, u32[]{:S(2)}) collective-permute-start(f16[4,4,1,128,128]{4,3,2,1,0:T(8,128)(2,1)S(1)} %convert_element_type.173), channel_id=1, source_target_pairs={{0,2},{2,0},{4,6},{6,4},{1,3},{3,1},{5,7},{7,5},{8,10},{10,8},{12,... | collective-permute-start | bytes 1572872 | tf_op jit(solution)/shard_map/ppermute | solution.py:313
  16.1 2.8 %collective-permute-start.8 = (f16[4,4,2,64,128]{4,3,2,1,0:T(8,128)(2,1)S(1)}, f16[4,4,2,64,128]{4,3,2,1,0:T(8,128)(2,1)S(1)}, u32[]{:S(2)}, u32[]{:S(2)}) collective-permute-start(f16[4,4,2,64,128]{4,3,2,1,0:T(8,128)(2,1)S(1)} %convert_element_type.186), channel_id=1, source_target_pairs={{2,4},{4,2},{6,0},{0,6},{3,5},{5,3},{7,1},{1,7},{10,12},{12,10},{1... | collective-permute-start | bytes 1572872 | tf_op jit(solution)/shard_map/ppermute | solution.py:313
  20.4 1.7 %collective-permute-start.12 = (f16[4,4,4,32,128]{4,3,2,1,0:T(8,128)(2,1)S(1)}, f16[4,4,4,32,128]{4,3,2,1,0:T(8,128)(2,1)S(1)}, u32[]{:S(2)}, u32[]{:S(2)}) collective-permute-start(f16[4,4,4,32,128]{4,3,2,1,0:T(8,128)(2,1)S(1)} %convert_element_type.199), channel_id=1, source_target_pairs={{0,16},{16,0},{32,48},{48,32},{1,17},{17,1},{33,49},{49,33},{2,18}... | collective-permute-start | bytes 1572872 | tf_op jit(solution)/shard_map/ppermute | solution.py:313
  22.0 2.2 %collective-permute-start.16 = (f16[4,4,8,16,128]{4,3,2,1,0:T(8,128)(2,1)S(1)}, f16[4,4,8,16,128]{4,3,2,1,0:T(8,128)(2,1)S(1)}, u32[]{:S(2)}, u32[]{:S(2)}) collective-permute-start(f16[4,4,8,16,128]{4,3,2,1,0:T(8,128)(2,1)S(1)} %convert_element_type.172), channel_id=1, source_target_pairs={{16,32},{32,16},{48,0},{0,48},{17,33},{33,17},{49,1},{1,49},{18,34... | collective-permute-start | bytes 1572872 | tf_op jit(solution)/shard_map/ppermute | solution.py:313
  24.2 2.6 %merge_keep.1 = (f32[4,4,1,128,128]{4,3,2,1,0:T(8,128)S(1)}, f32[4,4,2,64,128]{4,3,2,1,0:T(8,128)S(1)}, f32[4,4,4,32,128]{4,3,2,1,0:T(8,128)S(1)}, f32[4,4,8,16,128]{4,3,2,1,0:T(8,128)S(1)}) custom-call(s32[16,128]{1,0:T(8,128)S(1)} %broadcast_in_dim.58.first_ref, s32[16,128]{1,0:T(8,128)S(1)} %broadcast_in_dim.60.other_ref, ...), custom_call_target="tpu_custom_call" | custom-call | flops 4294967296 | bytes 8388608 | tf_op jit(solution)/shard_map/merge_keep/pallas_call | solution.py:190
  27.1 2.3 %collective-permute-start.5 = (f16[4,4,1,1,2,2,16,128]{7,6,5,4,3,1,0,2:T(8,128)(2,1)S(1)}, f16[4,4,1,1,2,2,16,128]{7,6,5,4,3,1,0,2:T(8,128)(2,1)S(1)}, u32[]{:S(2)}, u32[]{:S(2)}) collective-permute-start(f16[4,4,1,1,2,2,16,128]{7,6,5,4,3,1,0,2:T(8,128)(2,1)S(1)} %get-tuple-element.60), channel_id=1, source_target_pairs={{2,4},{4,2},{6,0},{0,6},{3,5},{5,3},{7,1},{1,7},{10,12},{12,10},{1... | collective-permute-start | bytes 786440 | tf_op jit(solution)/shard_map/ppermute | solution.py:335
  29.4 2.8 %collective-permute-done.8 = f16[4,4,2,64,128]{4,3,2,1,0:T(8,128)(2,1)S(1)} collective-permute-done((f16[4,4,2,64,128]{4,3,2,1,0:T(8,128)(2,1)S(1)}, f16[4,4,2,64,128]{4,3,2,1,0:T(8,128)(2,1)S(1)}, u32[]{:S(2)}, u32[]{:S(2)}) %collective-permute-start.8) | collective-permute-done | bytes 524320 | tf_op jit(solution)/shard_map/ppermute | solution.py:313
  32.8 1.6 %collective-permute-done.12 = f16[4,4,4,32,128]{4,3,2,1,0:T(8,128)(2,1)S(1)} collective-permute-done((f16[4,4,4,32,128]{4,3,2,1,0:T(8,128)(2,1)S(1)}, f16[4,4,4,32,128]{4,3,2,1,0:T(8,128)(2,1)S(1)}, u32[]{:S(2)}, u32[]{:S(2)}) %collective-permute-start.12) | collective-permute-done | bytes 524320 | tf_op jit(solution)/shard_map/ppermute | solution.py:313
  34.6 3.1 %collective-permute-start.13 = (f16[4,4,2,2,1,1,16,128]{7,6,5,3,2,1,0,4:T(8,128)(2,1)S(1)}, f16[4,4,2,2,1,1,16,128]{7,6,5,3,2,1,0,4:T(8,128)(2,1)S(1)}, u32[]{:S(2)}, u32[]{:S(2)}) collective-permute-start(f16[4,4,2,2,1,1,16,128]{7,6,5,3,2,1,0,4:T(8,128)(2,1)S(1)} %get-tuple-element.66), channel_id=1, source_target_pairs={{16,32},{32,16},{48,0},{0,48},{17,33},{33,17},{49,1},{1,49},{18,34... | collective-permute-start | bytes 786440 | tf_op jit(solution)/shard_map/ppermute | solution.py:335
  38.1 2.0 %collective-permute-start.6 = (f16[4,4,1,1,1,2,16,128]{7,6,5,4,3,1,0,2:T(8,128)(2,1)S(1)}, f16[4,4,1,1,1,2,16,128]{7,6,5,4,3,1,0,2:T(8,128)(2,1)S(1)}, u32[]{:S(2)}, u32[]{:S(2)}) collective-permute-start(f16[4,4,1,1,1,2,16,128]{7,6,5,4,3,1,0,2:T(8,128)(2,1)S(1)} %add_convert_fusion.3), channel_id=1, source_target_pairs={{0,16},{16,0},{32,48},{48,32},{1,17},{17,1},{33,49},{49,33},{2,18}... | collective-permute-start | bytes 393224 | tf_op jit(solution)/shard_map/ppermute | solution.py:335
  40.1 2.7 %collective-permute-start.10 = (f16[4,4,1,1,2,1,16,128]{7,6,5,4,2,1,0,3:T(8,128)(2,1)S(1)}, f16[4,4,1,1,2,1,16,128]{7,6,5,4,2,1,0,3:T(8,128)(2,1)S(1)}, u32[]{:S(2)}, u32[]{:S(2)}) collective-permute-start(f16[4,4,1,1,2,1,16,128]{7,6,5,4,2,1,0,3:T(8,128)(2,1)S(1)} %add_convert_fusion.2), channel_id=1, source_target_pairs={{16,32},{32,16},{48,0},{0,48},{17,33},{33,17},{49,1},{1,49},{18,34... | collective-permute-start | bytes 393224 | tf_op jit(solution)/shard_map/ppermute | solution.py:335
  44.7 1.8 %collective-permute-done.17 = f16[4,4,2,2,1,1,16,128]{7,6,4,3,2,1,0,5:T(8,128)(2,1)S(1)} collective-permute-done((f16[4,4,2,2,1,1,16,128]{7,6,4,3,2,1,0,5:T(8,128)(2,1)S(1)}, f16[4,4,2,2,1,1,16,128]{7,6,4,3,2,1,0,5:T(8,128)(2,1)S(1)}, u32[]{:S(2)}, u32[]{:S(2)}) %collective-permute-start.17) | collective-permute-done | bytes 262176 | tf_op jit(solution)/shard_map/ppermute | solution.py:335
  48.1 1.6 %collective-permute-start.7 = (f16[4,4,1,1,1,1,16,128]{7,6,5,4,3,1,0,2:T(8,128)(2,1)S(1)}, f16[4,4,1,1,1,1,16,128]{7,6,5,4,3,1,0,2:T(8,128)(2,1)S(1)}, u32[]{:S(2)}, u32[]{:S(2)}) collective-permute-start(f16[4,4,1,1,1,1,16,128]{7,6,5,4,3,1,0,2:T(8,128)(2,1)S(1)} %add_convert_fusion.11), channel_id=1, source_target_pairs={{16,32},{32,16},{48,0},{0,48},{17,33},{33,17},{49,1},{1,49},{18,34... | collective-permute-start | bytes 196616 | tf_op jit(solution)/shard_map/ppermute | solution.py:335
  49.9 2.0 %collective-permute-start.15 = (f16[4,4,1,1,1,1,16,128]{7,6,5,3,2,1,0,4:T(8,128)(2,1)S(1)}, f16[4,4,1,1,1,1,16,128]{7,6,5,3,2,1,0,4:T(8,128)(2,1)S(1)}, u32[]{:S(2)}, u32[]{:S(2)}) collective-permute-start(f16[4,4,1,1,1,1,16,128]{7,6,5,3,2,1,0,4:T(8,128)(2,1)S(1)} %add_convert_fusion.7), channel_id=1, source_target_pairs={{2,4},{4,2},{6,0},{0,6},{3,5},{5,3},{7,1},{1,7},{10,12},{12,10},{1... | collective-permute-start | bytes 196616 | tf_op jit(solution)/shard_map/ppermute | solution.py:335
  51.9 1.6 %collective-permute-done.18 = f16[4,4,2,1,1,1,16,128]{7,6,4,3,2,1,0,5:T(8,128)(2,1)S(1)} collective-permute-done((f16[4,4,2,1,1,1,16,128]{7,6,4,3,2,1,0,5:T(8,128)(2,1)S(1)}, f16[4,4,2,1,1,1,16,128]{7,6,4,3,2,1,0,5:T(8,128)(2,1)S(1)}, u32[]{:S(2)}, u32[]{:S(2)}) %collective-permute-start.18) | collective-permute-done | bytes 131104 | tf_op jit(solution)/shard_map/ppermute | solution.py:335
  55.7 2.1 %collective-permute-done.19 = f16[4,4,1,1,1,1,16,128]{7,6,4,3,2,1,0,5:T(8,128)(2,1)S(1)} collective-permute-done((f16[4,4,1,1,1,1,16,128]{7,6,4,3,2,1,0,5:T(8,128)(2,1)S(1)}, f16[4,4,1,1,1,1,16,128]{7,6,4,3,2,1,0,5:T(8,128)(2,1)S(1)}, u32[]{:S(2)}, u32[]{:S(2)}) %collective-permute-start.19) | collective-permute-done | bytes 65568 | tf_op jit(solution)/shard_map/ppermute | solution.py:335
  58.9 8.6 %all-to-all-start = ((f16[8,2,64,128]{3,2,1,0:T(8,128)(2,1)}), f16[8,2,64,128]{3,2,1,0:T(8,128)(2,1)S(1)}, u32[]{:S(2)}, u32[]{:S(2)}) async-start(f16[8,2,64,128]{3,2,1,0:T(8,128)(2,1)} %bitcast.31), calls=%async_computation | async-start | bytes 524288 | tf_op jit(solution)/shard_map/all_to_all | solution.py:341
  67.6 8.9 %all-to-all-done = f16[8,2,64,128]{3,2,1,0:T(8,128)(2,1)S(1)} async-done(((f16[8,2,64,128]{3,2,1,0:T(8,128)(2,1)}), f16[8,2,64,128]{3,2,1,0:T(8,128)(2,1)S(1)}, u32[]{:S(2)}, u32[]{:S(2)}) %all-to-all-start) | async-done | bytes 262176 | tf_op jit(solution)/shard_map/all_to_all | solution.py:341
  76.9 4.4 %collective-permute-start.20 = (f16[4,4,16,128]{3,2,1,0:T(8,128)(2,1)S(1)}, f16[4,4,16,128]{3,2,1,0:T(8,128)(2,1)S(1)}, u32[]{:S(2)}, u32[]{:S(2)}) collective-permute-start(f16[4,4,16,128]{3,2,1,0:T(8,128)(2,1)S(1)} %get-tuple-element.82), channel_id=1, source_target_pairs={{1,2},{3,4},{5,6},{7,8},{9,10},{11,12},{13,14},{15,16},{17,18},{19... | collective-permute-start | bytes 196616 | tf_op jit(solution)/shard_map/ppermute | solution.py:353
  81.5 3.2 %inner.1.partial_ref = f32[8,2,4,16,128]{4,3,2,1,0:T(8,128)S(1)} custom-call(f32[8,128]{1,0:T(8,128)S(1)} %broadcast_in_dim.61.cross_ref, f32[2,8,128]{2,1,0:T(8,128)S(1)} %get-tuple-element.85.near_share_ref, f32[4,64,128]{2,1,0:T(8,128)S(1)} %broadcast_in_dim.56.natt_ref, bf16[16,128]{1,0:T(8,128)(2,1)S(1)} %fusion.48.resp_ref, ...), custom_call_target="tpu_custom_call" | custom-call | flops 2147483648 | bytes 1048576 | tf_op jit(solution)/shard_map/inner/pallas_call | solution.py:244
  84.7 6.0 %collective-permute-done.20 = f16[4,4,16,128]{3,2,1,0:T(8,128)(2,1)S(1)} collective-permute-done((f16[4,4,16,128]{3,2,1,0:T(8,128)(2,1)S(1)}, f16[4,4,16,128]{3,2,1,0:T(8,128)(2,1)S(1)}, u32[]{:S(2)}, u32[]{:S(2)}) %collective-permute-start.20) | collective-permute-done | bytes 65568 | tf_op jit(solution)/shard_map/ppermute | solution.py:353
  90.7 2.2 %finish.1 = f32[8,2,16,512]{3,2,1,0:T(8,128)} custom-call(f32[2,8,128]{2,1,0:T(8,128)S(1)} %get-tuple-element.86.far_share_ref, f32[4,64,128]{2,1,0:T(8,128)S(1)} %broadcast_in_dim.56.natt_ref, bf16[16,128]{1,0:T(8,128)(2,1)S(1)} %fusion.48.resp_ref, f32[4,4,16,128]{3,2,1,0:T(8,128)S(1)} %convert_element_type.226.far_ref, ...), custom_call_target="tpu_custom_call" | custom-call | flops 2147483648 | bytes 1048576 | tf_op jit(solution)/shard_map/finish/pallas_call | solution.py:269
  (91 shorter events, 15.4 us)
Async XLA Ops:
  4.9 6.2 %collective-permute-start = (f32[4,2,256,128]{3,2,1,0:T(8,128)}, f32[4,2,256,128]{3,2,1,0:T(8,128)S(1)}, u32[]{:S(2)}, u32[]{:S(2)}) collective-permute-start(f32[4,2,256,128]{3,2,1,0:T(8,128)} %get-tuple-element.39), channel_id=1, source_target_pairs={{0,1},{1,0},{2,3},{3,2},{4,5},{5,4},{6,7},{7,6},{8,9},{9,8},{10,11... | collective-permute-start | bytes 3145736 | tf_op jit(solution)/shard_map/ppermute | solution.py:296
  9.8 4.1 %collective-permute-start.3 = (f32[4,2,256,128]{3,2,1,0:T(8,128)}, f32[4,2,256,128]{3,2,1,0:T(8,128)S(1)}, u32[]{:S(2)}, u32[]{:S(2)}) collective-permute-start(f32[4,2,256,128]{3,2,1,0:T(8,128)} %get-tuple-element.49), channel_id=1, source_target_pairs={{0,1},{1,0},{2,3},{3,2},{4,5},{5,4},{6,7},{7,6},{8,9},{9,8},{10,11... | collective-permute-start | bytes 3145736 | tf_op jit(solution)/shard_map/ppermute | solution.py:296
  10.4 4.1 %collective-permute-start.1 = (f32[4,2,256,128]{3,2,1,0:T(8,128)}, f32[4,2,256,128]{3,2,1,0:T(8,128)}, u32[]{:S(2)}, u32[]{:S(2)}) collective-permute-start(f32[4,2,256,128]{3,2,1,0:T(8,128)} %get-tuple-element.45), channel_id=1, source_target_pairs={{0,1},{1,0},{2,3},{3,2},{4,5},{5,4},{6,7},{7,6},{8,9},{9,8},{10,11... | collective-permute-start | bytes 3145736 | tf_op jit(solution)/shard_map/ppermute | solution.py:296
  10.5 5.5 %collective-permute-start.2 = (f32[4,2,256,128]{3,2,1,0:T(8,128)}, f32[4,2,256,128]{3,2,1,0:T(8,128)}, u32[]{:S(2)}, u32[]{:S(2)}) collective-permute-start(f32[4,2,256,128]{3,2,1,0:T(8,128)} %get-tuple-element.47), channel_id=1, source_target_pairs={{0,1},{1,0},{2,3},{3,2},{4,5},{5,4},{6,7},{7,6},{8,9},{9,8},{10,11... | collective-permute-start | bytes 3145736 | tf_op jit(solution)/shard_map/ppermute | solution.py:296
  12.4 14.5 %collective-permute-start.4 = (f16[4,4,1,128,128]{4,3,2,1,0:T(8,128)(2,1)S(1)}, f16[4,4,1,128,128]{4,3,2,1,0:T(8,128)(2,1)S(1)}, u32[]{:S(2)}, u32[]{:S(2)}) collective-permute-start(f16[4,4,1,128,128]{4,3,2,1,0:T(8,128)(2,1)S(1)} %convert_element_type.173), channel_id=1, source_target_pairs={{0,2},{2,0},{4,6},{6,4},{1,3},{3,1},{5,7},{7,5},{8,10},{10,8},{12,... | collective-permute-start | bytes 1572872 | tf_op jit(solution)/shard_map/ppermute | solution.py:313
  16.1 16.1 %collective-permute-start.8 = (f16[4,4,2,64,128]{4,3,2,1,0:T(8,128)(2,1)S(1)}, f16[4,4,2,64,128]{4,3,2,1,0:T(8,128)(2,1)S(1)}, u32[]{:S(2)}, u32[]{:S(2)}) collective-permute-start(f16[4,4,2,64,128]{4,3,2,1,0:T(8,128)(2,1)S(1)} %convert_element_type.186), channel_id=1, source_target_pairs={{2,4},{4,2},{6,0},{0,6},{3,5},{5,3},{7,1},{1,7},{10,12},{12,10},{1... | collective-permute-start | bytes 1572872 | tf_op jit(solution)/shard_map/ppermute | solution.py:313
  20.4 14.0 %collective-permute-start.12 = (f16[4,4,4,32,128]{4,3,2,1,0:T(8,128)(2,1)S(1)}, f16[4,4,4,32,128]{4,3,2,1,0:T(8,128)(2,1)S(1)}, u32[]{:S(2)}, u32[]{:S(2)}) collective-permute-start(f16[4,4,4,32,128]{4,3,2,1,0:T(8,128)(2,1)S(1)} %convert_element_type.199), channel_id=1, source_target_pairs={{0,16},{16,0},{32,48},{48,32},{1,17},{17,1},{33,49},{49,33},{2,18}... | collective-permute-start | bytes 1572872 | tf_op jit(solution)/shard_map/ppermute | solution.py:313
  22.0 15.6 %collective-permute-start.16 = (f16[4,4,8,16,128]{4,3,2,1,0:T(8,128)(2,1)S(1)}, f16[4,4,8,16,128]{4,3,2,1,0:T(8,128)(2,1)S(1)}, u32[]{:S(2)}, u32[]{:S(2)}) collective-permute-start(f16[4,4,8,16,128]{4,3,2,1,0:T(8,128)(2,1)S(1)} %convert_element_type.172), channel_id=1, source_target_pairs={{16,32},{32,16},{48,0},{0,48},{17,33},{33,17},{49,1},{1,49},{18,34... | collective-permute-start | bytes 1572872 | tf_op jit(solution)/shard_map/ppermute | solution.py:313
  27.1 11.0 %collective-permute-start.5 = (f16[4,4,1,1,2,2,16,128]{7,6,5,4,3,1,0,2:T(8,128)(2,1)S(1)}, f16[4,4,1,1,2,2,16,128]{7,6,5,4,3,1,0,2:T(8,128)(2,1)S(1)}, u32[]{:S(2)}, u32[]{:S(2)}) collective-permute-start(f16[4,4,1,1,2,2,16,128]{7,6,5,4,3,1,0,2:T(8,128)(2,1)S(1)} %get-tuple-element.60), channel_id=1, source_target_pairs={{2,4},{4,2},{6,0},{0,6},{3,5},{5,3},{7,1},{1,7},{10,12},{12,10},{1... | collective-permute-start | bytes 786440 | tf_op jit(solution)/shard_map/ppermute | solution.py:335
  32.4 7.7 %collective-permute-start.9 = (f16[4,4,1,1,2,2,16,128]{7,6,5,4,2,1,0,3:T(8,128)(2,1)S(1)}, f16[4,4,1,1,2,2,16,128]{7,6,5,4,2,1,0,3:T(8,128)(2,1)S(1)}, u32[]{:S(2)}, u32[]{:S(2)}) collective-permute-start(f16[4,4,1,1,2,2,16,128]{7,6,5,4,2,1,0,3:T(8,128)(2,1)S(1)} %get-tuple-element.63), channel_id=1, source_target_pairs={{0,2},{2,0},{4,6},{6,4},{1,3},{3,1},{5,7},{7,5},{8,10},{10,8},{12,... | collective-permute-start | bytes 786440 | tf_op jit(solution)/shard_map/ppermute | solution.py:335
  34.6 9.8 %collective-permute-start.13 = (f16[4,4,2,2,1,1,16,128]{7,6,5,3,2,1,0,4:T(8,128)(2,1)S(1)}, f16[4,4,2,2,1,1,16,128]{7,6,5,3,2,1,0,4:T(8,128)(2,1)S(1)}, u32[]{:S(2)}, u32[]{:S(2)}) collective-permute-start(f16[4,4,2,2,1,1,16,128]{7,6,5,3,2,1,0,4:T(8,128)(2,1)S(1)} %get-tuple-element.66), channel_id=1, source_target_pairs={{16,32},{32,16},{48,0},{0,48},{17,33},{33,17},{49,1},{1,49},{18,34... | collective-permute-start | bytes 786440 | tf_op jit(solution)/shard_map/ppermute | solution.py:335
  37.8 8.7 %collective-permute-start.17 = (f16[4,4,2,2,1,1,16,128]{7,6,4,3,2,1,0,5:T(8,128)(2,1)S(1)}, f16[4,4,2,2,1,1,16,128]{7,6,4,3,2,1,0,5:T(8,128)(2,1)S(1)}, u32[]{:S(2)}, u32[]{:S(2)}) collective-permute-start(f16[4,4,2,2,1,1,16,128]{7,6,4,3,2,1,0,5:T(8,128)(2,1)S(1)} %get-tuple-element.70), channel_id=1, source_target_pairs={{0,16},{16,0},{32,48},{48,32},{1,17},{17,1},{33,49},{49,33},{2,18}... | collective-permute-start | bytes 786440 | tf_op jit(solution)/shard_map/ppermute | solution.py:335
  38.1 9.9 %collective-permute-start.6 = (f16[4,4,1,1,1,2,16,128]{7,6,5,4,3,1,0,2:T(8,128)(2,1)S(1)}, f16[4,4,1,1,1,2,16,128]{7,6,5,4,3,1,0,2:T(8,128)(2,1)S(1)}, u32[]{:S(2)}, u32[]{:S(2)}) collective-permute-start(f16[4,4,1,1,1,2,16,128]{7,6,5,4,3,1,0,2:T(8,128)(2,1)S(1)} %add_convert_fusion.3), channel_id=1, source_target_pairs={{0,16},{16,0},{32,48},{48,32},{1,17},{17,1},{33,49},{49,33},{2,18}... | collective-permute-start | bytes 393224 | tf_op jit(solution)/shard_map/ppermute | solution.py:335
  40.1 9.6 %collective-permute-start.10 = (f16[4,4,1,1,2,1,16,128]{7,6,5,4,2,1,0,3:T(8,128)(2,1)S(1)}, f16[4,4,1,1,2,1,16,128]{7,6,5,4,2,1,0,3:T(8,128)(2,1)S(1)}, u32[]{:S(2)}, u32[]{:S(2)}) collective-permute-start(f16[4,4,1,1,2,1,16,128]{7,6,5,4,2,1,0,3:T(8,128)(2,1)S(1)} %add_convert_fusion.2), channel_id=1, source_target_pairs={{16,32},{32,16},{48,0},{0,48},{17,33},{33,17},{49,1},{1,49},{18,34... | collective-permute-start | bytes 393224 | tf_op jit(solution)/shard_map/ppermute | solution.py:335
  44.4 5.5 %collective-permute-start.14 = (f16[4,4,1,2,1,1,16,128]{7,6,5,3,2,1,0,4:T(8,128)(2,1)S(1)}, f16[4,4,1,2,1,1,16,128]{7,6,5,3,2,1,0,4:T(8,128)(2,1)S(1)}, u32[]{:S(2)}, u32[]{:S(2)}) collective-permute-start(f16[4,4,1,2,1,1,16,128]{7,6,5,3,2,1,0,4:T(8,128)(2,1)S(1)} %add_convert_fusion.1), channel_id=1, source_target_pairs={{0,2},{2,0},{4,6},{6,4},{1,3},{3,1},{5,7},{7,5},{8,10},{10,8},{12,... | collective-permute-start | bytes 393224 | tf_op jit(solution)/shard_map/ppermute | solution.py:335
  46.5 6.9 %collective-permute-start.18 = (f16[4,4,2,1,1,1,16,128]{7,6,4,3,2,1,0,5:T(8,128)(2,1)S(1)}, f16[4,4,2,1,1,1,16,128]{7,6,4,3,2,1,0,5:T(8,128)(2,1)S(1)}, u32[]{:S(2)}, u32[]{:S(2)}) collective-permute-start(f16[4,4,2,1,1,1,16,128]{7,6,4,3,2,1,0,5:T(8,128)(2,1)S(1)} %add_convert_fusion), channel_id=1, source_target_pairs={{2,4},{4,2},{6,0},{0,6},{3,5},{5,3},{7,1},{1,7},{10,12},{12,10},{1... | collective-permute-start | bytes 393224 | tf_op jit(solution)/shard_map/ppermute | solution.py:335
  48.1 19.5 %copy-start.6 = (f32[8]{0:T(128)S(1)}, f32[8]{0:T(128)}, u32[]{:S(2)}) copy-start(f32[8]{0:T(128)} %param.11) | copy-start | bytes 100
  48.1 5.6 %collective-permute-start.7 = (f16[4,4,1,1,1,1,16,128]{7,6,5,4,3,1,0,2:T(8,128)(2,1)S(1)}, f16[4,4,1,1,1,1,16,128]{7,6,5,4,3,1,0,2:T(8,128)(2,1)S(1)}, u32[]{:S(2)}, u32[]{:S(2)}) collective-permute-start(f16[4,4,1,1,1,1,16,128]{7,6,5,4,3,1,0,2:T(8,128)(2,1)S(1)} %add_convert_fusion.11), channel_id=1, source_target_pairs={{16,32},{32,16},{48,0},{0,48},{17,33},{33,17},{49,1},{1,49},{18,34... | collective-permute-start | bytes 196616 | tf_op jit(solution)/shard_map/ppermute | solution.py:335
  49.8 4.4 %collective-permute-start.11 = (f16[4,4,1,1,1,1,16,128]{7,6,5,4,2,1,0,3:T(8,128)(2,1)S(1)}, f16[4,4,1,1,1,1,16,128]{7,6,5,4,2,1,0,3:T(8,128)(2,1)S(1)}, u32[]{:S(2)}, u32[]{:S(2)}) collective-permute-start(f16[4,4,1,1,1,1,16,128]{7,6,5,4,2,1,0,3:T(8,128)(2,1)S(1)} %add_convert_fusion.9), channel_id=1, source_target_pairs={{0,16},{16,0},{32,48},{48,32},{1,17},{17,1},{33,49},{49,33},{2,18}... | collective-permute-start | bytes 196616 | tf_op jit(solution)/shard_map/ppermute | solution.py:335
  49.9 5.6 %collective-permute-start.15 = (f16[4,4,1,1,1,1,16,128]{7,6,5,3,2,1,0,4:T(8,128)(2,1)S(1)}, f16[4,4,1,1,1,1,16,128]{7,6,5,3,2,1,0,4:T(8,128)(2,1)S(1)}, u32[]{:S(2)}, u32[]{:S(2)}) collective-permute-start(f16[4,4,1,1,1,1,16,128]{7,6,5,3,2,1,0,4:T(8,128)(2,1)S(1)} %add_convert_fusion.7), channel_id=1, source_target_pairs={{2,4},{4,2},{6,0},{0,6},{3,5},{5,3},{7,1},{1,7},{10,12},{12,10},{1... | collective-permute-start | bytes 196616 | tf_op jit(solution)/shard_map/ppermute | solution.py:335
  53.5 4.4 %collective-permute-start.19 = (f16[4,4,1,1,1,1,16,128]{7,6,4,3,2,1,0,5:T(8,128)(2,1)S(1)}, f16[4,4,1,1,1,1,16,128]{7,6,4,3,2,1,0,5:T(8,128)(2,1)S(1)}, u32[]{:S(2)}, u32[]{:S(2)}) collective-permute-start(f16[4,4,1,1,1,1,16,128]{7,6,4,3,2,1,0,5:T(8,128)(2,1)S(1)} %add_convert_fusion.5), channel_id=1, source_target_pairs={{0,2},{2,0},{4,6},{6,4},{1,3},{3,1},{5,7},{7,5},{8,10},{10,8},{12,... | collective-permute-start | bytes 196616 | tf_op jit(solution)/shard_map/ppermute | solution.py:335
  58.9 17.6 %all-to-all-start = ((f16[8,2,64,128]{3,2,1,0:T(8,128)(2,1)}), f16[8,2,64,128]{3,2,1,0:T(8,128)(2,1)S(1)}, u32[]{:S(2)}, u32[]{:S(2)}) async-start(f16[8,2,64,128]{3,2,1,0:T(8,128)(2,1)} %bitcast.31), calls=%async_computation | async-start | bytes 524288 | tf_op jit(solution)/shard_map/all_to_all | solution.py:341
  76.7 4.6 %collective-permute-start.21 = (f16[4,4,16,128]{3,2,1,0:T(8,128)(2,1)S(1)}, f16[4,4,16,128]{3,2,1,0:T(8,128)(2,1)S(1)}, u32[]{:S(2)}, u32[]{:S(2)}) collective-permute-start(f16[4,4,16,128]{3,2,1,0:T(8,128)(2,1)S(1)} %get-tuple-element.81), channel_id=1, source_target_pairs={{0,1},{1,0},{2,3},{3,2},{4,5},{5,4},{6,7},{7,6},{8,9},{9,8},{10,11... | collective-permute-start | bytes 196616 | tf_op jit(solution)/shard_map/ppermute | solution.py:352
  76.9 13.8 %collective-permute-start.20 = (f16[4,4,16,128]{3,2,1,0:T(8,128)(2,1)S(1)}, f16[4,4,16,128]{3,2,1,0:T(8,128)(2,1)S(1)}, u32[]{:S(2)}, u32[]{:S(2)}) collective-permute-start(f16[4,4,16,128]{3,2,1,0:T(8,128)(2,1)S(1)} %get-tuple-element.82), channel_id=1, source_target_pairs={{1,2},{3,4},{5,6},{7,8},{9,10},{11,12},{13,14},{15,16},{17,18},{19... | collective-permute-start | bytes 196616 | tf_op jit(solution)/shard_map/ppermute | solution.py:353
  (7 other events, 59.1 us)

commit v5 on v4

--- a/solution.py
+++ b/solution.py
@@ -30,13 +30,13 @@
 
 
 def pair_bits(i):
-    return ((i + 1) // 2) % 2, i // 2
+    return ((i + 1) >> 1) & 1, i >> 1
 
 
 def row_order(slice_count):
-    pos = jnp.arange(slice_count, dtype=jnp.int32)
-    bits = [(pos // (256 >> n)) % 2 for n in range(5)]
-    rest = pos % 16
+    pos = lax.broadcasted_iota(jnp.int32, (slice_count, 1), 0)
+    bits = [(pos >> (8 - n)) & 1 for n in range(5)]
+    rest = pos & 15
     core = bits[0] ^ lax.axis_index("core")
 
     def place(b0, b1, name):
@@ -46,7 +46,7 @@
 
     x = place(bits[1], bits[2], "x")
     y = place(bits[3], bits[4], "y")
-    mat, zh, r = rest // 4, (rest // 2) % 2, rest % 2
+    mat, zh, r = rest >> 2, (rest >> 1) & 1, rest & 1
     return mat * 128 + y * 32 + zh * 16 + x * 4 + core * 2 + r
 
 
@@ -81,7 +81,7 @@
 
 
 def first_body(
-    order_ref, vol_hbm, sys_hbm, own_hbm, away_hbm, col_ref, m1_ref, m2_ref, m3_ref, vol_buf, m0_buf, buf, sems, out_sems
+    vol_hbm, sys_hbm, own_hbm, away_hbm, col_ref, m1_ref, m2_ref, m3_ref, vol_buf, m0_buf, buf, sems, out_sems
 ):
     copies = [pltpu.make_async_copy(vol_hbm, vol_buf, sems.at[4])]
     for w, target in enumerate((m0_buf, m1_ref, m2_ref, m3_ref)):
@@ -89,7 +89,7 @@
     for copy in copies:
         copy.start()
     rows = vol_buf.shape[0]
-    chosen = (order_ref[...] == lax.broadcasted_iota(jnp.int32, (rows, rows), 1)).astype(jnp.bfloat16)
+    chosen = (row_order(rows) == lax.broadcasted_iota(jnp.int32, (rows, rows), 1)).astype(jnp.bfloat16)
     copies[0].wait()
     columns = jnp.dot(chosen, vol_buf[...], preferred_element_type=jnp.float32).astype(jnp.bfloat16)
     col_ref[...] = columns
@@ -107,13 +107,13 @@
     return pltpu.with_memory_space_constraint(x, pltpu.VMEM)
 
 
-def project_first(order, vol, matrix):
+def project_first(vol, matrix):
     rows, depth = vol.shape
     half = pltpu.HBM((4, 2, rows // 2, PB), jnp.float32)
     part = pltpu.VMEM((depth, 8, PB), jnp.bfloat16)
     return pl.pallas_call(
         first_body,
-        in_specs=[VMEM, HBM, HBM],
+        in_specs=[HBM, HBM],
         out_specs=[HBM] * 2 + [VMEM] * 4,
         out_shape=[half, half, pltpu.VMEM((rows, depth), jnp.bfloat16), part, part, part],
         scratch_shapes=[
@@ -126,7 +126,7 @@
         cost_estimate=pl.CostEstimate(flops=2 * rows * depth * 12 * PB, transcendentals=0, bytes_accessed=12 << 20),
         compiler_params=vmem_params(16),
         name="project_first",
-    )(order, in_hbm(vol), in_hbm(matrix))
+    )(in_hbm(vol), in_hbm(matrix))
 
 
 def project_body(col_ref, *refs):
@@ -199,14 +199,17 @@
     )(first, other, *inputs)
 
 
-def detect(natt_ref, resp_ref, sums):
+LARGEST = float(jnp.finfo(jnp.bfloat16).max)
+
+
+def detect(natt_ref, resp_ref, row_of):
     high, low = [], []
     for v in range(16):
-        power = natt_ref[0] * sums[0][v : v + 1]
+        power = natt_ref[0] * row_of(0, v)
         for m in range(1, MATS):
-            power = power + natt_ref[m] * sums[m][v : v + 1]
+            power = power + natt_ref[m] * row_of(m, v)
         passed = jnp.exp(power)
-        top = passed.astype(jnp.bfloat16)
+        top = jnp.minimum(passed, LARGEST).astype(jnp.bfloat16)
         high.append(top)
         low.append((passed - top.astype(jnp.float32)).astype(jnp.bfloat16))
     terms = jnp.concatenate([jnp.concatenate(high, axis=1), jnp.concatenate(low, axis=1)], axis=0)
@@ -226,18 +229,18 @@
 
 
 def inner_body(cross_ref, near_share_ref, natt_ref, resp_ref, sums_ref, near_ref, partial_ref):
-    def block(b, carry):
-        own = [detect(natt_ref, resp_ref, [sums_ref[m, r, b] for m in range(MATS)]) for r in (0, 1)]
-        near = detect(natt_ref, resp_ref, [near_ref[m, b] for m in range(MATS)])
+    def rows(ref, r, b):
+        return lambda m, v: ref[m, r, PBLK * v + b : PBLK * v + b + 1, :]
+
+    for b in range(PBLK):
+        own = [detect(natt_ref, resp_ref, rows(sums_ref, r, b)) for r in (0, 1)]
+        near = detect(natt_ref, resp_ref, rows(near_ref, 0, b))
         for c in range(CBINS):
             leak = cross_ref[c : c + 1]
             for row in (0, 1):
                 share = near_share_ref[row, c : c + 1]
                 side = jnp.where(share > 0.0, share * near[c], 0.0)
                 partial_ref[c, row, b] = (1.0 - 2.0 * leak) * own[row][c] + leak * own[1 - row][c] + side
-        return carry
-
-    lax.fori_loop(0, PBLK, block, 0)
 
 
 def inner(leak, share, natt, resp, sums, near):
@@ -245,7 +248,7 @@
         inner_body,
         in_specs=[VMEM] * 6,
         out_specs=VMEM,
-        out_shape=jax.ShapeDtypeStruct((CBINS,) + sums.shape[1:], jnp.float32),
+        out_shape=jax.ShapeDtypeStruct((CBINS, 2, PBLK, 16, PB), jnp.float32),
         cost_estimate=DETECT_COST,
         compiler_params=vmem_params(8),
         name="inner",
@@ -253,16 +256,13 @@
 
 
 def finish_body(far_share_ref, natt_ref, resp_ref, far_ref, partial_ref, out_ref):
-    def block(b, carry):
-        far = detect(natt_ref, resp_ref, [far_ref[m, b] for m in range(MATS)])
-        columns = pl.ds(pl.multiple_of(b * PB, PB), PB)
+    for b in range(PBLK):
+        far = detect(natt_ref, resp_ref, lambda m, v: far_ref[m, 0, PBLK * v + b : PBLK * v + b + 1, :])
         for c in range(CBINS):
             for row in (0, 1):
                 share = far_share_ref[row, c : c + 1]
-                out_ref[c, row, :, columns] = partial_ref[c, row, b] + jnp.where(share > 0.0, share * far[c], 0.0)
-        return carry
-
-    lax.fori_loop(0, PBLK, block, 0)
+                side = jnp.where(share > 0.0, share * far[c], 0.0)
+                out_ref[c, row, :, b * PB : (b + 1) * PB] = partial_ref[c, row, b] + side
 
 
 def finish(share, natt, resp, far, partial):
@@ -282,13 +282,12 @@
     depth = volume.shape[3]
     tile = lax.axis_index(TILE_AXES)
     vol = volume.reshape(rows, depth)
-    order = row_order(rows)[:, None]
     matrix = system.reshape(depth, 32, PB)
     mine = lax.dynamic_index_in_dim(geometry, tile, 0, keepdims=False)
     partner = lax.dynamic_index_in_dim(geometry, tile ^ 1, 0, keepdims=False)
     mine, partner = (jnp.broadcast_to(t[:, None], (16, PB)) for t in (mine, partner))
 
-    own, away, columns, *rest = project_first(order, vol, matrix)
+    own, away, columns, *rest = project_first(vol, matrix)
     crossing = [None] * 4
     current = [None] * 4
 
@@ -337,14 +336,14 @@
         current[w] = total(current[w]).astype(jnp.float16)
 
     whole = jnp.concatenate([c.reshape(4, PBLK, MATS, 2, 2, PB) for c in current], axis=0)
-    outgoing = whole.transpose(3, 2, 4, 1, 0, 5).reshape(8, 2, 64, PB)
+    outgoing = whole.transpose(3, 2, 4, 0, 1, 5).reshape(8, 2, 64, PB)
     received = lax.all_to_all(outgoing, ("zh", "mat"), 0, 0, tiled=True)
-    received = received.reshape(2, MATS, 2, PBLK, 16, PB).astype(jnp.float32)
+    received = received.reshape(2, MATS, 2, 64, PB).astype(jnp.float32)
     sums = received[0] + received[1]
 
     core = lax.axis_index("core")
     rounded = sums.astype(jnp.float16)
-    top, bottom = rounded[:, 0], rounded[:, 1]
+    top, bottom = rounded[:, 0:1], rounded[:, 1:2]
     axes = ("mat",) + TILE_AXES
     count = lax.axis_size(axes)
     me = lax.axis_index(axes)

time: 93.2 us -> 97.5 us (1.046)
  waiting for transfers between devices: 28.4 us -> 31.4 us
  local copies, waits for them, and re-layouts: 0.78 us -> 3.61 us
  Pallas kernels: 21.2 us -> 19.6 us
  starting transfers between devices: 38.7 us -> 40.1 us
  other arithmetic: 3.39 us -> 2.11 us
    ppermute x4, waiting for transfers between devices: 0.21 us -> 4.33 us  [cross(): crossing[w] = (own, lax.ppermute(away, 'core', [(0, 1), (1, 0)]))]
    ppermute x12, waiting for transfers between devices: 8.83 us -> 7.03 us  [per_device(): current[w].append(lax.ppermute(sends[w], axis, PAIRS[which]))]
    ppermute x4, waiting for transfers between devices: 4.39 us -> 5.75 us  [per_device(): got = lax.ppermute(sends[w], axis, PAIRS[which])]
    ppermute x12, starting transfers between devices: 16.2 us -> 17.5 us  [per_device(): current[w].append(lax.ppermute(sends[w], axis, PAIRS[which]))]
    pallas_call x5, Pallas kernels: 6.62 us -> 5.34 us  [merge(): pl.pallas_call(functools.partial(merge_body, portions=portions, side=side...]
    unnamed x16, local copies, waits for them, and re-layouts: 0.04 us -> 1.26 us
    slice x0 -> x8, local copies, waits for them, and re-layouts: none -> 1.01 us  [per_device(): current[w] = [lax.slice_in_dim(t, 0, 1, axis=dim) for t in current[w]]]
  transfers between devices with their start and end apart: 23 -> 23, of which waited for: 12 -> 16; matrix products, arithmetic and copies ran while one was open for 3% -> 3% of each run, Pallas kernels for 16% -> 5%
where the time goes in v5:
time: 97.5 us; the launch traced here: 97.2 us
  starting transfers between devices  40.1 us (41%)
  waiting for transfers between devices  31.4 us (32%)
  Pallas kernels  19.6 us (20%)
  local copies, waits for them, and re-layouts  3.61 us (4%)
  other arithmetic  2.11 us (2%)
    ppermute x12, starting transfers between devices, per_device(): current[w].append(lax.ppermute(sends[w], axis, PAIRS[which]))  17.5 us
    all_to_all x1, waiting for transfers between devices, per_device(): received = lax.all_to_all(outgoing, ('zh', 'mat'), 0, 0, tiled=True)  8.9 us
    all_to_all x1, starting transfers between devices, per_device(): received = lax.all_to_all(outgoing, ('zh', 'mat'), 0, 0, tiled=True)  8.57 us
    ppermute x4, starting transfers between devices, per_device(): got = lax.ppermute(sends[w], axis, PAIRS[which])  7.6 us
    ppermute x12, waiting for transfers between devices, per_device(): current[w].append(lax.ppermute(sends[w], axis, PAIRS[which]))  7.03 us
    ppermute x4, waiting for transfers between devices, per_device(): got = lax.ppermute(sends[w], axis, PAIRS[which])  5.75 us
    ppermute x1, waiting for transfers between devices, per_device(): lax.ppermute(jnp.where(core == 0, top, bottom), axes, swap + [(j, i) for...  5.35 us
    pallas_call x5, Pallas kernels, merge(): pl.pallas_call(functools.partial(merge_body, portions=portions, side=side...  5.34 us
  transfers between devices with their start and end apart: 23, of which 16 were waited for; matrix products, arithmetic and copies ran while one was open for 3% of the time, Pallas kernels for 5%

profile of v5, /device:TPU:32, one launch (start us, length us, event | category | flops | bytes accessed | tf_op | source)
XLA Modules:
  0.0 97.2 jit_solution(12966711468871485472)
XLA Ops:
  0.0 4.4 %project_first.1 = (f32[4,2,256,128]{3,2,1,0:T(8,128)}, f32[4,2,256,128]{3,2,1,0:T(8,128)}, bf16[512,1024]{1,0:T(8,128)(2,1)S(1)}, bf16[1024,8,128]{2,1,0:T(8,12...) custom-call(bf16[512,1024]{1,0:T(8,128)(2,1)} %bitcast.52, bf16[1024,32,128]{2,1,0:T(8,128)(2,1)} %bitcast.51), custom_call_target="tpu_custom_call" | custom-call | flops 1610612736 | bytes 12582912 | tf_op jit(solution)/shard_map/project_first/pallas_call | solution.py:114
  4.4 4.9 %project.1 = (f32[4,2,256,128]{3,2,1,0:T(8,128)}, f32[4,2,256,128]{3,2,1,0:T(8,128)}, f32[4,2,256,128]{3,2,1,0:T(8,128)}, f32[4,2,256,128]{3,2,1,0:T(8,128)}, f3...) custom-call(bf16[512,1024]{1,0:T(8,128)(2,1)S(1)} %get-tuple-element.40.col_ref, ...), custom_call_target="tpu_custom_call" | custom-call | flops 3221225472 | bytes 15728640 | tf_op jit(solution)/shard_map/project/pallas_call | solution.py:144
  10.6 1.6 %collective-permute-done.3 = f32[4,2,256,128]{3,2,1,0:T(8,128)S(1)} collective-permute-done((f32[4,2,256,128]{3,2,1,0:T(8,128)}, f32[4,2,256,128]{3,2,1,0:T(8,128)S(1)}, u32[]{:S(2)}, u32[]{:S(2)}) %collective-permute-start.3) | collective-permute-done | bytes 1048608 | tf_op jit(solution)/shard_map/ppermute | solution.py:295
  15.2 1.6 %collective-permute-done = f32[4,2,256,128]{3,2,1,0:T(8,128)} collective-permute-done((f32[4,2,256,128]{3,2,1,0:T(8,128)}, f32[4,2,256,128]{3,2,1,0:T(8,128)}, u32[]{:S(2)}, u32[]{:S(2)}) %collective-permute-start) | collective-permute-done | bytes 1048608 | tf_op jit(solution)/shard_map/ppermute | solution.py:295
  16.9 2.3 %merge_keep.1 = (f32[4,4,1,128,128]{4,3,2,1,0:T(8,128)S(1)}, f32[4,4,2,64,128]{4,3,2,1,0:T(8,128)S(1)}, f32[4,4,4,32,128]{4,3,2,1,0:T(8,128)S(1)}, f32[4,4,8,16,128]{4,3,2,1,0:T(8,128)S(1)}) custom-call(s32[16,128]{1,0:T(8,128)S(1)} %broadcast_in_dim.57.first_ref, s32[16,128]{1,0:T(8,128)S(1)} %broadcast_in_dim.59.other_ref, ...), custom_call_target="tpu_custom_call" | custom-call | flops 4294967296 | bytes 8388608 | tf_op jit(solution)/shard_map/merge_keep/pallas_call | solution.py:190
  19.3 1.4 %merge_send.5 = f32[4,4,1,128,128]{4,3,2,1,0:T(8,128)S(1)} custom-call(s32[16,128]{1,0:T(8,128)S(1)} %broadcast_in_dim.57.first_ref, s32[16,128]{1,0:T(8,128)S(1)} %broadcast_in_dim.59.other_ref, f32[4,2,1,2,128,128]{5,4,3,2,1,0:T(8,128)S(1)} %bitcast.38, f32[4,2,1,2,128,128]{5,4,3,2,1,0:T(8,128)} %bitcast.14.refs_1_), custom_call_target="tpu_custom_call" | custom-call | flops 1073741824 | bytes 2097152 | tf_op jit(solution)/shard_map/merge_send/pallas_call | solution.py:190
  20.9 1.6 %collective-permute-start.4 = (f16[4,4,1,128,128]{4,3,2,1,0:T(8,128)(2,1)S(1)}, f16[4,4,1,128,128]{4,3,2,1,0:T(8,128)(2,1)S(1)}, u32[]{:S(2)}, u32[]{:S(2)}) collective-permute-start(f16[4,4,1,128,128]{4,3,2,1,0:T(8,128)(2,1)S(1)} %convert_element_type.173), channel_id=1, source_target_pairs={{0,2},{2,0},{4,6},{6,4},{1,3},{3,1},{5,7},{7,5},{8,10},{10,8},{12,... | collective-permute-start | bytes 1572872 | tf_op jit(solution)/shard_map/ppermute | solution.py:312
  23.2 2.2 %collective-permute-start.8 = (f16[4,4,2,64,128]{4,3,2,1,0:T(8,128)(2,1)S(1)}, f16[4,4,2,64,128]{4,3,2,1,0:T(8,128)(2,1)S(1)}, u32[]{:S(2)}, u32[]{:S(2)}) collective-permute-start(f16[4,4,2,64,128]{4,3,2,1,0:T(8,128)(2,1)S(1)} %convert_element_type.186), channel_id=1, source_target_pairs={{2,4},{4,2},{6,0},{0,6},{3,5},{5,3},{7,1},{1,7},{10,12},{12,10},{1... | collective-permute-start | bytes 1572872 | tf_op jit(solution)/shard_map/ppermute | solution.py:312
  26.1 1.7 %collective-permute-start.12 = (f16[4,4,4,32,128]{4,3,2,1,0:T(8,128)(2,1)S(1)}, f16[4,4,4,32,128]{4,3,2,1,0:T(8,128)(2,1)S(1)}, u32[]{:S(2)}, u32[]{:S(2)}) collective-permute-start(f16[4,4,4,32,128]{4,3,2,1,0:T(8,128)(2,1)S(1)} %convert_element_type.199), channel_id=1, source_target_pairs={{0,16},{16,0},{32,48},{48,32},{1,17},{17,1},{33,49},{49,33},{2,18}... | collective-permute-start | bytes 1572872 | tf_op jit(solution)/shard_map/ppermute | solution.py:312
  27.7 2.2 %collective-permute-start.16 = (f16[4,4,8,16,128]{4,3,2,1,0:T(8,128)(2,1)S(1)}, f16[4,4,8,16,128]{4,3,2,1,0:T(8,128)(2,1)S(1)}, u32[]{:S(2)}, u32[]{:S(2)}) collective-permute-start(f16[4,4,8,16,128]{4,3,2,1,0:T(8,128)(2,1)S(1)} %convert_element_type.172), channel_id=1, source_target_pairs={{16,32},{32,16},{48,0},{0,48},{17,33},{33,17},{49,1},{1,49},{18,34... | collective-permute-start | bytes 1572872 | tf_op jit(solution)/shard_map/ppermute | solution.py:312
  30.2 4.7 %collective-permute-done.4 = f16[4,4,1,128,128]{4,3,2,1,0:T(8,128)(2,1)S(1)} collective-permute-done((f16[4,4,1,128,128]{4,3,2,1,0:T(8,128)(2,1)S(1)}, f16[4,4,1,128,128]{4,3,2,1,0:T(8,128)(2,1)S(1)}, u32[]{:S(2)}, u32[]{:S(2)}) %collective-permute-start.4) | collective-permute-done | bytes 524320 | tf_op jit(solution)/shard_map/ppermute | solution.py:312
  35.2 2.8 %collective-permute-start.5 = (f16[4,4,1,1,2,2,16,128]{7,6,1,0,5,4,3,2:T(8,128)(2,1)S(1)}, f16[4,4,1,1,2,2,16,128]{7,6,1,0,5,4,3,2:T(8,128)(2,1)S(1)}, u32[]{:S(2)}, u32[]{:S(2)}) collective-permute-start(f16[4,4,1,1,2,2,16,128]{7,6,1,0,5,4,3,2:T(8,128)(2,1)S(1)} %get-tuple-element.60), channel_id=1, source_target_pairs={{2,4},{4,2},{6,0},{0,6},{3,5},{5,3},{7,1},{1,7},{10,12},{12,10},{1... | collective-permute-start | bytes 786440 | tf_op jit(solution)/shard_map/ppermute | solution.py:334
  39.8 3.1 %collective-permute-start.13 = (f16[4,4,2,2,1,1,16,128]{7,6,1,0,5,4,3,2:T(8,128)(2,1)S(1)}, f16[4,4,2,2,1,1,16,128]{7,6,1,0,5,4,3,2:T(8,128)(2,1)S(1)}, u32[]{:S(2)}, u32[]{:S(2)}) collective-permute-start(f16[4,4,2,2,1,1,16,128]{7,6,1,0,5,4,3,2:T(8,128)(2,1)S(1)} %get-tuple-element.66), channel_id=1, source_target_pairs={{16,32},{32,16},{48,0},{0,48},{17,33},{33,17},{49,1},{1,49},{18,34... | collective-permute-start | bytes 786440 | tf_op jit(solution)/shard_map/ppermute | solution.py:334
  44.0 1.7 %collective-permute-start.6 = (f16[4,4,1,1,1,2,16,128]{7,6,1,0,5,4,3,2:T(8,128)(2,1)S(1)}, f16[4,4,1,1,1,2,16,128]{7,6,1,0,5,4,3,2:T(8,128)(2,1)S(1)}, u32[]{:S(2)}, u32[]{:S(2)}) collective-permute-start(f16[4,4,1,1,1,2,16,128]{7,6,1,0,5,4,3,2:T(8,128)(2,1)S(1)} %add_convert_fusion.3), channel_id=1, source_target_pairs={{0,16},{16,0},{32,48},{48,32},{1,17},{17,1},{33,49},{49,33},{2,18}... | collective-permute-start | bytes 393224 | tf_op jit(solution)/shard_map/ppermute | solution.py:334
  45.8 3.1 %collective-permute-start.10 = (f16[4,4,1,1,2,1,16,128]{7,6,1,0,5,4,3,2:T(8,128)(2,1)S(1)}, f16[4,4,1,1,2,1,16,128]{7,6,1,0,5,4,3,2:T(8,128)(2,1)S(1)}, u32[]{:S(2)}, u32[]{:S(2)}) collective-permute-start(f16[4,4,1,1,2,1,16,128]{7,6,1,0,5,4,3,2:T(8,128)(2,1)S(1)} %add_convert_fusion.2), channel_id=1, source_target_pairs={{16,32},{32,16},{48,0},{0,48},{17,33},{33,17},{49,1},{1,49},{18,34... | collective-permute-start | bytes 393224 | tf_op jit(solution)/shard_map/ppermute | solution.py:334
  51.4 1.5 %collective-permute-start.18 = (f16[4,4,2,1,1,1,16,128]{7,6,1,0,5,4,3,2:T(8,128)(2,1)S(1)}, f16[4,4,2,1,1,1,16,128]{7,6,1,0,5,4,3,2:T(8,128)(2,1)S(1)}, u32[]{:S(2)}, u32[]{:S(2)}) collective-permute-start(f16[4,4,2,1,1,1,16,128]{7,6,1,0,5,4,3,2:T(8,128)(2,1)S(1)} %add_convert_fusion), channel_id=1, source_target_pairs={{2,4},{4,2},{6,0},{0,6},{3,5},{5,3},{7,1},{1,7},{10,12},{12,10},{1... | collective-permute-start | bytes 393224 | tf_op jit(solution)/shard_map/ppermute | solution.py:334
  52.9 2.4 %collective-permute-start.7 = (f16[4,4,1,1,1,1,16,128]{7,6,1,0,5,4,3,2:T(8,128)(2,1)S(1)}, f16[4,4,1,1,1,1,16,128]{7,6,1,0,5,4,3,2:T(8,128)(2,1)S(1)}, u32[]{:S(2)}, u32[]{:S(2)}) collective-permute-start(f16[4,4,1,1,1,1,16,128]{7,6,1,0,5,4,3,2:T(8,128)(2,1)S(1)} %add_convert_fusion.11), channel_id=1, source_target_pairs={{16,32},{32,16},{48,0},{0,48},{17,33},{33,17},{49,1},{1,49},{18,34... | collective-permute-start | bytes 196616 | tf_op jit(solution)/shard_map/ppermute | solution.py:334
  59.7 1.3 %collective-permute-done.15 = f16[4,4,1,1,1,1,16,128]{7,6,1,0,5,4,3,2:T(8,128)(2,1)S(1)} collective-permute-done((f16[4,4,1,1,1,1,16,128]{7,6,1,0,5,4,3,2:T(8,128)(2,1)S(1)}, f16[4,4,1,1,1,1,16,128]{7,6,1,0,5,4,3,2:T(8,128)(2,1)S(1)}, u32[]{:S(2)}, u32[]{:S(2)}) %collective-permute-start.15) | collective-permute-done | bytes 65568 | tf_op jit(solution)/shard_map/ppermute | solution.py:334
  63.6 8.6 %all-to-all-start = ((f16[8,2,64,128]{3,2,1,0:T(8,128)(2,1)}), f16[8,2,64,128]{3,2,1,0:T(8,128)(2,1)S(1)}, u32[]{:S(2)}, u32[]{:S(2)}) async-start(f16[8,2,64,128]{3,2,1,0:T(8,128)(2,1)} %bitcast.31), calls=%async_computation | async-start | bytes 524288 | tf_op jit(solution)/shard_map/all_to_all | solution.py:340
  72.3 8.9 %all-to-all-done = f16[8,2,64,128]{3,2,1,0:T(8,128)(2,1)S(1)} async-done(((f16[8,2,64,128]{3,2,1,0:T(8,128)(2,1)}), f16[8,2,64,128]{3,2,1,0:T(8,128)(2,1)S(1)}, u32[]{:S(2)}, u32[]{:S(2)}) %all-to-all-start) | async-done | bytes 262176 | tf_op jit(solution)/shard_map/all_to_all | solution.py:340
  81.5 5.2 %collective-permute-start.20 = (f16[4,1,64,128]{3,2,1,0:T(8,128)(2,1)S(1)}, f16[4,1,64,128]{3,2,1,0:T(8,128)(2,1)S(1)}, u32[]{:S(2)}, u32[]{:S(2)}) collective-permute-start(f16[4,1,64,128]{3,2,1,0:T(8,128)(2,1)S(1)} %get-tuple-element.92), channel_id=1, source_target_pairs={{1,2},{3,4},{5,6},{7,8},{9,10},{11,12},{13,14},{15,16},{17,18},{19... | collective-permute-start | bytes 196616 | tf_op jit(solution)/shard_map/ppermute | solution.py:352
  86.8 3.1 %inner.1.partial_ref = f32[8,2,4,16,128]{4,3,2,1,0:T(8,128)S(1)} custom-call(f32[8,128]{1,0:T(8,128)S(1)} %broadcast_in_dim.60.cross_ref, f32[2,8,128]{2,1,0:T(8,128)S(1)} %get-tuple-element.95.near_share_ref, f32[4,64,128]{2,1,0:T(8,128)S(1)} %broadcast_in_dim.55.natt_ref, bf16[16,128]{1,0:T(8,128)(2,1)S(1)} %fusion.6.resp_ref, ...), custom_call_target="tpu_custom_call" | custom-call | flops 2147483648 | bytes 1048576 | tf_op jit(solution)/shard_map/inner/pallas_call | solution.py:247
  89.9 5.3 %collective-permute-done.20 = f16[4,1,64,128]{3,2,1,0:T(8,128)(2,1)S(1)} collective-permute-done((f16[4,1,64,128]{3,2,1,0:T(8,128)(2,1)S(1)}, f16[4,1,64,128]{3,2,1,0:T(8,128)(2,1)S(1)}, u32[]{:S(2)}, u32[]{:S(2)}) %collective-permute-start.20) | collective-permute-done | bytes 65568 | tf_op jit(solution)/shard_map/ppermute | solution.py:352
  95.3 1.9 %finish.1 = f32[8,2,16,512]{3,2,1,0:T(8,128)} custom-call(f32[2,8,128]{2,1,0:T(8,128)S(1)} %get-tuple-element.96.far_share_ref, f32[4,64,128]{2,1,0:T(8,128)S(1)} %broadcast_in_dim.55.natt_ref, bf16[16,128]{1,0:T(8,128)(2,1)S(1)} %fusion.6.resp_ref, f32[4,1,64,128]{3,2,1,0:T(8,128)S(1)} %convert_element_type.226.far_ref, ...), custom_call_target="tpu_custom_call" | custom-call | flops 2147483648 | bytes 1048576 | tf_op jit(solution)/shard_map/finish/pallas_call | solution.py:269
  (93 shorter events, 19.3 us)
Async XLA Ops:
  9.3 3.0 %collective-permute-start.3 = (f32[4,2,256,128]{3,2,1,0:T(8,128)}, f32[4,2,256,128]{3,2,1,0:T(8,128)S(1)}, u32[]{:S(2)}, u32[]{:S(2)}) collective-permute-start(f32[4,2,256,128]{3,2,1,0:T(8,128)} %get-tuple-element.49), channel_id=1, source_target_pairs={{0,1},{1,0},{2,3},{3,2},{4,5},{5,4},{6,7},{7,6},{8,9},{9,8},{10,11... | collective-permute-start | bytes 3145736 | tf_op jit(solution)/shard_map/ppermute | solution.py:295
  9.4 4.8 %collective-permute-start.1 = (f32[4,2,256,128]{3,2,1,0:T(8,128)}, f32[4,2,256,128]{3,2,1,0:T(8,128)S(1)}, u32[]{:S(2)}, u32[]{:S(2)}) collective-permute-start(f32[4,2,256,128]{3,2,1,0:T(8,128)} %get-tuple-element.45), channel_id=1, source_target_pairs={{0,1},{1,0},{2,3},{3,2},{4,5},{5,4},{6,7},{7,6},{8,9},{9,8},{10,11... | collective-permute-start | bytes 3145736 | tf_op jit(solution)/shard_map/ppermute | solution.py:295
  9.9 5.4 %collective-permute-start.2 = (f32[4,2,256,128]{3,2,1,0:T(8,128)}, f32[4,2,256,128]{3,2,1,0:T(8,128)S(1)}, u32[]{:S(2)}, u32[]{:S(2)}) collective-permute-start(f32[4,2,256,128]{3,2,1,0:T(8,128)} %get-tuple-element.47), channel_id=1, source_target_pairs={{0,1},{1,0},{2,3},{3,2},{4,5},{5,4},{6,7},{7,6},{8,9},{9,8},{10,11... | collective-permute-start | bytes 3145736 | tf_op jit(solution)/shard_map/ppermute | solution.py:295
  10.0 6.9 %collective-permute-start = (f32[4,2,256,128]{3,2,1,0:T(8,128)}, f32[4,2,256,128]{3,2,1,0:T(8,128)}, u32[]{:S(2)}, u32[]{:S(2)}) collective-permute-start(f32[4,2,256,128]{3,2,1,0:T(8,128)} %get-tuple-element.39), channel_id=1, source_target_pairs={{0,1},{1,0},{2,3},{3,2},{4,5},{5,4},{6,7},{7,6},{8,9},{9,8},{10,11... | collective-permute-start | bytes 3145736 | tf_op jit(solution)/shard_map/ppermute | solution.py:295
  20.9 14.0 %collective-permute-start.4 = (f16[4,4,1,128,128]{4,3,2,1,0:T(8,128)(2,1)S(1)}, f16[4,4,1,128,128]{4,3,2,1,0:T(8,128)(2,1)S(1)}, u32[]{:S(2)}, u32[]{:S(2)}) collective-permute-start(f16[4,4,1,128,128]{4,3,2,1,0:T(8,128)(2,1)S(1)} %convert_element_type.173), channel_id=1, source_target_pairs={{0,2},{2,0},{4,6},{6,4},{1,3},{3,1},{5,7},{7,5},{8,10},{10,8},{12,... | collective-permute-start | bytes 1572872 | tf_op jit(solution)/shard_map/ppermute | solution.py:312
  23.2 15.0 %collective-permute-start.8 = (f16[4,4,2,64,128]{4,3,2,1,0:T(8,128)(2,1)S(1)}, f16[4,4,2,64,128]{4,3,2,1,0:T(8,128)(2,1)S(1)}, u32[]{:S(2)}, u32[]{:S(2)}) collective-permute-start(f16[4,4,2,64,128]{4,3,2,1,0:T(8,128)(2,1)S(1)} %convert_element_type.186), channel_id=1, source_target_pairs={{2,4},{4,2},{6,0},{0,6},{3,5},{5,3},{7,1},{1,7},{10,12},{12,10},{1... | collective-permute-start | bytes 1572872 | tf_op jit(solution)/shard_map/ppermute | solution.py:312
  26.1 13.5 %collective-permute-start.12 = (f16[4,4,4,32,128]{4,3,2,1,0:T(8,128)(2,1)S(1)}, f16[4,4,4,32,128]{4,3,2,1,0:T(8,128)(2,1)S(1)}, u32[]{:S(2)}, u32[]{:S(2)}) collective-permute-start(f16[4,4,4,32,128]{4,3,2,1,0:T(8,128)(2,1)S(1)} %convert_element_type.199), channel_id=1, source_target_pairs={{0,16},{16,0},{32,48},{48,32},{1,17},{17,1},{33,49},{49,33},{2,18}... | collective-permute-start | bytes 1572872 | tf_op jit(solution)/shard_map/ppermute | solution.py:312
  27.7 15.2 %collective-permute-start.16 = (f16[4,4,8,16,128]{4,3,2,1,0:T(8,128)(2,1)S(1)}, f16[4,4,8,16,128]{4,3,2,1,0:T(8,128)(2,1)S(1)}, u32[]{:S(2)}, u32[]{:S(2)}) collective-permute-start(f16[4,4,8,16,128]{4,3,2,1,0:T(8,128)(2,1)S(1)} %convert_element_type.172), channel_id=1, source_target_pairs={{16,32},{32,16},{48,0},{0,48},{17,33},{33,17},{49,1},{1,49},{18,34... | collective-permute-start | bytes 1572872 | tf_op jit(solution)/shard_map/ppermute | solution.py:312
  35.2 8.8 %collective-permute-start.5 = (f16[4,4,1,1,2,2,16,128]{7,6,1,0,5,4,3,2:T(8,128)(2,1)S(1)}, f16[4,4,1,1,2,2,16,128]{7,6,1,0,5,4,3,2:T(8,128)(2,1)S(1)}, u32[]{:S(2)}, u32[]{:S(2)}) collective-permute-start(f16[4,4,1,1,2,2,16,128]{7,6,1,0,5,4,3,2:T(8,128)(2,1)S(1)} %get-tuple-element.60), channel_id=1, source_target_pairs={{2,4},{4,2},{6,0},{0,6},{3,5},{5,3},{7,1},{1,7},{10,12},{12,10},{1... | collective-permute-start | bytes 786440 | tf_op jit(solution)/shard_map/ppermute | solution.py:334
  38.5 7.3 %collective-permute-start.9 = (f16[4,4,1,1,2,2,16,128]{7,6,1,0,5,4,3,2:T(8,128)(2,1)S(1)}, f16[4,4,1,1,2,2,16,128]{7,6,1,0,5,4,3,2:T(8,128)(2,1)S(1)}, u32[]{:S(2)}, u32[]{:S(2)}) collective-permute-start(f16[4,4,1,1,2,2,16,128]{7,6,1,0,5,4,3,2:T(8,128)(2,1)S(1)} %get-tuple-element.63), channel_id=1, source_target_pairs={{0,2},{2,0},{4,6},{6,4},{1,3},{3,1},{5,7},{7,5},{8,10},{10,8},{12,... | collective-permute-start | bytes 786440 | tf_op jit(solution)/shard_map/ppermute | solution.py:334
  39.8 9.1 %collective-permute-start.13 = (f16[4,4,2,2,1,1,16,128]{7,6,1,0,5,4,3,2:T(8,128)(2,1)S(1)}, f16[4,4,2,2,1,1,16,128]{7,6,1,0,5,4,3,2:T(8,128)(2,1)S(1)}, u32[]{:S(2)}, u32[]{:S(2)}) collective-permute-start(f16[4,4,2,2,1,1,16,128]{7,6,1,0,5,4,3,2:T(8,128)(2,1)S(1)} %get-tuple-element.66), channel_id=1, source_target_pairs={{16,32},{32,16},{48,0},{0,48},{17,33},{33,17},{49,1},{1,49},{18,34... | collective-permute-start | bytes 786440 | tf_op jit(solution)/shard_map/ppermute | solution.py:334
  43.2 8.1 %collective-permute-start.17 = (f16[4,4,2,2,1,1,16,128]{7,6,1,0,5,4,3,2:T(8,128)(2,1)S(1)}, f16[4,4,2,2,1,1,16,128]{7,6,1,0,5,4,3,2:T(8,128)(2,1)S(1)}, u32[]{:S(2)}, u32[]{:S(2)}) collective-permute-start(f16[4,4,2,2,1,1,16,128]{7,6,1,0,5,4,3,2:T(8,128)(2,1)S(1)} %get-tuple-element.70), channel_id=1, source_target_pairs={{0,16},{16,0},{32,48},{48,32},{1,17},{17,1},{33,49},{49,33},{2,18}... | collective-permute-start | bytes 786440 | tf_op jit(solution)/shard_map/ppermute | solution.py:334
  44.0 8.8 %collective-permute-start.6 = (f16[4,4,1,1,1,2,16,128]{7,6,1,0,5,4,3,2:T(8,128)(2,1)S(1)}, f16[4,4,1,1,1,2,16,128]{7,6,1,0,5,4,3,2:T(8,128)(2,1)S(1)}, u32[]{:S(2)}, u32[]{:S(2)}) collective-permute-start(f16[4,4,1,1,1,2,16,128]{7,6,1,0,5,4,3,2:T(8,128)(2,1)S(1)} %add_convert_fusion.3), channel_id=1, source_target_pairs={{0,16},{16,0},{32,48},{48,32},{1,17},{17,1},{33,49},{49,33},{2,18}... | collective-permute-start | bytes 393224 | tf_op jit(solution)/shard_map/ppermute | solution.py:334
  45.8 9.5 %collective-permute-start.10 = (f16[4,4,1,1,2,1,16,128]{7,6,1,0,5,4,3,2:T(8,128)(2,1)S(1)}, f16[4,4,1,1,2,1,16,128]{7,6,1,0,5,4,3,2:T(8,128)(2,1)S(1)}, u32[]{:S(2)}, u32[]{:S(2)}) collective-permute-start(f16[4,4,1,1,2,1,16,128]{7,6,1,0,5,4,3,2:T(8,128)(2,1)S(1)} %add_convert_fusion.2), channel_id=1, source_target_pairs={{16,32},{32,16},{48,0},{0,48},{17,33},{33,17},{49,1},{1,49},{18,34... | collective-permute-start | bytes 393224 | tf_op jit(solution)/shard_map/ppermute | solution.py:334
  48.9 6.5 %collective-permute-start.14 = (f16[4,4,1,2,1,1,16,128]{7,6,1,0,5,4,3,2:T(8,128)(2,1)S(1)}, f16[4,4,1,2,1,1,16,128]{7,6,1,0,5,4,3,2:T(8,128)(2,1)S(1)}, u32[]{:S(2)}, u32[]{:S(2)}) collective-permute-start(f16[4,4,1,2,1,1,16,128]{7,6,1,0,5,4,3,2:T(8,128)(2,1)S(1)} %add_convert_fusion.1), channel_id=1, source_target_pairs={{0,2},{2,0},{4,6},{6,4},{1,3},{3,1},{5,7},{7,5},{8,10},{10,8},{12,... | collective-permute-start | bytes 393224 | tf_op jit(solution)/shard_map/ppermute | solution.py:334
  51.4 6.4 %collective-permute-start.18 = (f16[4,4,2,1,1,1,16,128]{7,6,1,0,5,4,3,2:T(8,128)(2,1)S(1)}, f16[4,4,2,1,1,1,16,128]{7,6,1,0,5,4,3,2:T(8,128)(2,1)S(1)}, u32[]{:S(2)}, u32[]{:S(2)}) collective-permute-start(f16[4,4,2,1,1,1,16,128]{7,6,1,0,5,4,3,2:T(8,128)(2,1)S(1)} %add_convert_fusion), channel_id=1, source_target_pairs={{2,4},{4,2},{6,0},{0,6},{3,5},{5,3},{7,1},{1,7},{10,12},{12,10},{1... | collective-permute-start | bytes 393224 | tf_op jit(solution)/shard_map/ppermute | solution.py:334
  52.9 19.3 %copy-start.6 = (f32[8]{0:T(128)S(1)}, f32[8]{0:T(128)}, u32[]{:S(2)}) copy-start(f32[8]{0:T(128)} %param.11) | copy-start | bytes 100
  52.9 5.6 %collective-permute-start.7 = (f16[4,4,1,1,1,1,16,128]{7,6,1,0,5,4,3,2:T(8,128)(2,1)S(1)}, f16[4,4,1,1,1,1,16,128]{7,6,1,0,5,4,3,2:T(8,128)(2,1)S(1)}, u32[]{:S(2)}, u32[]{:S(2)}) collective-permute-start(f16[4,4,1,1,1,1,16,128]{7,6,1,0,5,4,3,2:T(8,128)(2,1)S(1)} %add_convert_fusion.11), channel_id=1, source_target_pairs={{16,32},{32,16},{48,0},{0,48},{17,33},{33,17},{49,1},{1,49},{18,34... | collective-permute-start | bytes 196616 | tf_op jit(solution)/shard_map/ppermute | solution.py:334
  55.3 4.4 %collective-permute-start.11 = (f16[4,4,1,1,1,1,16,128]{7,6,1,0,5,4,3,2:T(8,128)(2,1)S(1)}, f16[4,4,1,1,1,1,16,128]{7,6,1,0,5,4,3,2:T(8,128)(2,1)S(1)}, u32[]{:S(2)}, u32[]{:S(2)}) collective-permute-start(f16[4,4,1,1,1,1,16,128]{7,6,1,0,5,4,3,2:T(8,128)(2,1)S(1)} %add_convert_fusion.9), channel_id=1, source_target_pairs={{0,16},{16,0},{32,48},{48,32},{1,17},{17,1},{33,49},{49,33},{2,18}... | collective-permute-start | bytes 196616 | tf_op jit(solution)/shard_map/ppermute | solution.py:334
  55.5 5.6 %collective-permute-start.15 = (f16[4,4,1,1,1,1,16,128]{7,6,1,0,5,4,3,2:T(8,128)(2,1)S(1)}, f16[4,4,1,1,1,1,16,128]{7,6,1,0,5,4,3,2:T(8,128)(2,1)S(1)}, u32[]{:S(2)}, u32[]{:S(2)}) collective-permute-start(f16[4,4,1,1,1,1,16,128]{7,6,1,0,5,4,3,2:T(8,128)(2,1)S(1)} %add_convert_fusion.7), channel_id=1, source_target_pairs={{2,4},{4,2},{6,0},{0,6},{3,5},{5,3},{7,1},{1,7},{10,12},{12,10},{1... | collective-permute-start | bytes 196616 | tf_op jit(solution)/shard_map/ppermute | solution.py:334
  57.8 4.4 %collective-permute-start.19 = (f16[4,4,1,1,1,1,16,128]{7,6,1,0,5,4,3,2:T(8,128)(2,1)S(1)}, f16[4,4,1,1,1,1,16,128]{7,6,1,0,5,4,3,2:T(8,128)(2,1)S(1)}, u32[]{:S(2)}, u32[]{:S(2)}) collective-permute-start(f16[4,4,1,1,1,1,16,128]{7,6,1,0,5,4,3,2:T(8,128)(2,1)S(1)} %add_convert_fusion.5), channel_id=1, source_target_pairs={{0,2},{2,0},{4,6},{6,4},{1,3},{3,1},{5,7},{7,5},{8,10},{10,8},{12,... | collective-permute-start | bytes 196616 | tf_op jit(solution)/shard_map/ppermute | solution.py:334
  63.6 17.6 %all-to-all-start = ((f16[8,2,64,128]{3,2,1,0:T(8,128)(2,1)}), f16[8,2,64,128]{3,2,1,0:T(8,128)(2,1)S(1)}, u32[]{:S(2)}, u32[]{:S(2)}) async-start(f16[8,2,64,128]{3,2,1,0:T(8,128)(2,1)} %bitcast.31), calls=%async_computation | async-start | bytes 524288 | tf_op jit(solution)/shard_map/all_to_all | solution.py:340
  81.3 5.3 %collective-permute-start.21 = (f16[4,1,64,128]{3,2,1,0:T(8,128)(2,1)S(1)}, f16[4,1,64,128]{3,2,1,0:T(8,128)(2,1)S(1)}, u32[]{:S(2)}, u32[]{:S(2)}) collective-permute-start(f16[4,1,64,128]{3,2,1,0:T(8,128)(2,1)S(1)} %get-tuple-element.91), channel_id=1, source_target_pairs={{0,1},{1,0},{2,3},{3,2},{4,5},{5,4},{6,7},{7,6},{8,9},{9,8},{10,11... | collective-permute-start | bytes 196616 | tf_op jit(solution)/shard_map/ppermute | solution.py:351
  81.5 13.8 %collective-permute-start.20 = (f16[4,1,64,128]{3,2,1,0:T(8,128)(2,1)S(1)}, f16[4,1,64,128]{3,2,1,0:T(8,128)(2,1)S(1)}, u32[]{:S(2)}, u32[]{:S(2)}) collective-permute-start(f16[4,1,64,128]{3,2,1,0:T(8,128)(2,1)S(1)} %get-tuple-element.92), channel_id=1, source_target_pairs={{1,2},{3,4},{5,6},{7,8},{9,10},{11,12},{13,14},{15,16},{17,18},{19... | collective-permute-start | bytes 196616 | tf_op jit(solution)/shard_map/ppermute | solution.py:352
  (7 other events, 55.5 us)

commit v6 on v5

--- a/solution.py
+++ b/solution.py
@@ -255,7 +255,8 @@
     )(leak, share, natt, resp, sums, near)
 
 
-def finish_body(far_share_ref, natt_ref, resp_ref, far_ref, partial_ref, out_ref):
+def finish_body(far_share_ref, natt_ref, resp_ref, far_ref, partial_ref, out_hbm, out_ref, sems):
+    copies = []
     for b in range(PBLK):
         far = detect(natt_ref, resp_ref, lambda m, v: far_ref[m, 0, PBLK * v + b : PBLK * v + b + 1, :])
         for c in range(CBINS):
@@ -263,14 +264,19 @@
                 share = far_share_ref[row, c : c + 1]
                 side = jnp.where(share > 0.0, share * far[c], 0.0)
                 out_ref[c, row, :, b * PB : (b + 1) * PB] = partial_ref[c, row, b] + side
+        columns = (slice(None),) * 3 + (pl.ds(b * PB, PB),)
+        copies.append(pltpu.make_async_copy(out_ref.at[columns], out_hbm.at[columns], sems.at[b]))
+        copies[-1].start()
+    wait_all(copies)
 
 
 def finish(share, natt, resp, far, partial):
     return pl.pallas_call(
         finish_body,
         in_specs=[VMEM] * 5,
-        out_specs=VMEM,
-        out_shape=jax.ShapeDtypeStruct((CBINS, 2, 16, PBLK * PB), jnp.float32),
+        out_specs=HBM,
+        out_shape=pltpu.HBM((CBINS, 2, 16, PBLK * PB), jnp.float32),
+        scratch_shapes=[pltpu.VMEM((CBINS, 2, 16, PBLK * PB), jnp.float32), pltpu.SemaphoreType.DMA((PBLK,))],
         cost_estimate=DETECT_COST,
         compiler_params=vmem_params(8),
         name="finish",

time: 97.5 us -> 97.6 us (level)
  no operation moved by 1% of the time
where the time goes in v6:
time: 97.6 us; the launch traced here: 97.3 us
  starting transfers between devices  40.1 us (41%)
  waiting for transfers between devices  31.4 us (32%)
  Pallas kernels  19.5 us (20%)
  local copies, waits for them, and re-layouts  3.61 us (4%)
  other arithmetic  2.11 us (2%)
    ppermute x12, starting transfers between devices, per_device(): current[w].append(lax.ppermute(sends[w], axis, PAIRS[which]))  17.5 us
    all_to_all x1, waiting for transfers between devices, per_device(): received = lax.all_to_all(outgoing, ('zh', 'mat'), 0, 0, tiled=True)  8.9 us
    all_to_all x1, starting transfers between devices, per_device(): received = lax.all_to_all(outgoing, ('zh', 'mat'), 0, 0, tiled=True)  8.57 us
    ppermute x4, starting transfers between devices, per_device(): got = lax.ppermute(sends[w], axis, PAIRS[which])  7.6 us
    ppermute x12, waiting for transfers between devices, per_device(): current[w].append(lax.ppermute(sends[w], axis, PAIRS[which]))  7.03 us
    ppermute x4, waiting for transfers between devices, per_device(): got = lax.ppermute(sends[w], axis, PAIRS[which])  5.75 us
    ppermute x1, waiting for transfers between devices, per_device(): lax.ppermute(jnp.where(core == 0, top, bottom), axes, swap + [(j, i) for...  5.35 us
    pallas_call x5, Pallas kernels, merge(): pl.pallas_call(functools.partial(merge_body, portions=portions, side=side...  5.34 us
  transfers between devices with their start and end apart: 23, of which 16 were waited for; matrix products, arithmetic and copies ran while one was open for 3% of the time, Pallas kernels for 5%

profile of v6, /device:TPU:32, one launch (start us, length us, event | category | flops | bytes accessed | tf_op | source)
XLA Modules:
  0.0 97.3 jit_solution(8823166510198991702)
XLA Ops:
  0.0 4.4 %project_first.1 = (f32[4,2,256,128]{3,2,1,0:T(8,128)}, f32[4,2,256,128]{3,2,1,0:T(8,128)}, bf16[512,1024]{1,0:T(8,128)(2,1)S(1)}, bf16[1024,8,128]{2,1,0:T(8,12...) custom-call(bf16[512,1024]{1,0:T(8,128)(2,1)} %bitcast.52, bf16[1024,32,128]{2,1,0:T(8,128)(2,1)} %bitcast.51), custom_call_target="tpu_custom_call" | custom-call | flops 1610612736 | bytes 12582912 | tf_op jit(solution)/shard_map/project_first/pallas_call | solution.py:114
  4.4 4.9 %project.1 = (f32[4,2,256,128]{3,2,1,0:T(8,128)}, f32[4,2,256,128]{3,2,1,0:T(8,128)}, f32[4,2,256,128]{3,2,1,0:T(8,128)}, f32[4,2,256,128]{3,2,1,0:T(8,128)}, f3...) custom-call(bf16[512,1024]{1,0:T(8,128)(2,1)S(1)} %get-tuple-element.40.col_ref, ...), custom_call_target="tpu_custom_call" | custom-call | flops 3221225472 | bytes 15728640 | tf_op jit(solution)/shard_map/project/pallas_call | solution.py:144
  10.6 1.6 %collective-permute-done.3 = f32[4,2,256,128]{3,2,1,0:T(8,128)S(1)} collective-permute-done((f32[4,2,256,128]{3,2,1,0:T(8,128)}, f32[4,2,256,128]{3,2,1,0:T(8,128)S(1)}, u32[]{:S(2)}, u32[]{:S(2)}) %collective-permute-start.3) | collective-permute-done | bytes 1048608 | tf_op jit(solution)/shard_map/ppermute | solution.py:301
  15.2 1.6 %collective-permute-done = f32[4,2,256,128]{3,2,1,0:T(8,128)} collective-permute-done((f32[4,2,256,128]{3,2,1,0:T(8,128)}, f32[4,2,256,128]{3,2,1,0:T(8,128)}, u32[]{:S(2)}, u32[]{:S(2)}) %collective-permute-start) | collective-permute-done | bytes 1048608 | tf_op jit(solution)/shard_map/ppermute | solution.py:301
  16.9 2.3 %merge_keep.1 = (f32[4,4,1,128,128]{4,3,2,1,0:T(8,128)S(1)}, f32[4,4,2,64,128]{4,3,2,1,0:T(8,128)S(1)}, f32[4,4,4,32,128]{4,3,2,1,0:T(8,128)S(1)}, f32[4,4,8,16,128]{4,3,2,1,0:T(8,128)S(1)}) custom-call(s32[16,128]{1,0:T(8,128)S(1)} %broadcast_in_dim.57.first_ref, s32[16,128]{1,0:T(8,128)S(1)} %broadcast_in_dim.59.other_ref, ...), custom_call_target="tpu_custom_call" | custom-call | flops 4294967296 | bytes 8388608 | tf_op jit(solution)/shard_map/merge_keep/pallas_call | solution.py:190
  19.3 1.4 %merge_send.5 = f32[4,4,1,128,128]{4,3,2,1,0:T(8,128)S(1)} custom-call(s32[16,128]{1,0:T(8,128)S(1)} %broadcast_in_dim.57.first_ref, s32[16,128]{1,0:T(8,128)S(1)} %broadcast_in_dim.59.other_ref, f32[4,2,1,2,128,128]{5,4,3,2,1,0:T(8,128)S(1)} %bitcast.38, f32[4,2,1,2,128,128]{5,4,3,2,1,0:T(8,128)} %bitcast.14.refs_1_), custom_call_target="tpu_custom_call" | custom-call | flops 1073741824 | bytes 2097152 | tf_op jit(solution)/shard_map/merge_send/pallas_call | solution.py:190
  20.9 1.6 %collective-permute-start.4 = (f16[4,4,1,128,128]{4,3,2,1,0:T(8,128)(2,1)S(1)}, f16[4,4,1,128,128]{4,3,2,1,0:T(8,128)(2,1)S(1)}, u32[]{:S(2)}, u32[]{:S(2)}) collective-permute-start(f16[4,4,1,128,128]{4,3,2,1,0:T(8,128)(2,1)S(1)} %convert_element_type.173), channel_id=1, source_target_pairs={{0,2},{2,0},{4,6},{6,4},{1,3},{3,1},{5,7},{7,5},{8,10},{10,8},{12,... | collective-permute-start | bytes 1572872 | tf_op jit(solution)/shard_map/ppermute | solution.py:318
  23.2 2.2 %collective-permute-start.8 = (f16[4,4,2,64,128]{4,3,2,1,0:T(8,128)(2,1)S(1)}, f16[4,4,2,64,128]{4,3,2,1,0:T(8,128)(2,1)S(1)}, u32[]{:S(2)}, u32[]{:S(2)}) collective-permute-start(f16[4,4,2,64,128]{4,3,2,1,0:T(8,128)(2,1)S(1)} %convert_element_type.186), channel_id=1, source_target_pairs={{2,4},{4,2},{6,0},{0,6},{3,5},{5,3},{7,1},{1,7},{10,12},{12,10},{1... | collective-permute-start | bytes 1572872 | tf_op jit(solution)/shard_map/ppermute | solution.py:318
  26.1 1.7 %collective-permute-start.12 = (f16[4,4,4,32,128]{4,3,2,1,0:T(8,128)(2,1)S(1)}, f16[4,4,4,32,128]{4,3,2,1,0:T(8,128)(2,1)S(1)}, u32[]{:S(2)}, u32[]{:S(2)}) collective-permute-start(f16[4,4,4,32,128]{4,3,2,1,0:T(8,128)(2,1)S(1)} %convert_element_type.199), channel_id=1, source_target_pairs={{0,16},{16,0},{32,48},{48,32},{1,17},{17,1},{33,49},{49,33},{2,18}... | collective-permute-start | bytes 1572872 | tf_op jit(solution)/shard_map/ppermute | solution.py:318
  27.7 2.2 %collective-permute-start.16 = (f16[4,4,8,16,128]{4,3,2,1,0:T(8,128)(2,1)S(1)}, f16[4,4,8,16,128]{4,3,2,1,0:T(8,128)(2,1)S(1)}, u32[]{:S(2)}, u32[]{:S(2)}) collective-permute-start(f16[4,4,8,16,128]{4,3,2,1,0:T(8,128)(2,1)S(1)} %convert_element_type.172), channel_id=1, source_target_pairs={{16,32},{32,16},{48,0},{0,48},{17,33},{33,17},{49,1},{1,49},{18,34... | collective-permute-start | bytes 1572872 | tf_op jit(solution)/shard_map/ppermute | solution.py:318
  30.2 4.7 %collective-permute-done.4 = f16[4,4,1,128,128]{4,3,2,1,0:T(8,128)(2,1)S(1)} collective-permute-done((f16[4,4,1,128,128]{4,3,2,1,0:T(8,128)(2,1)S(1)}, f16[4,4,1,128,128]{4,3,2,1,0:T(8,128)(2,1)S(1)}, u32[]{:S(2)}, u32[]{:S(2)}) %collective-permute-start.4) | collective-permute-done | bytes 524320 | tf_op jit(solution)/shard_map/ppermute | solution.py:318
  35.2 2.8 %collective-permute-start.5 = (f16[4,4,1,1,2,2,16,128]{7,6,1,0,5,4,3,2:T(8,128)(2,1)S(1)}, f16[4,4,1,1,2,2,16,128]{7,6,1,0,5,4,3,2:T(8,128)(2,1)S(1)}, u32[]{:S(2)}, u32[]{:S(2)}) collective-permute-start(f16[4,4,1,1,2,2,16,128]{7,6,1,0,5,4,3,2:T(8,128)(2,1)S(1)} %get-tuple-element.60), channel_id=1, source_target_pairs={{2,4},{4,2},{6,0},{0,6},{3,5},{5,3},{7,1},{1,7},{10,12},{12,10},{1... | collective-permute-start | bytes 786440 | tf_op jit(solution)/shard_map/ppermute | solution.py:340
  39.8 3.1 %collective-permute-start.13 = (f16[4,4,2,2,1,1,16,128]{7,6,1,0,5,4,3,2:T(8,128)(2,1)S(1)}, f16[4,4,2,2,1,1,16,128]{7,6,1,0,5,4,3,2:T(8,128)(2,1)S(1)}, u32[]{:S(2)}, u32[]{:S(2)}) collective-permute-start(f16[4,4,2,2,1,1,16,128]{7,6,1,0,5,4,3,2:T(8,128)(2,1)S(1)} %get-tuple-element.66), channel_id=1, source_target_pairs={{16,32},{32,16},{48,0},{0,48},{17,33},{33,17},{49,1},{1,49},{18,34... | collective-permute-start | bytes 786440 | tf_op jit(solution)/shard_map/ppermute | solution.py:340
  44.0 1.7 %collective-permute-start.6 = (f16[4,4,1,1,1,2,16,128]{7,6,1,0,5,4,3,2:T(8,128)(2,1)S(1)}, f16[4,4,1,1,1,2,16,128]{7,6,1,0,5,4,3,2:T(8,128)(2,1)S(1)}, u32[]{:S(2)}, u32[]{:S(2)}) collective-permute-start(f16[4,4,1,1,1,2,16,128]{7,6,1,0,5,4,3,2:T(8,128)(2,1)S(1)} %add_convert_fusion.3), channel_id=1, source_target_pairs={{0,16},{16,0},{32,48},{48,32},{1,17},{17,1},{33,49},{49,33},{2,18}... | collective-permute-start | bytes 393224 | tf_op jit(solution)/shard_map/ppermute | solution.py:340
  45.8 3.1 %collective-permute-start.10 = (f16[4,4,1,1,2,1,16,128]{7,6,1,0,5,4,3,2:T(8,128)(2,1)S(1)}, f16[4,4,1,1,2,1,16,128]{7,6,1,0,5,4,3,2:T(8,128)(2,1)S(1)}, u32[]{:S(2)}, u32[]{:S(2)}) collective-permute-start(f16[4,4,1,1,2,1,16,128]{7,6,1,0,5,4,3,2:T(8,128)(2,1)S(1)} %add_convert_fusion.2), channel_id=1, source_target_pairs={{16,32},{32,16},{48,0},{0,48},{17,33},{33,17},{49,1},{1,49},{18,34... | collective-permute-start | bytes 393224 | tf_op jit(solution)/shard_map/ppermute | solution.py:340
  51.4 1.5 %collective-permute-start.18 = (f16[4,4,2,1,1,1,16,128]{7,6,1,0,5,4,3,2:T(8,128)(2,1)S(1)}, f16[4,4,2,1,1,1,16,128]{7,6,1,0,5,4,3,2:T(8,128)(2,1)S(1)}, u32[]{:S(2)}, u32[]{:S(2)}) collective-permute-start(f16[4,4,2,1,1,1,16,128]{7,6,1,0,5,4,3,2:T(8,128)(2,1)S(1)} %add_convert_fusion), channel_id=1, source_target_pairs={{2,4},{4,2},{6,0},{0,6},{3,5},{5,3},{7,1},{1,7},{10,12},{12,10},{1... | collective-permute-start | bytes 393224 | tf_op jit(solution)/shard_map/ppermute | solution.py:340
  52.9 2.4 %collective-permute-start.7 = (f16[4,4,1,1,1,1,16,128]{7,6,1,0,5,4,3,2:T(8,128)(2,1)S(1)}, f16[4,4,1,1,1,1,16,128]{7,6,1,0,5,4,3,2:T(8,128)(2,1)S(1)}, u32[]{:S(2)}, u32[]{:S(2)}) collective-permute-start(f16[4,4,1,1,1,1,16,128]{7,6,1,0,5,4,3,2:T(8,128)(2,1)S(1)} %add_convert_fusion.11), channel_id=1, source_target_pairs={{16,32},{32,16},{48,0},{0,48},{17,33},{33,17},{49,1},{1,49},{18,34... | collective-permute-start | bytes 196616 | tf_op jit(solution)/shard_map/ppermute | solution.py:340
  59.7 1.3 %collective-permute-done.15 = f16[4,4,1,1,1,1,16,128]{7,6,1,0,5,4,3,2:T(8,128)(2,1)S(1)} collective-permute-done((f16[4,4,1,1,1,1,16,128]{7,6,1,0,5,4,3,2:T(8,128)(2,1)S(1)}, f16[4,4,1,1,1,1,16,128]{7,6,1,0,5,4,3,2:T(8,128)(2,1)S(1)}, u32[]{:S(2)}, u32[]{:S(2)}) %collective-permute-start.15) | collective-permute-done | bytes 65568 | tf_op jit(solution)/shard_map/ppermute | solution.py:340
  63.6 8.6 %all-to-all-start = ((f16[8,2,64,128]{3,2,1,0:T(8,128)(2,1)}), f16[8,2,64,128]{3,2,1,0:T(8,128)(2,1)S(1)}, u32[]{:S(2)}, u32[]{:S(2)}) async-start(f16[8,2,64,128]{3,2,1,0:T(8,128)(2,1)} %bitcast.31), calls=%async_computation | async-start | bytes 524288 | tf_op jit(solution)/shard_map/all_to_all | solution.py:346
  72.3 8.9 %all-to-all-done = f16[8,2,64,128]{3,2,1,0:T(8,128)(2,1)S(1)} async-done(((f16[8,2,64,128]{3,2,1,0:T(8,128)(2,1)}), f16[8,2,64,128]{3,2,1,0:T(8,128)(2,1)S(1)}, u32[]{:S(2)}, u32[]{:S(2)}) %all-to-all-start) | async-done | bytes 262176 | tf_op jit(solution)/shard_map/all_to_all | solution.py:346
  81.5 5.2 %collective-permute-start.20 = (f16[4,1,64,128]{3,2,1,0:T(8,128)(2,1)S(1)}, f16[4,1,64,128]{3,2,1,0:T(8,128)(2,1)S(1)}, u32[]{:S(2)}, u32[]{:S(2)}) collective-permute-start(f16[4,1,64,128]{3,2,1,0:T(8,128)(2,1)S(1)} %get-tuple-element.92), channel_id=1, source_target_pairs={{1,2},{3,4},{5,6},{7,8},{9,10},{11,12},{13,14},{15,16},{17,18},{19... | collective-permute-start | bytes 196616 | tf_op jit(solution)/shard_map/ppermute | solution.py:358
  86.8 3.1 %inner.1.partial_ref = f32[8,2,4,16,128]{4,3,2,1,0:T(8,128)S(1)} custom-call(f32[8,128]{1,0:T(8,128)S(1)} %broadcast_in_dim.60.cross_ref, f32[2,8,128]{2,1,0:T(8,128)S(1)} %get-tuple-element.95.near_share_ref, f32[4,64,128]{2,1,0:T(8,128)S(1)} %broadcast_in_dim.55.natt_ref, bf16[16,128]{1,0:T(8,128)(2,1)S(1)} %fusion.6.resp_ref, ...), custom_call_target="tpu_custom_call" | custom-call | flops 2147483648 | bytes 1048576 | tf_op jit(solution)/shard_map/inner/pallas_call | solution.py:247
  89.9 5.3 %collective-permute-done.20 = f16[4,1,64,128]{3,2,1,0:T(8,128)(2,1)S(1)} collective-permute-done((f16[4,1,64,128]{3,2,1,0:T(8,128)(2,1)S(1)}, f16[4,1,64,128]{3,2,1,0:T(8,128)(2,1)S(1)}, u32[]{:S(2)}, u32[]{:S(2)}) %collective-permute-start.20) | collective-permute-done | bytes 65568 | tf_op jit(solution)/shard_map/ppermute | solution.py:358
  95.3 1.8 %finish.1 = f32[8,2,16,512]{3,2,1,0:T(8,128)} custom-call(f32[2,8,128]{2,1,0:T(8,128)S(1)} %get-tuple-element.96.far_share_ref, f32[4,64,128]{2,1,0:T(8,128)S(1)} %broadcast_in_dim.55.natt_ref, bf16[16,128]{1,0:T(8,128)(2,1)S(1)} %fusion.6.resp_ref, f32[4,1,64,128]{3,2,1,0:T(8,128)S(1)} %convert_element_type.226.far_ref, ...), custom_call_target="tpu_custom_call" | custom-call | flops 2147483648 | bytes 1048576 | tf_op jit(solution)/shard_map/finish/pallas_call | solution.py:274
  (93 shorter events, 19.3 us)
Async XLA Ops:
  9.3 3.0 %collective-permute-start.3 = (f32[4,2,256,128]{3,2,1,0:T(8,128)}, f32[4,2,256,128]{3,2,1,0:T(8,128)S(1)}, u32[]{:S(2)}, u32[]{:S(2)}) collective-permute-start(f32[4,2,256,128]{3,2,1,0:T(8,128)} %get-tuple-element.49), channel_id=1, source_target_pairs={{0,1},{1,0},{2,3},{3,2},{4,5},{5,4},{6,7},{7,6},{8,9},{9,8},{10,11... | collective-permute-start | bytes 3145736 | tf_op jit(solution)/shard_map/ppermute | solution.py:301
  9.4 4.8 %collective-permute-start.1 = (f32[4,2,256,128]{3,2,1,0:T(8,128)}, f32[4,2,256,128]{3,2,1,0:T(8,128)S(1)}, u32[]{:S(2)}, u32[]{:S(2)}) collective-permute-start(f32[4,2,256,128]{3,2,1,0:T(8,128)} %get-tuple-element.45), channel_id=1, source_target_pairs={{0,1},{1,0},{2,3},{3,2},{4,5},{5,4},{6,7},{7,6},{8,9},{9,8},{10,11... | collective-permute-start | bytes 3145736 | tf_op jit(solution)/shard_map/ppermute | solution.py:301
  9.9 5.4 %collective-permute-start.2 = (f32[4,2,256,128]{3,2,1,0:T(8,128)}, f32[4,2,256,128]{3,2,1,0:T(8,128)S(1)}, u32[]{:S(2)}, u32[]{:S(2)}) collective-permute-start(f32[4,2,256,128]{3,2,1,0:T(8,128)} %get-tuple-element.47), channel_id=1, source_target_pairs={{0,1},{1,0},{2,3},{3,2},{4,5},{5,4},{6,7},{7,6},{8,9},{9,8},{10,11... | collective-permute-start | bytes 3145736 | tf_op jit(solution)/shard_map/ppermute | solution.py:301
  10.0 6.9 %collective-permute-start = (f32[4,2,256,128]{3,2,1,0:T(8,128)}, f32[4,2,256,128]{3,2,1,0:T(8,128)}, u32[]{:S(2)}, u32[]{:S(2)}) collective-permute-start(f32[4,2,256,128]{3,2,1,0:T(8,128)} %get-tuple-element.39), channel_id=1, source_target_pairs={{0,1},{1,0},{2,3},{3,2},{4,5},{5,4},{6,7},{7,6},{8,9},{9,8},{10,11... | collective-permute-start | bytes 3145736 | tf_op jit(solution)/shard_map/ppermute | solution.py:301
  20.9 14.0 %collective-permute-start.4 = (f16[4,4,1,128,128]{4,3,2,1,0:T(8,128)(2,1)S(1)}, f16[4,4,1,128,128]{4,3,2,1,0:T(8,128)(2,1)S(1)}, u32[]{:S(2)}, u32[]{:S(2)}) collective-permute-start(f16[4,4,1,128,128]{4,3,2,1,0:T(8,128)(2,1)S(1)} %convert_element_type.173), channel_id=1, source_target_pairs={{0,2},{2,0},{4,6},{6,4},{1,3},{3,1},{5,7},{7,5},{8,10},{10,8},{12,... | collective-permute-start | bytes 1572872 | tf_op jit(solution)/shard_map/ppermute | solution.py:318
  23.2 15.0 %collective-permute-start.8 = (f16[4,4,2,64,128]{4,3,2,1,0:T(8,128)(2,1)S(1)}, f16[4,4,2,64,128]{4,3,2,1,0:T(8,128)(2,1)S(1)}, u32[]{:S(2)}, u32[]{:S(2)}) collective-permute-start(f16[4,4,2,64,128]{4,3,2,1,0:T(8,128)(2,1)S(1)} %convert_element_type.186), channel_id=1, source_target_pairs={{2,4},{4,2},{6,0},{0,6},{3,5},{5,3},{7,1},{1,7},{10,12},{12,10},{1... | collective-permute-start | bytes 1572872 | tf_op jit(solution)/shard_map/ppermute | solution.py:318
  26.1 13.5 %collective-permute-start.12 = (f16[4,4,4,32,128]{4,3,2,1,0:T(8,128)(2,1)S(1)}, f16[4,4,4,32,128]{4,3,2,1,0:T(8,128)(2,1)S(1)}, u32[]{:S(2)}, u32[]{:S(2)}) collective-permute-start(f16[4,4,4,32,128]{4,3,2,1,0:T(8,128)(2,1)S(1)} %convert_element_type.199), channel_id=1, source_target_pairs={{0,16},{16,0},{32,48},{48,32},{1,17},{17,1},{33,49},{49,33},{2,18}... | collective-permute-start | bytes 1572872 | tf_op jit(solution)/shard_map/ppermute | solution.py:318
  27.7 15.2 %collective-permute-start.16 = (f16[4,4,8,16,128]{4,3,2,1,0:T(8,128)(2,1)S(1)}, f16[4,4,8,16,128]{4,3,2,1,0:T(8,128)(2,1)S(1)}, u32[]{:S(2)}, u32[]{:S(2)}) collective-permute-start(f16[4,4,8,16,128]{4,3,2,1,0:T(8,128)(2,1)S(1)} %convert_element_type.172), channel_id=1, source_target_pairs={{16,32},{32,16},{48,0},{0,48},{17,33},{33,17},{49,1},{1,49},{18,34... | collective-permute-start | bytes 1572872 | tf_op jit(solution)/shard_map/ppermute | solution.py:318
  35.2 8.8 %collective-permute-start.5 = (f16[4,4,1,1,2,2,16,128]{7,6,1,0,5,4,3,2:T(8,128)(2,1)S(1)}, f16[4,4,1,1,2,2,16,128]{7,6,1,0,5,4,3,2:T(8,128)(2,1)S(1)}, u32[]{:S(2)}, u32[]{:S(2)}) collective-permute-start(f16[4,4,1,1,2,2,16,128]{7,6,1,0,5,4,3,2:T(8,128)(2,1)S(1)} %get-tuple-element.60), channel_id=1, source_target_pairs={{2,4},{4,2},{6,0},{0,6},{3,5},{5,3},{7,1},{1,7},{10,12},{12,10},{1... | collective-permute-start | bytes 786440 | tf_op jit(solution)/shard_map/ppermute | solution.py:340
  38.5 7.3 %collective-permute-start.9 = (f16[4,4,1,1,2,2,16,128]{7,6,1,0,5,4,3,2:T(8,128)(2,1)S(1)}, f16[4,4,1,1,2,2,16,128]{7,6,1,0,5,4,3,2:T(8,128)(2,1)S(1)}, u32[]{:S(2)}, u32[]{:S(2)}) collective-permute-start(f16[4,4,1,1,2,2,16,128]{7,6,1,0,5,4,3,2:T(8,128)(2,1)S(1)} %get-tuple-element.63), channel_id=1, source_target_pairs={{0,2},{2,0},{4,6},{6,4},{1,3},{3,1},{5,7},{7,5},{8,10},{10,8},{12,... | collective-permute-start | bytes 786440 | tf_op jit(solution)/shard_map/ppermute | solution.py:340
  39.8 9.1 %collective-permute-start.13 = (f16[4,4,2,2,1,1,16,128]{7,6,1,0,5,4,3,2:T(8,128)(2,1)S(1)}, f16[4,4,2,2,1,1,16,128]{7,6,1,0,5,4,3,2:T(8,128)(2,1)S(1)}, u32[]{:S(2)}, u32[]{:S(2)}) collective-permute-start(f16[4,4,2,2,1,1,16,128]{7,6,1,0,5,4,3,2:T(8,128)(2,1)S(1)} %get-tuple-element.66), channel_id=1, source_target_pairs={{16,32},{32,16},{48,0},{0,48},{17,33},{33,17},{49,1},{1,49},{18,34... | collective-permute-start | bytes 786440 | tf_op jit(solution)/shard_map/ppermute | solution.py:340
  43.2 8.1 %collective-permute-start.17 = (f16[4,4,2,2,1,1,16,128]{7,6,1,0,5,4,3,2:T(8,128)(2,1)S(1)}, f16[4,4,2,2,1,1,16,128]{7,6,1,0,5,4,3,2:T(8,128)(2,1)S(1)}, u32[]{:S(2)}, u32[]{:S(2)}) collective-permute-start(f16[4,4,2,2,1,1,16,128]{7,6,1,0,5,4,3,2:T(8,128)(2,1)S(1)} %get-tuple-element.70), channel_id=1, source_target_pairs={{0,16},{16,0},{32,48},{48,32},{1,17},{17,1},{33,49},{49,33},{2,18}... | collective-permute-start | bytes 786440 | tf_op jit(solution)/shard_map/ppermute | solution.py:340
  44.0 8.8 %collective-permute-start.6 = (f16[4,4,1,1,1,2,16,128]{7,6,1,0,5,4,3,2:T(8,128)(2,1)S(1)}, f16[4,4,1,1,1,2,16,128]{7,6,1,0,5,4,3,2:T(8,128)(2,1)S(1)}, u32[]{:S(2)}, u32[]{:S(2)}) collective-permute-start(f16[4,4,1,1,1,2,16,128]{7,6,1,0,5,4,3,2:T(8,128)(2,1)S(1)} %add_convert_fusion.3), channel_id=1, source_target_pairs={{0,16},{16,0},{32,48},{48,32},{1,17},{17,1},{33,49},{49,33},{2,18}... | collective-permute-start | bytes 393224 | tf_op jit(solution)/shard_map/ppermute | solution.py:340
  45.8 9.5 %collective-permute-start.10 = (f16[4,4,1,1,2,1,16,128]{7,6,1,0,5,4,3,2:T(8,128)(2,1)S(1)}, f16[4,4,1,1,2,1,16,128]{7,6,1,0,5,4,3,2:T(8,128)(2,1)S(1)}, u32[]{:S(2)}, u32[]{:S(2)}) collective-permute-start(f16[4,4,1,1,2,1,16,128]{7,6,1,0,5,4,3,2:T(8,128)(2,1)S(1)} %add_convert_fusion.2), channel_id=1, source_target_pairs={{16,32},{32,16},{48,0},{0,48},{17,33},{33,17},{49,1},{1,49},{18,34... | collective-permute-start | bytes 393224 | tf_op jit(solution)/shard_map/ppermute | solution.py:340
  48.9 6.5 %collective-permute-start.14 = (f16[4,4,1,2,1,1,16,128]{7,6,1,0,5,4,3,2:T(8,128)(2,1)S(1)}, f16[4,4,1,2,1,1,16,128]{7,6,1,0,5,4,3,2:T(8,128)(2,1)S(1)}, u32[]{:S(2)}, u32[]{:S(2)}) collective-permute-start(f16[4,4,1,2,1,1,16,128]{7,6,1,0,5,4,3,2:T(8,128)(2,1)S(1)} %add_convert_fusion.1), channel_id=1, source_target_pairs={{0,2},{2,0},{4,6},{6,4},{1,3},{3,1},{5,7},{7,5},{8,10},{10,8},{12,... | collective-permute-start | bytes 393224 | tf_op jit(solution)/shard_map/ppermute | solution.py:340
  51.4 6.4 %collective-permute-start.18 = (f16[4,4,2,1,1,1,16,128]{7,6,1,0,5,4,3,2:T(8,128)(2,1)S(1)}, f16[4,4,2,1,1,1,16,128]{7,6,1,0,5,4,3,2:T(8,128)(2,1)S(1)}, u32[]{:S(2)}, u32[]{:S(2)}) collective-permute-start(f16[4,4,2,1,1,1,16,128]{7,6,1,0,5,4,3,2:T(8,128)(2,1)S(1)} %add_convert_fusion), channel_id=1, source_target_pairs={{2,4},{4,2},{6,0},{0,6},{3,5},{5,3},{7,1},{1,7},{10,12},{12,10},{1... | collective-permute-start | bytes 393224 | tf_op jit(solution)/shard_map/ppermute | solution.py:340
  52.9 19.3 %copy-start.6 = (f32[8]{0:T(128)S(1)}, f32[8]{0:T(128)}, u32[]{:S(2)}) copy-start(f32[8]{0:T(128)} %param.11) | copy-start | bytes 100
  52.9 5.6 %collective-permute-start.7 = (f16[4,4,1,1,1,1,16,128]{7,6,1,0,5,4,3,2:T(8,128)(2,1)S(1)}, f16[4,4,1,1,1,1,16,128]{7,6,1,0,5,4,3,2:T(8,128)(2,1)S(1)}, u32[]{:S(2)}, u32[]{:S(2)}) collective-permute-start(f16[4,4,1,1,1,1,16,128]{7,6,1,0,5,4,3,2:T(8,128)(2,1)S(1)} %add_convert_fusion.11), channel_id=1, source_target_pairs={{16,32},{32,16},{48,0},{0,48},{17,33},{33,17},{49,1},{1,49},{18,34... | collective-permute-start | bytes 196616 | tf_op jit(solution)/shard_map/ppermute | solution.py:340
  55.3 4.4 %collective-permute-start.11 = (f16[4,4,1,1,1,1,16,128]{7,6,1,0,5,4,3,2:T(8,128)(2,1)S(1)}, f16[4,4,1,1,1,1,16,128]{7,6,1,0,5,4,3,2:T(8,128)(2,1)S(1)}, u32[]{:S(2)}, u32[]{:S(2)}) collective-permute-start(f16[4,4,1,1,1,1,16,128]{7,6,1,0,5,4,3,2:T(8,128)(2,1)S(1)} %add_convert_fusion.9), channel_id=1, source_target_pairs={{0,16},{16,0},{32,48},{48,32},{1,17},{17,1},{33,49},{49,33},{2,18}... | collective-permute-start | bytes 196616 | tf_op jit(solution)/shard_map/ppermute | solution.py:340
  55.5 5.6 %collective-permute-start.15 = (f16[4,4,1,1,1,1,16,128]{7,6,1,0,5,4,3,2:T(8,128)(2,1)S(1)}, f16[4,4,1,1,1,1,16,128]{7,6,1,0,5,4,3,2:T(8,128)(2,1)S(1)}, u32[]{:S(2)}, u32[]{:S(2)}) collective-permute-start(f16[4,4,1,1,1,1,16,128]{7,6,1,0,5,4,3,2:T(8,128)(2,1)S(1)} %add_convert_fusion.7), channel_id=1, source_target_pairs={{2,4},{4,2},{6,0},{0,6},{3,5},{5,3},{7,1},{1,7},{10,12},{12,10},{1... | collective-permute-start | bytes 196616 | tf_op jit(solution)/shard_map/ppermute | solution.py:340
  57.8 4.4 %collective-permute-start.19 = (f16[4,4,1,1,1,1,16,128]{7,6,1,0,5,4,3,2:T(8,128)(2,1)S(1)}, f16[4,4,1,1,1,1,16,128]{7,6,1,0,5,4,3,2:T(8,128)(2,1)S(1)}, u32[]{:S(2)}, u32[]{:S(2)}) collective-permute-start(f16[4,4,1,1,1,1,16,128]{7,6,1,0,5,4,3,2:T(8,128)(2,1)S(1)} %add_convert_fusion.5), channel_id=1, source_target_pairs={{0,2},{2,0},{4,6},{6,4},{1,3},{3,1},{5,7},{7,5},{8,10},{10,8},{12,... | collective-permute-start | bytes 196616 | tf_op jit(solution)/shard_map/ppermute | solution.py:340
  63.6 17.6 %all-to-all-start = ((f16[8,2,64,128]{3,2,1,0:T(8,128)(2,1)}), f16[8,2,64,128]{3,2,1,0:T(8,128)(2,1)S(1)}, u32[]{:S(2)}, u32[]{:S(2)}) async-start(f16[8,2,64,128]{3,2,1,0:T(8,128)(2,1)} %bitcast.31), calls=%async_computation | async-start | bytes 524288 | tf_op jit(solution)/shard_map/all_to_all | solution.py:346
  81.3 5.3 %collective-permute-start.21 = (f16[4,1,64,128]{3,2,1,0:T(8,128)(2,1)S(1)}, f16[4,1,64,128]{3,2,1,0:T(8,128)(2,1)S(1)}, u32[]{:S(2)}, u32[]{:S(2)}) collective-permute-start(f16[4,1,64,128]{3,2,1,0:T(8,128)(2,1)S(1)} %get-tuple-element.91), channel_id=1, source_target_pairs={{0,1},{1,0},{2,3},{3,2},{4,5},{5,4},{6,7},{7,6},{8,9},{9,8},{10,11... | collective-permute-start | bytes 196616 | tf_op jit(solution)/shard_map/ppermute | solution.py:357
  81.5 13.8 %collective-permute-start.20 = (f16[4,1,64,128]{3,2,1,0:T(8,128)(2,1)S(1)}, f16[4,1,64,128]{3,2,1,0:T(8,128)(2,1)S(1)}, u32[]{:S(2)}, u32[]{:S(2)}) collective-permute-start(f16[4,1,64,128]{3,2,1,0:T(8,128)(2,1)S(1)} %get-tuple-element.92), channel_id=1, source_target_pairs={{1,2},{3,4},{5,6},{7,8},{9,10},{11,12},{13,14},{15,16},{17,18},{19... | collective-permute-start | bytes 196616 | tf_op jit(solution)/shard_map/ppermute | solution.py:358
  (7 other events, 55.5 us)
